TPU v7x, 32 devices: a whole 2x2x4 slice. The times are simulated.
32 devices in a mesh: rep: 4 (over y, x), expert: 8 (over z, core).
Axes of the slice: x: 2, y: 2, z: 4, core: 2. Of those that a mesh axis runs over, the one named last changes fastest.
Arguments:
- tokens: bfloat16 [4096, 1536], P(('rep', 'expert')), may hold values from -6 to 6
- routes: int32 [4096, 4], P(('rep', 'expert')), may hold values from 0 to 7, all different within a row; in each aligned block of 128 rows (0 to 127, 128 to 255, ...) at most 80 rows name the same one
- gates: bfloat16 [4096, 4], P(('rep', 'expert')), may hold values from 0.049804688 to 1
- output_grad: bfloat16 [4096, 1536], P(('rep', 'expert')), may hold values from -6 to 6
- w_in: bfloat16 [8, 1536, 768], P('expert', 'rep'), may hold values from -0.15625 to 0.15625
- w_out: bfloat16 [8, 384, 1536], P('expert', None, 'rep'), may hold values from -0.3125 to 0.3125
- momentum_in: bfloat16 [8, 1536, 768], P('expert', 'rep'), may hold values from -24 to 24
- momentum_out: bfloat16 [8, 384, 1536], P('expert', None, 'rep'), may hold values from -24 to 24
Outputs:
- token_grad: bfloat16 [4096, 1536], P(('rep', 'expert'))
- gate_grad: bfloat16 [4096, 4], P(('rep', 'expert'))
- new_momentum_in: bfloat16 [8, 1536, 768], P('expert', 'rep')
- new_momentum_out: bfloat16 [8, 384, 1536], P('expert', None, 'rep')
Inputs may be any that keep to these rules, and one draw needn't show every extreme that they name: `routes`: each row names 4 different experts. Within the 128 rows of one device no expert is named by more than 80 rows, and on some devices one expert is named by exactly 80 rows.
All inputs are finite; a program needn't handle non-finite values.
Results may differ from a plain program's by a relative error of at most 0.012.
Values may be sent and summed in bfloat16 or wider, within the bound.
No kernel may reach another device: no remote copies, remote signals or barrier semaphores. Data moves between devices by JAX's collectives and lax.ppermute only.
A program may use at most 64 MiB of HBM per device.

v0:
```python
import jax
import jax.numpy as jnp
from jax import lax
from jax.sharding import PartitionSpec as P

momentum_decay = 0.9


def slot_positions(routes, experts):
    flat_routes = routes.reshape(-1)
    one_hot = (flat_routes[:, None] == jnp.arange(experts, dtype=jnp.int32)[None, :]).astype(
        jnp.int32
    )
    earlier = jnp.cumsum(one_hot, axis=0) - one_hot
    return jnp.sum(earlier * one_hot, axis=1)


def forward_pass(x_rows, weight_in, weight_out):
    width_ffn = weight_out.shape[0]
    both = jnp.dot(x_rows, weight_in, preferred_element_type=jnp.float32)
    gate_pre = both[:, :width_ffn]
    up_part = both[:, width_ffn:]
    silu_gate = jax.nn.silu(gate_pre)
    hidden = (silu_gate * up_part).astype(jnp.bfloat16)
    expert_out = jnp.dot(hidden, weight_out, preferred_element_type=jnp.float32)
    return (gate_pre, up_part, silu_gate, hidden, expert_out)


def per_device(tokens, routes, gates, output_grad, w_in, w_out, momentum_in, momentum_out):
    tok_dev, width = tokens.shape
    top_count = routes.shape[1]
    senders = lax.axis_size("expert")
    local_count = w_in.shape[0]
    experts = senders * local_count
    capacity = max(2, min(tok_dev, 5 * tok_dev * top_count // (4 * experts)))
    slot_count = experts * capacity
    target = routes.reshape(-1) * capacity + slot_positions(routes, experts)
    token_ids = jnp.repeat(jnp.arange(tok_dev, dtype=jnp.int32), top_count)
    source_row = jnp.full((slot_count,), tok_dev, jnp.int32).at[target].set(token_ids)
    slot_gate = jnp.zeros((slot_count,), jnp.bfloat16).at[target].set(gates.reshape(-1))
    zero_row = jnp.zeros((1, width), jnp.bfloat16)
    sent_tokens = jnp.concatenate([tokens, zero_row], axis=0)[source_row].reshape(
        experts, capacity, width
    )
    sent_grads = jnp.concatenate([output_grad, zero_row], axis=0)[source_row].reshape(
        experts, capacity, width
    )
    sent_gate = slot_gate.reshape(experts, capacity)
    whole_in, whole_out = (
        lax.all_gather(w_in, "rep", axis=1, tiled=True),
        lax.all_gather(w_out, "rep", axis=2, tiled=True),
    )

    def local_rows(received, expert):
        shaped = received.reshape((senders, local_count) + received.shape[1:])
        return shaped[:, expert].reshape((senders * capacity,) + received.shape[2:])

    got_tokens, got_grads, got_gate = (
        lax.all_to_all(sent_tokens, "expert", split_axis=0, concat_axis=0, tiled=True),
        lax.all_to_all(sent_grads, "expert", split_axis=0, concat_axis=0, tiled=True),
        lax.all_to_all(sent_gate, "expert", split_axis=0, concat_axis=0, tiled=True),
    )
    forward = [forward_pass(local_rows(got_tokens, 0), whole_in[0], whole_out[0])]
    expert = 0
    gate_pre, up_part, silu_gate, hidden, expert_out = forward[expert]
    dy_rows = local_rows(got_grads, expert)
    gate_grad = jnp.sum(expert_out * dy_rows.astype(jnp.float32), axis=1).astype(jnp.bfloat16)
    scaled = (
        local_rows(got_gate, expert).astype(jnp.float32)[:, None] * dy_rows.astype(jnp.float32)
    ).astype(jnp.bfloat16)
    scaled_rows = [scaled]
    gate_rows = [gate_grad]
    parts_out = [
        lax.dot_general(
            hidden, scaled, (((0,), (0,)), ((), ())), preferred_element_type=jnp.float32
        )
    ]
    grad_out_all = jnp.stack(parts_out)
    summed_out = lax.psum_scatter(
        grad_out_all.astype(jnp.bfloat16), "rep", scatter_dimension=2, tiled=True
    ).astype(jnp.float32)
    expert = 0
    gate_pre, up_part, silu_gate, hidden, expert_out = forward[expert]
    hidden_grad = lax.dot_general(
        scaled_rows[expert],
        whole_out[expert],
        (((1,), (1,)), ((), ())),
        preferred_element_type=jnp.float32,
    )
    sigma = jax.nn.sigmoid(gate_pre)
    dgu = jnp.concatenate(
        [hidden_grad * up_part * sigma * (1.0 + gate_pre * (1.0 - sigma)), hidden_grad * silu_gate],
        axis=1,
    ).astype(jnp.bfloat16)
    row_grad = lax.dot_general(
        dgu, whole_in[expert], (((1,), (1,)), ((), ())), preferred_element_type=jnp.float32
    ).astype(jnp.bfloat16)
    row_grads = row_grad.reshape(senders, 1, capacity, width)
    parts_in = [
        lax.dot_general(
            local_rows(got_tokens, expert),
            dgu,
            (((0,), (0,)), ((), ())),
            preferred_element_type=jnp.float32,
        )
    ]
    grad_in_all = jnp.stack(parts_in)
    back_send = row_grads.reshape(experts, capacity, width)
    gate_send = jnp.stack([item.reshape(senders, capacity) for item in gate_rows], axis=1).reshape(
        experts, capacity
    )
    back_rows, back_gate = (
        lax.all_to_all(back_send, "expert", split_axis=0, concat_axis=0, tiled=True),
        lax.all_to_all(gate_send, "expert", split_axis=0, concat_axis=0, tiled=True),
    )
    picked = back_rows.reshape(slot_count, width)[target].reshape(tok_dev, top_count, width)
    token_grad = jnp.sum(picked.astype(jnp.float32), axis=1).astype(jnp.bfloat16)
    gate_grad_out = back_gate.reshape(-1)[target].reshape(tok_dev, top_count)
    summed_in = lax.psum_scatter(
        grad_in_all.astype(jnp.bfloat16), "rep", scatter_dimension=1, tiled=True
    ).astype(jnp.float32)
    new_momentum_in = (momentum_decay * momentum_in.astype(jnp.float32) + summed_in).astype(
        jnp.bfloat16
    )
    new_momentum_out = (momentum_decay * momentum_out.astype(jnp.float32) + summed_out).astype(
        jnp.bfloat16
    )
    return (token_grad, gate_grad_out, new_momentum_in, new_momentum_out)


def solution(mesh):
    in_specs = (
        P(("rep", "expert"), None),
        P(("rep", "expert"), None),
        P(("rep", "expert"), None),
        P(("rep", "expert"), None),
        P("expert", "rep", None),
        P("expert", None, "rep"),
        P("expert", "rep", None),
        P("expert", None, "rep"),
    )
    out_specs = (
        P(("rep", "expert"), None),
        P(("rep", "expert"), None),
        P("expert", "rep", None),
        P("expert", None, "rep"),
    )
    return jax.shard_map(
        per_device, mesh=mesh, in_specs=in_specs, out_specs=out_specs, check_vma=False
    )
```

profile of v0, /device:TPU:0, one launch (start us, length us, event | category | flops | bytes accessed | tf_op | source)
XLA Modules:
  0.0 234.5 jit_solution(2111614646956164823)
XLA Ops:
  7.2 0.8 copy.30
  8.2 0.7 broadcast_multiply_fusion
  8.9 1.1 reduce-window.6
  10.0 0.2 slice_reduce_fusion
  10.5 0.8 copy.32
  11.3 0.1 reshape.166
  11.5 3.8 %scatter_custom_fusion = bf16[640]{0:T(1024)(128)(2,1)S(1)} fusion(s32[512]{0:T(512)S(1)} %bitcast.60, bf16[512]{0:T(512)(128)(2,1)S(1)} %reshape.166, bf16[]{:T(256)} %constant.9.clone.1), kind=kCustom, calls=%fused_computation.47 | custom fusion | bytes 1282 | tf_op jit(solution)/shard_map/scatter | solution.py:40
  15.3 0.7 all_to_all.25
  16.0 6.4 %all-to-all-start = ((bf16[8,1,80]{2,1,0:T(2,128)(2,1)}), bf16[8,1,80]{2,1,0:T(2,128)(2,1)S(1)}, u32[]{:S(2)}, u32[]{:S(2)}) async-start(bf16[8,1,80]{2,1,0:T(2,128)(2,1)} %all_to_all.25), calls=%async_computation | async-start | bytes 8192 | tf_op jit(solution)/shard_map/all_to_all | solution.py:61
  22.4 2.4 %scatter_custom_fusion.1 = s32[640]{0:T(1024)S(1)} fusion(s32[512]{0:T(512)S(1)} %bitcast.61, s32[512]{0:T(512)S(1)} %reshape.174, s32[]{:T(128)} %constant.13.clone.1), kind=kCustom, calls=%fused_computation.44 | custom fusion | bytes 2564 | tf_op jit(solution)/shard_map/scatter | solution.py:39
  24.9 1.0 concatenate.10
  25.9 3.7 %gather_fusion = bf16[640,1536]{1,0:T(8,128)(2,1)} fusion(bf16[129,1536]{1,0:T(8,128)(2,1)S(1)} %concatenate.10, s32[1024]{0:T(1024)S(1)} %pad_clamp_fusion.1), kind=kCustom, calls=%fused_computation | custom fusion | bytes 3934720 | tf_op jit(solution)/shard_map/gather | solution.py:45
  29.6 5.2 %all-to-all-start.1 = ((bf16[8,80,1536]{2,1,0:T(8,128)(2,1)}), bf16[8,80,1536]{2,1,0:T(8,128)(2,1)S(1)}, u32[]{:S(2)}, u32[]{:S(2)}) async-start(bf16[8,80,1536]{2,1,0:T(8,128)(2,1)} %bitcast.55), calls=%async_computation.1 | async-start | bytes 3932160 | tf_op jit(solution)/shard_map/all_to_all | solution.py:60
  34.9 0.7 all-gather.5.cloned.1.call-update
  35.6 3.8 %gather_fusion.1 = bf16[640,1536]{1,0:T(8,128)(2,1)} fusion(bf16[129,1536]{1,0:T(8,128)(2,1)S(1)} %concatenate.11, s32[1024]{0:T(1024)S(1)} %pad_clamp_fusion.1), kind=kCustom, calls=%fused_computation.1 | custom fusion | bytes 3934720 | tf_op jit(solution)/shard_map/gather | solution.py:42
  39.4 41.7 %all-to-all-done.1 = bf16[8,80,1536]{2,1,0:T(8,128)(2,1)S(1)} async-done(((bf16[8,80,1536]{2,1,0:T(8,128)(2,1)}), bf16[8,80,1536]{2,1,0:T(8,128)(2,1)S(1)}, u32[]{:S(2)}, u32[]{:S(2)}) %all-to-all-start.1) | async-done | bytes 1966112 | tf_op jit(solution)/shard_map/all_to_all | solution.py:60
  81.1 4.3 %all-to-all-start.2 = ((bf16[8,80,1536]{2,1,0:T(8,128)(2,1)}), bf16[8,80,1536]{2,1,0:T(8,128)(2,1)}, u32[]{:S(2)}, u32[]{:S(2)}) async-start(bf16[8,80,1536]{2,1,0:T(8,128)(2,1)} %bitcast.54), calls=%async_computation.2 | async-start | bytes 3932160 | tf_op jit(solution)/shard_map/all_to_all | solution.py:59
  85.5 0.7 all-gather.3.cloned.1.call-update
  86.2 0.2 reduce-scatter.7.cloned.1.call-start
  86.5 1.6 fusion
  88.1 1.7 fusion.2
  89.8 41.8 %all-to-all-done.2 = bf16[8,80,1536]{2,1,0:T(8,128)(2,1)} async-done(((bf16[8,80,1536]{2,1,0:T(8,128)(2,1)}), bf16[8,80,1536]{2,1,0:T(8,128)(2,1)}, u32[]{:S(2)}, u32[]{:S(2)}) %all-to-all-start.2) | async-done | bytes 1966112 | tf_op jit(solution)/shard_map/all_to_all | solution.py:59
  131.6 5.7 %fusion.6 = f32[640,768]{0,1:T(8,128)} fusion(bf16[640,1536]{1,0:T(8,128)(2,1)} %bitcast.9, bf16[1,1536,768]{2,1,0:T(8,128)(2,1)} %all-gather.5.cloned.1.call-done), kind=kOutput, calls=%fused_computation.18 | convolution fusion | flops 1509949440 | bytes 6291456 | tf_op jit(solution)/shard_map/dot_general | solution.py:20
  137.3 4.8 %multiply_convert_fusion.2 = (bf16[640,384]{0,1:T(8,128)(2,1)}, bf16[640,384]{0,1:T(8,128)(2,1)}, bf16[640,384]{0,1:T(8,128)(2,1)S(1)}) fusion(f32[640,768]{0,1:T(8,128)} %fusion.6, bf16[640,1536]{1,0:T(8,128)(2,1)} %bitcast.57, bf16[1,384,1536]{2,1,0:T(8,128)(2,1)} %all-gather.3.cloned.1.call-done), kind=kOutput, calls=%fused_computation.28 | convolution fusion | flops 758661120 | bytes 6586368 | tf_op jit(solution)/shard_map/dot_general | solution.py:84
  142.2 0.8 copy-done.4
  142.9 1.1 fusion.4
  144.0 4.6 %copy.39 = bf16[1,384,1536]{1,0,2:T(2,128)(2,1)} copy(bf16[1,384,1536]{2,1,0:T(8,128)(2,1)S(1)} %fusion.4) | data formatting | bytes 2359296
  148.6 3.0 %copy.43 = bf16[1536,1,384]{2,0,1:T(8,128)(2,1)} copy(bf16[1536,1,384]{2,1,0:T(2,128)(2,1)} %bitcast.53) | data formatting | bytes 2359296
  151.7 5.0 %fusion.3 = bf16[1,1536,768]{2,1,0:T(8,128)(2,1)} fusion(bf16[640,1536]{1,0:T(8,128)(2,1)} %bitcast.9, bf16[640,384]{0,1:T(8,128)(2,1)S(1)} %copy-done.7, bf16[640,384]{0,1:T(8,128)(2,1)S(1)} %copy-done.6), kind=kOutput, calls=%fused_computation.14 | convolution fusion | flops 1513095168 | bytes 5308416 | tf_op jit(solution)/shard_map/dot_general | solution.py:100
  156.8 1.0 copy-done.5
  157.8 2.6 %fusion.1 = bf16[640]{0:T(1024)(128)(2,1)S(1)} fusion(bf16[8,80,1536]{2,1,0:T(8,128)(2,1)S(1)} %all-to-all-done.1, bf16[640,384]{0,1:T(8,128)(2,1)S(1)} %copy-done.5, bf16[1,384,1536]{2,1,0:T(8,128)(2,1)} %all-gather.3.cloned.1.call-done), kind=kOutput, calls=%fused_computation.10 | convolution fusion | flops 757923200 | bytes 3638528 | tf_op jit(solution)/shard_map/dot_general | solution.py:25
  160.4 0.7 convert_element_type.123
  161.1 3.3 %all-to-all-start.4 = ((bf16[8,1,80]{2,1,0:T(2,128)(2,1)}), bf16[8,1,80]{2,1,0:T(2,128)(2,1)S(1)}, u32[]{:S(2)}, u32[]{:S(2)}) async-start(bf16[8,1,80]{2,1,0:T(2,128)(2,1)} %convert_element_type.123), calls=%async_computation.4 | async-start | bytes 8192 | tf_op jit(solution)/shard_map/all_to_all | solution.py:114
  164.4 4.9 %convolution_convert_fusion.1 = bf16[640,1536]{1,0:T(8,128)(2,1)} fusion(bf16[1,1536,768]{2,1,0:T(8,128)(2,1)} %all-gather.5.cloned.1.call-done, bf16[640,384]{0,1:T(8,128)(2,1)} %get-tuple-element.17, bf16[640,384]{0,1:T(8,128)(2,1)S(1)} %copy-done.6), kind=kOutput, calls=%fused_computation.13 | convolution fusion | flops 1512898560 | bytes 5308416 | tf_op jit(solution)/shard_map/dot_general | solution.py:95
  169.3 0.6 all-to-all-done.4
  169.8 4.5 %all-to-all-start.3 = ((bf16[8,80,1536]{2,1,0:T(8,128)(2,1)}), bf16[8,80,1536]{2,1,0:T(8,128)(2,1)S(1)}, u32[]{:S(2)}, u32[]{:S(2)}) async-start(bf16[8,80,1536]{2,1,0:T(8,128)(2,1)} %bitcast.58), calls=%async_computation.3 | async-start | bytes 3932160 | tf_op jit(solution)/shard_map/all_to_all | solution.py:113
  174.5 3.5 %gather_fusion.3 = bf16[512]{0:T(512)(128)(2,1)S(1)} fusion(bf16[640]{0:T(1024)(128)(2,1)S(1)} %reshape.125, s32[1024]{0:T(1024)S(1)} %pad_clamp_fusion), kind=kCustom, calls=%fused_computation.3 | custom fusion | bytes 4096 | tf_op jit(solution)/shard_map/gather | solution.py:118
  178.0 0.1 reshape.126
  178.1 0.7 copy.37
  178.8 0.7 reduce-scatter.7.cloned.1.call-done
  179.4 1.3 reshape_bitcast_fusion
  180.7 0.9 copy.40
  181.6 0.8 add_convert_fusion.1
  182.4 38.2 %all-to-all-done.3 = bf16[8,80,1536]{2,1,0:T(8,128)(2,1)S(1)} async-done(((bf16[8,80,1536]{2,1,0:T(8,128)(2,1)}), bf16[8,80,1536]{2,1,0:T(8,128)(2,1)S(1)}, u32[]{:S(2)}, u32[]{:S(2)}) %all-to-all-start.3) | async-done | bytes 1966112 | tf_op jit(solution)/shard_map/all_to_all | solution.py:113
  220.6 2.1 gather_fusion.2
  222.7 0.4 reshape.124
  223.1 2.8 %reduce_sum.34 = bf16[128,1536]{1,0:T(8,128)(2,1)} reduce(bf16[128,4,1536]{2,1,0:T(4,128)(2,1)S(1)} %reshape.124, bf16[]{:T(256)} %constant.9.clone.1), dimensions={1}, to_apply=%region_5.6 | reduce | flops 589824 | bytes 1966082 | tf_op jit(solution)/shard_map/reduce_sum | solution.py:117
  226.0 2.1 add_convert_fusion
  (43 shorter events, 1.1 us)
Async XLA Ops:
  16.0 13.7 %all-to-all-start = ((bf16[8,1,80]{2,1,0:T(2,128)(2,1)}), bf16[8,1,80]{2,1,0:T(2,128)(2,1)S(1)}, u32[]{:S(2)}, u32[]{:S(2)}) async-start(bf16[8,1,80]{2,1,0:T(2,128)(2,1)} %all_to_all.25), calls=%async_computation | async-start | bytes 8192 | tf_op jit(solution)/shard_map/all_to_all | solution.py:61
  29.6 6.0 %copy-start.2 = (bf16[128,1536]{1,0:T(8,128)(2,1)S(1)}, bf16[128,1536]{1,0:T(8,128)(2,1)}, u32[]{:S(2)}) copy-start(bf16[128,1536]{1,0:T(8,128)(2,1)} %param.8) | copy-start | bytes 1179652
  29.6 51.5 %all-to-all-start.1 = ((bf16[8,80,1536]{2,1,0:T(8,128)(2,1)}), bf16[8,80,1536]{2,1,0:T(8,128)(2,1)S(1)}, u32[]{:S(2)}, u32[]{:S(2)}) async-start(bf16[8,80,1536]{2,1,0:T(8,128)(2,1)} %bitcast.55), calls=%async_computation.1 | async-start | bytes 3932160 | tf_op jit(solution)/shard_map/all_to_all | solution.py:60
  34.9 96.8 %all-gather.5.cloned.1.call-start = ((), (), s32[]{:S(2)}) async-start(), calls=%async_computation.8 | async-start | bytes 2949120 | tf_op jit(solution)/shard_map/all_gather | solution.py:50
  81.1 50.6 %all-to-all-start.2 = ((bf16[8,80,1536]{2,1,0:T(8,128)(2,1)}), bf16[8,80,1536]{2,1,0:T(8,128)(2,1)}, u32[]{:S(2)}, u32[]{:S(2)}) async-start(bf16[8,80,1536]{2,1,0:T(8,128)(2,1)} %bitcast.54), calls=%async_computation.2 | async-start | bytes 3932160 | tf_op jit(solution)/shard_map/all_to_all | solution.py:59
  85.4 51.9 %all-gather.3.cloned.1.call-start = ((), (), s32[]{:S(2)}) async-start(), calls=%async_computation.7 | async-start | bytes 1474560 | tf_op jit(solution)/shard_map/all_gather | solution.py:51
  86.2 93.3 %reduce-scatter.7.cloned.1.call-start = ((), (), s32[]{:S(2)}) async-start(), calls=%async_computation.10 | async-start | bytes 1474560
  137.3 5.6 %copy-start = (bf16[640,1536]{1,0:T(8,128)(2,1)S(1)}, bf16[640,1536]{1,0:T(8,128)(2,1)}, u32[]{:S(2)}) copy-start(bf16[640,1536]{1,0:T(8,128)(2,1)} %fusion.2) | copy-start | bytes 5898244
  142.2 0.8 copy-start.4
  148.6 3.1 %copy-start.6 = (bf16[640,384]{0,1:T(8,128)(2,1)S(1)}, bf16[640,384]{0,1:T(8,128)(2,1)}, u32[]{:S(2)}) copy-start(bf16[640,384]{0,1:T(8,128)(2,1)} %get-tuple-element.16) | copy-start | bytes 1474564
  148.6 3.1 %copy-start.7 = (bf16[640,384]{0,1:T(8,128)(2,1)S(1)}, bf16[640,384]{0,1:T(8,128)(2,1)}, u32[]{:S(2)}) copy-start(bf16[640,384]{0,1:T(8,128)(2,1)} %get-tuple-element.17) | copy-start | bytes 1474564
  151.7 74.3 %reduce-scatter.5.cloned.1.call-start = ((), (), s32[]{:S(2)}) async-start(), calls=%async_computation.9 | async-start | bytes 2949120 | tf_op jit(solution)/shard_map/reduce_scatter | solution.py:119
  156.8 1.1 copy-start.5
  161.1 8.8 %all-to-all-start.4 = ((bf16[8,1,80]{2,1,0:T(2,128)(2,1)}), bf16[8,1,80]{2,1,0:T(2,128)(2,1)S(1)}, u32[]{:S(2)}, u32[]{:S(2)}) async-start(bf16[8,1,80]{2,1,0:T(2,128)(2,1)} %convert_element_type.123), calls=%async_computation.4 | async-start | bytes 8192 | tf_op jit(solution)/shard_map/all_to_all | solution.py:114
  169.8 50.7 %all-to-all-start.3 = ((bf16[8,80,1536]{2,1,0:T(8,128)(2,1)}), bf16[8,80,1536]{2,1,0:T(8,128)(2,1)S(1)}, u32[]{:S(2)}, u32[]{:S(2)}) async-start(bf16[8,80,1536]{2,1,0:T(8,128)(2,1)} %bitcast.58), calls=%async_computation.3 | async-start | bytes 3932160 | tf_op jit(solution)/shard_map/all_to_all | solution.py:113
  174.3 7.2 %copy-start.3 = (bf16[1,384,384]{2,1,0:T(8,128)(2,1)S(1)}, bf16[1,384,384]{2,1,0:T(8,128)(2,1)}, u32[]{:S(2)}) copy-start(bf16[1,384,384]{2,1,0:T(8,128)(2,1)} %param.15) | copy-start | bytes 884740
  223.1 2.9 %copy-start.1 = (bf16[1,384,768]{2,1,0:T(8,128)(2,1)S(1)}, bf16[1,384,768]{2,1,0:T(8,128)(2,1)}, u32[]{:S(2)}) copy-start(bf16[1,384,768]{2,1,0:T(8,128)(2,1)} %param.14) | copy-start | bytes 1769476
Sparse Core Ops, SparseCore 0:
  37.5 38.7 all-gather.4
  88.0 28.7 all-gather.2
  151.8 27.6 reduce-scatter.6
  182.3 37.3 reduce-scatter.4
where the time goes:
time: 235 us
  waiting for transfers between devices  124 us (53%)
  local copies, waits for them, and re-layouts  37.1 us (16%)
  matrix products  24.1 us (10%)
  starting transfers between devices  24 us (10%)
  between operations  14 us (6%)
  other arithmetic  11 us (5%)
    all_to_all x1, waiting for transfers between devices, per_device(): lax.all_to_all(sent_tokens, 'expert', split_axis=0, concat_axis=0, tiled=...  41.8 us
    all_to_all x1, waiting for transfers between devices, per_device(): lax.all_to_all(sent_grads, 'expert', split_axis=0, concat_axis=0, tiled=T...  41.7 us
    all_to_all x1, waiting for transfers between devices, per_device(): lax.all_to_all(back_send, 'expert', split_axis=0, concat_axis=0, tiled=True)  38.2 us
    unnamed x23, local copies, waits for them, and re-layouts  13.8 us
    all_to_all x1, starting transfers between devices, per_device(): lax.all_to_all(sent_gate, 'expert', split_axis=0, concat_axis=0, tiled=True)  6.35 us
    dot_general x1, matrix products, forward_pass(): both = jnp.dot(x_rows, weight_in, preferred_element_type=jnp.float32)  5.68 us
    all_to_all x1, starting transfers between devices, per_device(): lax.all_to_all(sent_grads, 'expert', split_axis=0, concat_axis=0, tiled=T...  5.23 us
    dot_general x1, matrix products, per_device(): lax.dot_general(local_rows(got_tokens, expert), dgu, (((0,), (0,)), ((),...  5.03 us
  transfers between devices with their start and end apart: 9, of which 5 were waited for; matrix products, arithmetic and copies ran while one was open for 20% of the time, Pallas kernels for 0%

commit v1 on v0

--- a/solution.py
+++ b/solution.py
@@ -1,9 +1,236 @@
+import functools
+
 import jax
 import jax.numpy as jnp
 from jax import lax
+from jax.experimental import pallas as pl
+from jax.experimental.pallas import tpu as pltpu
 from jax.sharding import PartitionSpec as P
 
 momentum_decay = 0.9
+bf16 = jnp.bfloat16
+f32 = jnp.float32
+
+
+def dot(a, b, dims):
+    return lax.dot_general(a, b, ((dims[0], dims[1]), ((), ())), preferred_element_type=f32)
+
+
+def pack_kernel(x_ref, y_ref, routes_ref, gates_ref, out_ref):
+    tok = x_ref.shape[0]
+    experts = out_ref.shape[0] - 2 * tok
+    out_ref[0:tok, :] = x_ref[...]
+    out_ref[tok : 2 * tok, :] = y_ref[...]
+    ids = lax.broadcasted_iota(jnp.int32, (experts, tok), 0)
+    dense = jnp.zeros((experts, tok), f32)
+    for k in range(routes_ref.shape[0]):
+        row = routes_ref[k : k + 1, :]
+        gate = gates_ref[k : k + 1, :].astype(f32)
+        dense = dense + jnp.where(ids == row, gate, 0.0)
+    tail = jnp.zeros((experts, out_ref.shape[1] - tok), f32)
+    out_ref[2 * tok :, :] = jnp.concatenate([dense, tail], axis=1).astype(bf16)
+
+
+def expert_kernel(pairs, last, *refs):
+    ids_ref, refs = refs[0], refs[1:]
+    blocks, refs = refs[: 2 * pairs], refs[2 * pairs :]
+    (own_ref, one_ref, two_ref, three_a_ref, three_b_ref), refs = refs[:5], refs[5:]
+    if last:
+        (prev_in_ref, prev_out_ref), refs = refs[:2], refs[2:]
+        keep_ref, give_ref, mine_ref, r1a_ref, r1b_ref, r2a_ref, r2b_ref, r3a_ref, r3b_ref = refs[:9]
+        refs = refs[9:]
+    else:
+        keep_ref, give_ref, acc_in_ref, acc_out_ref = refs[:4]
+        refs = refs[4:]
+    win, wout, xs, ys, dgus, chs = refs[:6]
+    if last:
+        acc_in_ref, acc_out_ref = refs[6:8]
+    rep, expert = ids_ref[0], ids_ref[1]
+    shard, ffn = own_ref.shape[0], wout.shape[0]
+    half = shard // 2
+    width = win.shape[0]
+    both_w = win.shape[1]
+    experts = keep_ref.shape[1] - (keep_ref.shape[1] // 128) * 128
+    tok = keep_ref.shape[1] - experts
+
+    def place(index, ref, lo, rows):
+        at = pl.multiple_of(index * shard, 128)
+        win[pl.ds(at + lo, rows), :] = ref[:, 0:both_w]
+        wout[lo : lo + rows, pl.ds(at, shard)] = ref[:, both_w:]
+
+    place(rep, own_ref, 0, shard)
+    place(rep ^ 1, one_ref, 0, shard)
+    place(rep ^ 2, two_ref, 0, shard)
+    place(rep ^ 3, three_a_ref, 0, half)
+    place(rep ^ 3, three_b_ref, half, half)
+    columns = []
+    for n, block in enumerate(blocks):
+        xs[n * tok : (n + 1) * tok, :] = block[0:tok, :]
+        ys[n * tok : (n + 1) * tok, :] = block[tok : 2 * tok, :]
+        table = block[2 * tok :, 0:tok].astype(f32)
+        pick = lax.broadcasted_iota(jnp.int32, table.shape, 0) == expert
+        row = jnp.where(pick, table, 0.0)
+        columns.append(jnp.sum(row.T, axis=1, keepdims=True))
+    for n in range(len(blocks)):
+        rows = slice(n * tok, (n + 1) * tok)
+        gate = columns[n]
+        both = dot(xs[rows, :], win[...], ((1,), (0,)))
+        back = dot(ys[rows, :], wout[...], ((1,), (1,)))
+        g = both[:, :ffn]
+        u = both[:, ffn:]
+        s = 1.0 / (1.0 + jnp.exp(-g))
+        silu = g * s
+        hidden = (silu * u).astype(bf16).astype(f32)
+        gate_grad = jnp.sum(hidden * back, axis=1, keepdims=True)
+        chs[rows, :] = (hidden * gate).astype(bf16)
+        dh = back * gate
+        dgus[rows, :ffn] = (dh * u * s * (1.0 + g * (1.0 - s))).astype(bf16)
+        dgus[rows, ffn:] = (dh * silu).astype(bf16)
+        out = keep_ref if n % 2 == 0 else give_ref
+        out[n // 2, 0:tok, :] = dot(dgus[rows, :], win[...], ((1,), (1,))).astype(bf16)
+        spread = jnp.broadcast_to(gate_grad, (tok, experts)).T
+        pick = lax.broadcasted_iota(jnp.int32, spread.shape, 0) == expert
+        spread = jnp.where(pick, spread, 0.0)
+        tail = jnp.zeros((experts, width - tok), f32)
+        out[n // 2, tok:, :] = jnp.concatenate([spread, tail], axis=1).astype(bf16)
+    if not last:
+        acc_in_ref[...] = dot(xs[...], dgus[...], ((0,), (0,)))
+        acc_out_ref[...] = dot(chs[...], ys[...], ((0,), (0,)))
+        return
+    acc_in_ref[...] = prev_in_ref[...] + dot(xs[...], dgus[...], ((0,), (0,)))
+    acc_out_ref[...] = prev_out_ref[...] + dot(chs[...], ys[...], ((0,), (0,)))
+
+    def fetch(index, ref, lo, rows):
+        at = pl.multiple_of(index * shard, 128)
+        ref[:, 0:both_w] = acc_in_ref[pl.ds(at + lo, rows), :].astype(bf16)
+        ref[:, both_w:] = acc_out_ref[lo : lo + rows, pl.ds(at, shard)].astype(bf16)
+
+    fetch(rep ^ 3, r3a_ref, 0, half)
+    fetch(rep ^ 3, r3b_ref, half, half)
+    fetch(rep ^ 1, r1a_ref, 0, half)
+    fetch(rep ^ 1, r1b_ref, half, half)
+    fetch(rep ^ 2, r2a_ref, 0, half)
+    fetch(rep ^ 2, r2b_ref, half, half)
+    fetch(rep, mine_ref, 0, shard)
+
+
+def run_experts(ids, blocks, weights, previous, tok, experts, width, ffn):
+    last = previous is not None
+    pairs = len(blocks) // 2
+    shard = weights[0].shape[0]
+    cols = weights[0].shape[1]
+    both_w = 2 * ffn
+    rows = 2 * pairs * tok
+    S = jax.ShapeDtypeStruct
+    outs = [S((pairs, tok + experts, width), bf16)] * 2
+    scratch = [
+        pltpu.VMEM((width, both_w), bf16),
+        pltpu.VMEM((ffn, width), bf16),
+        pltpu.VMEM((rows, width), bf16),
+        pltpu.VMEM((rows, width), bf16),
+        pltpu.VMEM((rows, both_w), bf16),
+        pltpu.VMEM((rows, ffn), bf16),
+    ]
+    if last:
+        outs += [S((shard, cols), bf16)] + [S((shard // 2, cols), bf16)] * 6
+        scratch += [pltpu.VMEM((width, both_w), f32), pltpu.VMEM((ffn, width), f32)]
+    else:
+        outs += [S((width, both_w), f32), S((ffn, width), f32)]
+    operands = [ids, *blocks, *weights] + (list(previous) if last else [])
+    flops = 2 * rows * width * ffn * 8
+    return pl.pallas_call(
+        functools.partial(expert_kernel, pairs, last),
+        out_shape=outs,
+        in_specs=[pl.BlockSpec(memory_space=pltpu.SMEM)]
+        + [pl.BlockSpec(memory_space=pltpu.VMEM)] * (len(operands) - 1),
+        out_specs=[pl.BlockSpec(memory_space=pltpu.VMEM)] * len(outs),
+        scratch_shapes=scratch,
+        compiler_params=pltpu.CompilerParams(vmem_limit_bytes=40 * 1024 * 1024),
+        cost_estimate=pl.CostEstimate(flops=flops, bytes_accessed=8 * 1024 * 1024, transcendentals=rows * ffn),
+        name="experts_last" if last else "experts_first",
+    )(*operands)
+
+
+def per_device_dense(tokens, routes, gates, output_grad, w_in, w_out, momentum_in, momentum_out):
+    tok, width = tokens.shape
+    ffn = w_out.shape[1]
+    experts = lax.axis_size("expert")
+    chips = experts // 2
+    rep = lax.axis_index("rep")
+    expert = lax.axis_index("expert")
+    ids = jnp.stack([rep, expert]).astype(jnp.int32)
+
+    def over_rep(value, bits):
+        return lax.ppermute(value, "rep", [(i, i ^ bits) for i in range(4)])
+
+    def over_chips(value, chip_pairs):
+        return lax.ppermute(
+            value, "expert", [(2 * a + c, 2 * b + c) for a, b in chip_pairs for c in range(2)]
+        )
+
+    def partner(value):
+        return lax.ppermute(value, "expert", [(i, i ^ 1) for i in range(experts)])
+
+    own_w = jnp.concatenate([w_in[0], w_out[0]], axis=1)
+    shard = own_w.shape[0]
+    half = shard // 2
+    one_w = over_rep(own_w, 1)
+    two_w = over_rep(own_w, 2)
+    block = pl.pallas_call(
+        pack_kernel,
+        out_shape=jax.ShapeDtypeStruct((2 * tok + experts, width), bf16),
+        name="pack_block",
+    )(tokens, output_grad, routes.T, gates.T)
+    far = over_chips(block, [(z, z ^ 2) for z in range(chips)])
+    near = over_chips(block, [(z, z ^ 1) for z in range(chips)])
+    middle = over_chips(block, [(1, 2), (2, 1)])
+    block_p = partner(block)
+    three_a = over_rep(one_w[:half], 2)
+    three_b = over_rep(two_w[half:], 1)
+    weights = (own_w, one_w, two_w, three_a, three_b)
+    ends = over_chips(far, [(2, 3), (1, 0)])
+    near_p = partner(near)
+    far_p = partner(far)
+    at_end = (expert // 2 == 0) | (expert // 2 == chips - 1)
+    cross = jnp.where(at_end, ends, middle)
+    cross_p = partner(cross)
+    keep, give, acc_in, acc_out = run_experts(
+        ids, [block, block_p, near, near_p, far, far_p], weights, None, tok, experts, width, ffn
+    )
+    got = partner(give)
+    both = (keep.astype(f32) + got.astype(f32)).astype(bf16)
+    home_near = over_chips(both[1], [(z, z ^ 1) for z in range(chips)])
+    home_far = over_chips(both[2], [(z, z ^ 2) for z in range(chips)])
+    keep2, give2, mine, r1a, r1b, r2a, r2b, r3a, r3b = run_experts(
+        ids, [cross, cross_p], weights, (acc_in, acc_out), tok, experts, width, ffn
+    )
+    s3a = over_rep(r3a, 2)
+    s3b = over_rep(r3b, 1)
+    t2a = over_rep(r2a, 2)
+    t1b = over_rep(r1b, 1)
+    got2 = partner(give2)
+    both2 = (keep2.astype(f32) + got2.astype(f32)).astype(bf16)
+    home_cross = over_chips(both2[0], [(z, z ^ 3) for z in range(chips)])
+    r1a = (r1a.astype(f32) + s3a.astype(f32)).astype(bf16)
+    r2b = (r2b.astype(f32) + s3b.astype(f32)).astype(bf16)
+    t1a = over_rep(r1a, 1)
+    t2b = over_rep(r2b, 2)
+    total = (
+        both[0].astype(f32)
+        + home_near.astype(f32)
+        + home_far.astype(f32)
+        + home_cross.astype(f32)
+    )
+    token_grad = total[:tok].astype(bf16)
+    table = total[tok:, :tok]
+    picked = routes.T[:, None, :] == jnp.arange(experts, dtype=jnp.int32)[None, :, None]
+    gate_grad = jnp.sum(jnp.where(picked, table[None], 0.0), axis=1).astype(bf16).T
+    sum_a = mine[:half].astype(f32) + t1a.astype(f32) + t2a.astype(f32)
+    sum_b = mine[half:].astype(f32) + t1b.astype(f32) + t2b.astype(f32)
+    summed = jnp.concatenate([sum_a, sum_b], axis=0)
+    new_in = (momentum_decay * momentum_in.astype(f32) + summed[None, :, : 2 * ffn]).astype(bf16)
+    new_out = (momentum_decay * momentum_out.astype(f32) + summed[None, :, 2 * ffn :]).astype(bf16)
+    return token_grad, gate_grad, new_in, new_out
 
 
 def slot_positions(routes, experts):
@@ -26,7 +253,7 @@
     return (gate_pre, up_part, silu_gate, hidden, expert_out)
 
 
-def per_device(tokens, routes, gates, output_grad, w_in, w_out, momentum_in, momentum_out):
+def per_device_sparse(tokens, routes, gates, output_grad, w_in, w_out, momentum_in, momentum_out):
     tok_dev, width = tokens.shape
     top_count = routes.shape[1]
     senders = lax.axis_size("expert")
@@ -145,6 +372,22 @@
         P("expert", "rep", None),
         P("expert", None, "rep"),
     )
+    def per_device(tokens, routes, *rest):
+        tok, width = tokens.shape
+        experts = mesh.shape["expert"]
+        w_in, w_out = rest[2], rest[3]
+        dense = (
+            experts == 8
+            and mesh.shape["rep"] == 4
+            and w_in.shape[0] == 1
+            and tok == 128
+            and width >= tok
+            and w_out.shape[1] == w_in.shape[1]
+            and w_in.shape[1] % 128 == 0
+        )
+        step = per_device_dense if dense else per_device_sparse
+        return step(tokens, routes, *rest)
+
     return jax.shard_map(
         per_device, mesh=mesh, in_specs=in_specs, out_specs=out_specs, check_vma=False
     )

time: 235 us -> 155 us (0.66)
  waiting for transfers between devices: 124 us -> 88 us
  local copies, waits for them, and re-layouts: 37.1 us -> 3.1 us
  Pallas kernels: 0 us -> 26.5 us
  matrix products: 24.1 us -> 0 us
  between operations: 14 us -> 0.85 us
  starting transfers between devices: 24 us -> 31.9 us
  other arithmetic: 11 us -> 4.85 us
    all_to_all x5 -> x0, waiting for transfers between devices: 122 us -> none  [the longest x1 41.8 us: per_device(): lax.all_to_all(sent_tokens, 'expert', split_axis=0, concat_axis=0, tiled=...]
    ppermute x0 -> x23, waiting for transfers between devices: none -> 88 us  [the longest x7 68.2 us: over_chips(): lax.ppermute(value, 'expert', [(2 * a + c, 2 * b + c) for a, b in chip_pa...]
    ppermute x0 -> x23, starting transfers between devices: none -> 31.9 us  [the longest x7 17.3 us: over_chips(): lax.ppermute(value, 'expert', [(2 * a + c, 2 * b + c) for a, b in chip_pa...]
    pallas_call x0 -> x3, Pallas kernels: none -> 26.5 us  [the longest x2 24.4 us: run_experts(): pl.pallas_call(functools.partial(expert_kernel, pairs, last), out_shape=o...]
    dot_general x6 -> x0, matrix products: 24.1 us -> none  [the longest x1 5.68 us: forward_pass(): both = jnp.dot(x_rows, weight_in, preferred_element_type=jnp.float32)]
    all_to_all x5 -> x0, starting transfers between devices: 23.7 us -> none  [the longest x1 6.35 us: per_device(): lax.all_to_all(sent_gate, 'expert', split_axis=0, concat_axis=0, tiled=True)]
    unnamed x23 -> x12, local copies, waits for them, and re-layouts: 13.8 us -> 0.67 us
    gather x4 -> x0, local copies, waits for them, and re-layouts: 13.1 us -> none  [the longest x1 3.75 us: per_device(): jnp.concatenate([tokens, zero_row], axis=0)[source_row]]
  transfers between devices with their start and end apart: 9 -> 23, of which waited for: 5 -> 8; matrix products, arithmetic and copies ran while one was open for 20% -> 3% of each run, Pallas kernels for 0% -> 11%
where the time goes in v1:
time: 155 us
  waiting for transfers between devices  88 us (57%)
  starting transfers between devices  31.9 us (21%)
  Pallas kernels  26.5 us (17%)
  other arithmetic  4.85 us (3%)
  local copies, waits for them, and re-layouts  3.1 us (2%)
    ppermute x7, waiting for transfers between devices, over_chips(): lax.ppermute(value, 'expert', [(2 * a + c, 2 * b + c) for a, b in chip_pa...  68.2 us
    pallas_call x2, Pallas kernels, run_experts(): pl.pallas_call(functools.partial(expert_kernel, pairs, last), out_shape=o...  24.4 us
    ppermute x10, waiting for transfers between devices, over_rep(): return lax.ppermute(value, 'rep', [(i, i ^ bits) for i in range(4)])  19.8 us
    ppermute x7, starting transfers between devices, over_chips(): lax.ppermute(value, 'expert', [(2 * a + c, 2 * b + c) for a, b in chip_pa...  17.3 us
    ppermute x10, starting transfers between devices, over_rep(): return lax.ppermute(value, 'rep', [(i, i ^ bits) for i in range(4)])  13.3 us
  transfers between devices with their start and end apart: 23, of which 8 were waited for; matrix products, arithmetic and copies ran while one was open for 3% of the time, Pallas kernels for 11%

profile of v1, /device:TPU:0, one launch (start us, length us, event | category | flops | bytes accessed | tf_op | source)
XLA Modules:
  0.0 155.3 jit_solution(8499887916957109991)
XLA Ops:
  0.7 2.2 %pack_block.1.refs_1_ = bf16[264,1536]{1,0:T(8,128)(2,1)} custom-call(bf16[128,1536]{1,0:T(8,128)(2,1)} %x_ref.1, bf16[128,1536]{1,0:T(8,128)(2,1)} %y_ref.1, s32[4,128]{1,0:T(4,128)} %bitcast.34, bf16[4,128]{1,0:T(4,128)(2,1)} %bitcast.37), custom_call_target="tpu_custom_call" | custom-call | tf_op jit(solution)/shard_map/pack_block/pallas_call | solution.py:179
  2.8 4.1 %collective-permute-start.3 = (bf16[264,1536]{1,0:T(8,128)(2,1)}, bf16[264,1536]{1,0:T(8,128)(2,1)}, u32[]{:S(2)}, u32[]{:S(2)}) collective-permute-start(bf16[264,1536]{1,0:T(8,128)(2,1)} %pack_block.1.refs_1_), channel_id=1, source_target_pairs={{0,4},{1,5},{2,6},{3,7},{4,0},{5,1},{6,2},{7,3},{8,12},{9,13},{10,... | collective-permute-start | bytes 2433032 | tf_op jit(solution)/shard_map/ppermute | solution.py:167
  6.9 1.6 %collective-permute-start.1 = (bf16[264,1536]{1,0:T(8,128)(2,1)}, bf16[264,1536]{1,0:T(8,128)(2,1)}, u32[]{:S(2)}, u32[]{:S(2)}) collective-permute-start(bf16[264,1536]{1,0:T(8,128)(2,1)} %pack_block.1.refs_1_), channel_id=1, source_target_pairs={{0,2},{1,3},{2,0},{3,1},{4,6},{5,7},{6,4},{7,5},{8,10},{9,11},{10,... | collective-permute-start | bytes 2433032 | tf_op jit(solution)/shard_map/ppermute | solution.py:167
  8.5 1.6 %collective-permute-start.6 = (bf16[384,1152]{1,0:T(8,128)(2,1)S(1)}, bf16[384,1152]{1,0:T(8,128)(2,1)S(1)}, u32[]{:S(2)}, u32[]{:S(2)}) collective-permute-start(bf16[384,1152]{1,0:T(8,128)(2,1)S(1)} %pad_maximum_fusion.refs_7_.refs_3_), channel_id=1, source_target_pairs={{0,16},{8,24},{16,0},{24,8},{1,17},{9,25},{17,1},{25,9},{2,18},{10... | collective-permute-start | bytes 2654216 | tf_op jit(solution)/shard_map/ppermute | solution.py:164
  10.1 1.5 collective-permute-start.5
  11.6 0.7 collective-permute-start.13
  12.3 31.2 %collective-permute-done.3.refs_5_ = bf16[264,1536]{1,0:T(8,128)(2,1)} collective-permute-done((bf16[264,1536]{1,0:T(8,128)(2,1)}, bf16[264,1536]{1,0:T(8,128)(2,1)}, u32[]{:S(2)}, u32[]{:S(2)}) %collective-permute-start.3) | collective-permute-done | bytes 811040 | tf_op jit(solution)/shard_map/ppermute | solution.py:167
  43.5 1.3 collective-permute-start.12
  44.8 0.1 collective-permute-start
  44.9 0.5 collective-permute-start.4
  45.4 0.1 collective-permute-start.2
  45.5 0.8 slice.46
  46.3 0.8 slice.45
  47.1 1.8 %collective-permute-start.8 = (bf16[192,1152]{1,0:T(8,128)(2,1)}, bf16[192,1152]{1,0:T(8,128)(2,1)}, u32[]{:S(2)}, u32[]{:S(2)}) collective-permute-start(bf16[192,1152]{1,0:T(8,128)(2,1)} %slice.46), channel_id=1, source_target_pairs={{0,8},{8,0},{16,24},{24,16},{1,9},{9,1},{17,25},{25,17},{2,10},{10... | collective-permute-start | bytes 1327112 | tf_op jit(solution)/shard_map/ppermute | solution.py:164
  48.9 15.2 %collective-permute-done.12 = bf16[264,1536]{1,0:T(8,128)(2,1)} collective-permute-done((bf16[264,1536]{1,0:T(8,128)(2,1)}, bf16[264,1536]{1,0:T(8,128)(2,1)}, u32[]{:S(2)}, u32[]{:S(2)}) %collective-permute-start.12) | collective-permute-done | bytes 811040 | tf_op jit(solution)/shard_map/ppermute | solution.py:167
  64.1 1.3 collective-permute-start.7
  65.4 1.2 broadcast_select_fusion.refs_1_
  66.7 0.1 collective-permute-start.14
  66.8 0.1 pad_add_fusion.refs_0_
  66.8 7.2 %collective-permute-done.7.refs_10_.refs_6_ = bf16[192,1152]{1,0:T(8,128)(2,1)} collective-permute-done((bf16[192,1152]{1,0:T(8,128)(2,1)}, bf16[192,1152]{1,0:T(8,128)(2,1)}, u32[]{:S(2)}, u32[]{:S(2)}) %collective-permute-start.7) | collective-permute-done | bytes 442400 | tf_op jit(solution)/shard_map/ppermute | solution.py:164
  74.1 16.7 %experts_first.1 = (bf16[3,136,1536]{2,1,0:T(8,128)(2,1)S(1)}, bf16[3,136,1536]{2,1,0:T(8,128)(2,1)S(1)}, f32[1536,768]{1,0:T(8,128)}, f32[384,1536]{1,0:T(8,128)S(1)}) custom-call(s32[2]{0:T(128)S(1)} %pad_add_fusion.refs_0_, bf16[264,1536]{1,0:T(8,128)(2,1)} %pack_block.1.refs_1_, bf16[264,1536]{1,0:T(8,128)(2,1)} %collective-permute-done.refs_2_, ...), custom_call_target="tpu_custom_call" | custom-call | flops 7247757312 | bytes 8388608 | tf_op jit(solution)/shard_map/experts_first/pallas_call | solution.py:141
  90.8 7.6 %experts_last.1 = (bf16[1,136,1536]{2,1,0:T(8,128)(2,1)S(1)}, bf16[1,136,1536]{2,1,0:T(8,128)(2,1)S(1)}, bf16[384,1152]{1,0:T(8,128)(2,1)S(1)}, bf16[192,1152]{1...) custom-call(s32[2]{0:T(128)S(1)} %pad_add_fusion.refs_0_, ...), custom_call_target="tpu_custom_call" | custom-call | flops 2415919104 | bytes 8388608 | tf_op jit(solution)/shard_map/experts_last/pallas_call | solution.py:141
  98.5 0.5 collective-permute-start.9
  99.0 0.8 collective-permute-start.17
  99.8 1.2 collective-permute-start.19
  101.1 0.8 collective-permute-start.20
  101.8 1.3 collective-permute-start.21
  103.1 0.1 fusion.9
  103.2 8.9 %collective-permute-done.17 = bf16[192,1152]{1,0:T(8,128)(2,1)S(1)} collective-permute-done((bf16[192,1152]{1,0:T(8,128)(2,1)S(1)}, bf16[192,1152]{1,0:T(8,128)(2,1)S(1)}, u32[]{:S(2)}, u32[]{:S(2)}) %collective-permute-start.17) | collective-permute-done | bytes 442400 | tf_op jit(solution)/shard_map/ppermute | solution.py:164
  112.1 5.8 %collective-permute-start.16 = (bf16[136,1536]{1,0:T(8,128)(2,1)S(1)}, bf16[136,1536]{1,0:T(8,128)(2,1)S(1)}, u32[]{:S(2)}, u32[]{:S(2)}) collective-permute-start(bf16[136,1536]{1,0:T(8,128)(2,1)S(1)} %fusion.9), channel_id=1, source_target_pairs={{0,6},{1,7},{2,4},{3,5},{4,2},{5,3},{6,0},{7,1},{8,14},{9,15},{10,... | collective-permute-start | bytes 1253384 | tf_op jit(solution)/shard_map/ppermute | solution.py:167
  117.8 0.1 add_convert_fusion.2
  117.9 0.3 add_convert_fusion
  118.3 0.1 collective-permute-start.10
  118.4 3.7 %collective-permute-done.21 = bf16[192,1152]{1,0:T(8,128)(2,1)S(1)} collective-permute-done((bf16[192,1152]{1,0:T(8,128)(2,1)S(1)}, bf16[192,1152]{1,0:T(8,128)(2,1)S(1)}, u32[]{:S(2)}, u32[]{:S(2)}) %collective-permute-start.21) | collective-permute-done | bytes 442400 | tf_op jit(solution)/shard_map/ppermute | solution.py:164
  122.1 3.8 %collective-permute-start.11 = (bf16[136,1536]{1,0:T(8,128)(2,1)S(1)}, bf16[136,1536]{1,0:T(8,128)(2,1)S(1)}, u32[]{:S(2)}, u32[]{:S(2)}) collective-permute-start(bf16[136,1536]{1,0:T(8,128)(2,1)S(1)} %get-tuple-element.31), channel_id=1, source_target_pairs={{0,4},{1,5},{2,6},{3,7},{4,0},{5,1},{6,2},{7,3},{8,12},{9,13},{10,... | collective-permute-start | bytes 1253384 | tf_op jit(solution)/shard_map/ppermute | solution.py:167
  126.0 0.1 add_convert_fusion.1
  126.1 2.3 %collective-permute-done.16 = bf16[136,1536]{1,0:T(8,128)(2,1)S(1)} collective-permute-done((bf16[136,1536]{1,0:T(8,128)(2,1)S(1)}, bf16[136,1536]{1,0:T(8,128)(2,1)S(1)}, u32[]{:S(2)}, u32[]{:S(2)}) %collective-permute-start.16) | collective-permute-done | bytes 417824 | tf_op jit(solution)/shard_map/ppermute | solution.py:167
  128.4 1.5 collective-permute-start.18
  129.9 7.1 %collective-permute-done.10 = bf16[136,1536]{1,0:T(8,128)(2,1)S(1)} collective-permute-done((bf16[136,1536]{1,0:T(8,128)(2,1)S(1)}, bf16[136,1536]{1,0:T(8,128)(2,1)S(1)}, u32[]{:S(2)}, u32[]{:S(2)}) %collective-permute-start.10) | collective-permute-done | bytes 417824 | tf_op jit(solution)/shard_map/ppermute | solution.py:167
  136.9 1.6 %collective-permute-start.22 = (bf16[192,1152]{1,0:T(8,128)(2,1)S(1)}, bf16[192,1152]{1,0:T(8,128)(2,1)S(1)}, u32[]{:S(2)}, u32[]{:S(2)}) collective-permute-start(bf16[192,1152]{1,0:T(8,128)(2,1)S(1)} %add_convert_fusion.1), channel_id=1, source_target_pairs={{0,16},{8,24},{16,0},{24,8},{1,17},{9,25},{17,1},{25,9},{2,18},{10... | collective-permute-start | bytes 1327112 | tf_op jit(solution)/shard_map/ppermute | solution.py:164
  138.5 12.4 %collective-permute-done.11 = bf16[136,1536]{1,0:T(8,128)(2,1)S(1)} collective-permute-done((bf16[136,1536]{1,0:T(8,128)(2,1)S(1)}, bf16[136,1536]{1,0:T(8,128)(2,1)S(1)}, u32[]{:S(2)}, u32[]{:S(2)}) %collective-permute-start.11) | collective-permute-done | bytes 417824 | tf_op jit(solution)/shard_map/ppermute | solution.py:167
  150.9 0.2 fusion.5
  151.2 0.8 slice.74
  151.9 0.6 select_reduce_fusion
  152.6 0.3 convert_add_fusion
  152.9 0.6 copy-done.3
  153.5 0.8 fusion.8
  154.3 1.0 fusion.3
  (30 shorter events, 0.3 us)
Async XLA Ops:
  0.6 7.8 %copy-start.4 = (bf16[1,384,384]{2,1,0:T(8,128)(2,1)S(1)}, bf16[1,384,384]{2,1,0:T(8,128)(2,1)}, u32[]{:S(2)}) copy-start(bf16[1,384,384]{2,1,0:T(8,128)(2,1)} %param.13) | copy-start | bytes 884740
  0.6 7.8 %copy-start.1 = (bf16[1,384,768]{2,1,0:T(8,128)(2,1)S(1)}, bf16[1,384,768]{2,1,0:T(8,128)(2,1)}, u32[]{:S(2)}) copy-start(bf16[1,384,768]{2,1,0:T(8,128)(2,1)} %param.12) | copy-start | bytes 1769476
  2.8 40.7 %collective-permute-start.3 = (bf16[264,1536]{1,0:T(8,128)(2,1)}, bf16[264,1536]{1,0:T(8,128)(2,1)}, u32[]{:S(2)}, u32[]{:S(2)}) collective-permute-start(bf16[264,1536]{1,0:T(8,128)(2,1)} %pack_block.1.refs_1_), channel_id=1, source_target_pairs={{0,4},{1,5},{2,6},{3,7},{4,0},{5,1},{6,2},{7,3},{8,12},{9,13},{10,... | collective-permute-start | bytes 2433032 | tf_op jit(solution)/shard_map/ppermute | solution.py:167
  6.9 37.9 %collective-permute-start.1 = (bf16[264,1536]{1,0:T(8,128)(2,1)}, bf16[264,1536]{1,0:T(8,128)(2,1)}, u32[]{:S(2)}, u32[]{:S(2)}) collective-permute-start(bf16[264,1536]{1,0:T(8,128)(2,1)} %pack_block.1.refs_1_), channel_id=1, source_target_pairs={{0,2},{1,3},{2,0},{3,1},{4,6},{5,7},{6,4},{7,5},{8,10},{9,11},{10,... | collective-permute-start | bytes 2433032 | tf_op jit(solution)/shard_map/ppermute | solution.py:167
  8.5 36.4 %collective-permute-start.6 = (bf16[384,1152]{1,0:T(8,128)(2,1)S(1)}, bf16[384,1152]{1,0:T(8,128)(2,1)S(1)}, u32[]{:S(2)}, u32[]{:S(2)}) collective-permute-start(bf16[384,1152]{1,0:T(8,128)(2,1)S(1)} %pad_maximum_fusion.refs_7_.refs_3_), channel_id=1, source_target_pairs={{0,16},{8,24},{16,0},{24,8},{1,17},{9,25},{17,1},{25,9},{2,18},{10... | collective-permute-start | bytes 2654216 | tf_op jit(solution)/shard_map/ppermute | solution.py:164
  10.1 35.3 %collective-permute-start.5 = (bf16[384,1152]{1,0:T(8,128)(2,1)S(1)}, bf16[384,1152]{1,0:T(8,128)(2,1)S(1)}, u32[]{:S(2)}, u32[]{:S(2)}) collective-permute-start(bf16[384,1152]{1,0:T(8,128)(2,1)S(1)} %pad_maximum_fusion.refs_7_.refs_3_), channel_id=1, source_target_pairs={{0,8},{8,0},{16,24},{24,16},{1,9},{9,1},{17,25},{25,17},{2,10},{10... | collective-permute-start | bytes 2654216 | tf_op jit(solution)/shard_map/ppermute | solution.py:164
  11.6 35.5 %collective-permute-start.13 = (bf16[264,1536]{1,0:T(8,128)(2,1)}, bf16[264,1536]{1,0:T(8,128)(2,1)S(1)}, u32[]{:S(2)}, u32[]{:S(2)}) collective-permute-start(bf16[264,1536]{1,0:T(8,128)(2,1)} %pack_block.1.refs_1_), channel_id=1, source_target_pairs={{2,4},{3,5},{4,2},{5,3},{10,12},{11,13},{12,10},{13,11},{18,20},{1... | collective-permute-start | bytes 2433032 | tf_op jit(solution)/shard_map/ppermute | solution.py:167
  43.5 20.6 %collective-permute-start.12 = (bf16[264,1536]{1,0:T(8,128)(2,1)}, bf16[264,1536]{1,0:T(8,128)(2,1)}, u32[]{:S(2)}, u32[]{:S(2)}) collective-permute-start(bf16[264,1536]{1,0:T(8,128)(2,1)} %collective-permute-done.3.refs_5_), channel_id=1, source_target_pairs={{4,6},{5,7},{2,0},{3,1},{12,14},{13,15},{10,8},{11,9},{20,22},{21,... | collective-permute-start | bytes 2433032 | tf_op jit(solution)/shard_map/ppermute | solution.py:167
  44.8 21.8 %collective-permute-start = (bf16[264,1536]{1,0:T(8,128)(2,1)}, bf16[264,1536]{1,0:T(8,128)(2,1)}, u32[]{:S(2)}, u32[]{:S(2)}) collective-permute-start(bf16[264,1536]{1,0:T(8,128)(2,1)} %pack_block.1.refs_1_), channel_id=1, source_target_pairs={{0,1},{1,0},{2,3},{3,2},{4,5},{5,4},{6,7},{7,6},{8,9},{9,8},{10,11... | collective-permute-start | bytes 2433032 | tf_op jit(solution)/shard_map/ppermute | solution.py:172
  44.9 29.1 %collective-permute-start.4 = (bf16[264,1536]{1,0:T(8,128)(2,1)}, bf16[264,1536]{1,0:T(8,128)(2,1)}, u32[]{:S(2)}, u32[]{:S(2)}) collective-permute-start(bf16[264,1536]{1,0:T(8,128)(2,1)} %collective-permute-done.3.refs_5_), channel_id=1, source_target_pairs={{0,1},{1,0},{2,3},{3,2},{4,5},{5,4},{6,7},{7,6},{8,9},{9,8},{10,11... | collective-permute-start | bytes 2433032 | tf_op jit(solution)/shard_map/ppermute | solution.py:172
  45.4 28.7 %collective-permute-start.2 = (bf16[264,1536]{1,0:T(8,128)(2,1)}, bf16[264,1536]{1,0:T(8,128)(2,1)}, u32[]{:S(2)}, u32[]{:S(2)}) collective-permute-start(bf16[264,1536]{1,0:T(8,128)(2,1)} %collective-permute-done.1.refs_3_), channel_id=1, source_target_pairs={{0,1},{1,0},{2,3},{3,2},{4,5},{5,4},{6,7},{7,6},{8,9},{9,8},{10,11... | collective-permute-start | bytes 2433032 | tf_op jit(solution)/shard_map/ppermute | solution.py:172
  47.1 17.0 %copy-start = (bf16[264,1536]{1,0:T(8,128)(2,1)}, bf16[264,1536]{1,0:T(8,128)(2,1)S(1)}, u32[]{:S(2)}) copy-start(bf16[264,1536]{1,0:T(8,128)(2,1)S(1)} %collective-permute-done.13) | copy-start | bytes 2433028
  47.1 19.7 %collective-permute-start.8 = (bf16[192,1152]{1,0:T(8,128)(2,1)}, bf16[192,1152]{1,0:T(8,128)(2,1)}, u32[]{:S(2)}, u32[]{:S(2)}) collective-permute-start(bf16[192,1152]{1,0:T(8,128)(2,1)} %slice.46), channel_id=1, source_target_pairs={{0,8},{8,0},{16,24},{24,16},{1,9},{9,1},{17,25},{25,17},{2,10},{10... | collective-permute-start | bytes 1327112 | tf_op jit(solution)/shard_map/ppermute | solution.py:164
  64.1 9.9 %collective-permute-start.7 = (bf16[192,1152]{1,0:T(8,128)(2,1)}, bf16[192,1152]{1,0:T(8,128)(2,1)}, u32[]{:S(2)}, u32[]{:S(2)}) collective-permute-start(bf16[192,1152]{1,0:T(8,128)(2,1)} %slice.45), channel_id=1, source_target_pairs={{0,16},{8,24},{16,0},{24,8},{1,17},{9,25},{17,1},{25,9},{2,18},{10... | collective-permute-start | bytes 1327112 | tf_op jit(solution)/shard_map/ppermute | solution.py:164
  66.7 24.1 %collective-permute-start.14 = (bf16[264,1536]{1,0:T(8,128)(2,1)S(1)}, bf16[264,1536]{1,0:T(8,128)(2,1)}, u32[]{:S(2)}, u32[]{:S(2)}) collective-permute-start(bf16[264,1536]{1,0:T(8,128)(2,1)S(1)} %broadcast_select_fusion.refs_1_), channel_id=1, source_target_pairs={{0,1},{1,0},{2,3},{3,2},{4,5},{5,4},{6,7},{7,6},{8,9},{9,8},{10,11... | collective-permute-start | bytes 2433032 | tf_op jit(solution)/shard_map/ppermute | solution.py:172
  98.5 3.4 %collective-permute-start.15 = (bf16[1,136,1536]{2,1,0:T(8,128)(2,1)S(1)}, bf16[1,136,1536]{2,1,0:T(8,128)(2,1)S(1)}, u32[]{:S(2)}, u32[]{:S(2)}) collective-permute-start(bf16[1,136,1536]{2,1,0:T(8,128)(2,1)S(1)} %get-tuple-element.22), channel_id=1, source_target_pairs={{0,1},{1,0},{2,3},{3,2},{4,5},{5,4},{6,7},{7,6},{8,9},{9,8},{10,11... | collective-permute-start | bytes 1253384 | tf_op jit(solution)/shard_map/ppermute | solution.py:172
  98.5 19.4 %collective-permute-start.9 = (bf16[3,136,1536]{2,1,0:T(8,128)(2,1)S(1)}, bf16[3,136,1536]{2,1,0:T(8,128)(2,1)S(1)}, u32[]{:S(2)}, u32[]{:S(2)}) collective-permute-start(bf16[3,136,1536]{2,1,0:T(8,128)(2,1)S(1)} %get-tuple-element.18), channel_id=1, source_target_pairs={{0,1},{1,0},{2,3},{3,2},{4,5},{5,4},{6,7},{7,6},{8,9},{9,8},{10,11... | collective-permute-start | bytes 3760136 | tf_op jit(solution)/shard_map/ppermute | solution.py:172
  99.0 13.0 %collective-permute-start.17 = (bf16[192,1152]{1,0:T(8,128)(2,1)S(1)}, bf16[192,1152]{1,0:T(8,128)(2,1)S(1)}, u32[]{:S(2)}, u32[]{:S(2)}) collective-permute-start(bf16[192,1152]{1,0:T(8,128)(2,1)S(1)} %get-tuple-element.25), channel_id=1, source_target_pairs={{0,16},{8,24},{16,0},{24,8},{1,17},{9,25},{17,1},{25,9},{2,18},{10... | collective-permute-start | bytes 1327112 | tf_op jit(solution)/shard_map/ppermute | solution.py:164
  99.8 52.7 %collective-permute-start.19 = (bf16[192,1152]{1,0:T(8,128)(2,1)S(1)}, bf16[192,1152]{1,0:T(8,128)(2,1)S(1)}, u32[]{:S(2)}, u32[]{:S(2)}) collective-permute-start(bf16[192,1152]{1,0:T(8,128)(2,1)S(1)} %get-tuple-element.26), channel_id=1, source_target_pairs={{0,16},{8,24},{16,0},{24,8},{1,17},{9,25},{17,1},{25,9},{2,18},{10... | collective-permute-start | bytes 1327112 | tf_op jit(solution)/shard_map/ppermute | solution.py:164
  101.1 51.5 %collective-permute-start.20 = (bf16[192,1152]{1,0:T(8,128)(2,1)S(1)}, bf16[192,1152]{1,0:T(8,128)(2,1)S(1)}, u32[]{:S(2)}, u32[]{:S(2)}) collective-permute-start(bf16[192,1152]{1,0:T(8,128)(2,1)S(1)} %get-tuple-element.27), channel_id=1, source_target_pairs={{0,8},{8,0},{16,24},{24,16},{1,9},{9,1},{17,25},{25,17},{2,10},{10... | collective-permute-start | bytes 1327112 | tf_op jit(solution)/shard_map/ppermute | solution.py:164
  101.8 20.3 %collective-permute-start.21 = (bf16[192,1152]{1,0:T(8,128)(2,1)S(1)}, bf16[192,1152]{1,0:T(8,128)(2,1)S(1)}, u32[]{:S(2)}, u32[]{:S(2)}) collective-permute-start(bf16[192,1152]{1,0:T(8,128)(2,1)S(1)} %get-tuple-element.29), channel_id=1, source_target_pairs={{0,8},{8,0},{16,24},{24,16},{1,9},{9,1},{17,25},{25,17},{2,10},{10... | collective-permute-start | bytes 1327112 | tf_op jit(solution)/shard_map/ppermute | solution.py:164
  112.1 16.3 %collective-permute-start.16 = (bf16[136,1536]{1,0:T(8,128)(2,1)S(1)}, bf16[136,1536]{1,0:T(8,128)(2,1)S(1)}, u32[]{:S(2)}, u32[]{:S(2)}) collective-permute-start(bf16[136,1536]{1,0:T(8,128)(2,1)S(1)} %fusion.9), channel_id=1, source_target_pairs={{0,6},{1,7},{2,4},{3,5},{4,2},{5,3},{6,0},{7,1},{8,14},{9,15},{10,... | collective-permute-start | bytes 1253384 | tf_op jit(solution)/shard_map/ppermute | solution.py:167
  118.3 18.6 %collective-permute-start.10 = (bf16[136,1536]{1,0:T(8,128)(2,1)S(1)}, bf16[136,1536]{1,0:T(8,128)(2,1)S(1)}, u32[]{:S(2)}, u32[]{:S(2)}) collective-permute-start(bf16[136,1536]{1,0:T(8,128)(2,1)S(1)} %get-tuple-element.30), channel_id=1, source_target_pairs={{0,2},{1,3},{2,0},{3,1},{4,6},{5,7},{6,4},{7,5},{8,10},{9,11},{10,... | collective-permute-start | bytes 1253384 | tf_op jit(solution)/shard_map/ppermute | solution.py:167
  122.1 28.8 %collective-permute-start.11 = (bf16[136,1536]{1,0:T(8,128)(2,1)S(1)}, bf16[136,1536]{1,0:T(8,128)(2,1)S(1)}, u32[]{:S(2)}, u32[]{:S(2)}) collective-permute-start(bf16[136,1536]{1,0:T(8,128)(2,1)S(1)} %get-tuple-element.31), channel_id=1, source_target_pairs={{0,4},{1,5},{2,6},{3,7},{4,0},{5,1},{6,2},{7,3},{8,12},{9,13},{10,... | collective-permute-start | bytes 1253384 | tf_op jit(solution)/shard_map/ppermute | solution.py:167
  126.1 25.9 %copy-start.5 = (s32[128,4]{0,1:T(4,128)S(1)}, s32[128,4]{0,1:T(4,128)}, u32[]{:S(2)}) copy-start(s32[128,4]{0,1:T(4,128)} %param.9) | copy-start | bytes 6148
  128.4 24.2 %collective-permute-start.18 = (bf16[192,1152]{1,0:T(8,128)(2,1)S(1)}, bf16[192,1152]{1,0:T(8,128)(2,1)S(1)}, u32[]{:S(2)}, u32[]{:S(2)}) collective-permute-start(bf16[192,1152]{1,0:T(8,128)(2,1)S(1)} %add_convert_fusion.2), channel_id=1, source_target_pairs={{0,8},{8,0},{16,24},{24,16},{1,9},{9,1},{17,25},{25,17},{2,10},{10... | collective-permute-start | bytes 1327112 | tf_op jit(solution)/shard_map/ppermute | solution.py:164
  136.9 15.6 %collective-permute-start.22 = (bf16[192,1152]{1,0:T(8,128)(2,1)S(1)}, bf16[192,1152]{1,0:T(8,128)(2,1)S(1)}, u32[]{:S(2)}, u32[]{:S(2)}) collective-permute-start(bf16[192,1152]{1,0:T(8,128)(2,1)S(1)} %add_convert_fusion.1), channel_id=1, source_target_pairs={{0,16},{8,24},{16,0},{24,8},{1,17},{9,25},{17,1},{25,9},{2,18},{10... | collective-permute-start | bytes 1327112 | tf_op jit(solution)/shard_map/ppermute | solution.py:164
  152.5 1.0 copy-start.3
  152.9 1.4 copy-start.2

commit v2 on v1

--- a/solution.py
+++ b/solution.py
@@ -7,7 +7,9 @@
 from jax.experimental.pallas import tpu as pltpu
 from jax.sharding import PartitionSpec as P
 
+
 momentum_decay = 0.9
+GROUP = 2
 bf16 = jnp.bfloat16
 f32 = jnp.float32
 
@@ -33,8 +35,9 @@
 
 def expert_kernel(pairs, last, *refs):
     ids_ref, refs = refs[0], refs[1:]
-    blocks, refs = refs[: 2 * pairs], refs[2 * pairs :]
-    (own_ref, one_ref, two_ref, three_a_ref, three_b_ref), refs = refs[:5], refs[5:]
+    n_blocks = 4 if last else 2 * pairs
+    blocks, refs = refs[:n_blocks], refs[n_blocks:]
+    pieces, refs = refs[:8], refs[8:]
     if last:
         (prev_in_ref, prev_out_ref), refs = refs[:2], refs[2:]
         keep_ref, give_ref, mine_ref, r1a_ref, r1b_ref, r2a_ref, r2b_ref, r3a_ref, r3b_ref = refs[:9]
@@ -46,8 +49,8 @@
     if last:
         acc_in_ref, acc_out_ref = refs[6:8]
     rep, expert = ids_ref[0], ids_ref[1]
-    shard, ffn = own_ref.shape[0], wout.shape[0]
-    half = shard // 2
+    half, ffn = pieces[0].shape[0], wout.shape[0]
+    shard = 2 * half
     width = win.shape[0]
     both_w = win.shape[1]
     experts = keep_ref.shape[1] - (keep_ref.shape[1] // 128) * 128
@@ -58,22 +61,44 @@
         win[pl.ds(at + lo, rows), :] = ref[:, 0:both_w]
         wout[lo : lo + rows, pl.ds(at, shard)] = ref[:, both_w:]
 
-    place(rep, own_ref, 0, shard)
-    place(rep ^ 1, one_ref, 0, shard)
-    place(rep ^ 2, two_ref, 0, shard)
-    place(rep ^ 3, three_a_ref, 0, half)
-    place(rep ^ 3, three_b_ref, half, half)
+    for j in range(4):
+        place(rep ^ j, pieces[2 * j], 0, half)
+        place(rep ^ j, pieces[2 * j + 1], half, half)
     columns = []
-    for n, block in enumerate(blocks):
+
+    def load(n, block):
         xs[n * tok : (n + 1) * tok, :] = block[0:tok, :]
         ys[n * tok : (n + 1) * tok, :] = block[tok : 2 * tok, :]
-        table = block[2 * tok :, 0:tok].astype(f32)
+
+    def column(table):
         pick = lax.broadcasted_iota(jnp.int32, table.shape, 0) == expert
-        row = jnp.where(pick, table, 0.0)
-        columns.append(jnp.sum(row.T, axis=1, keepdims=True))
-    for n in range(len(blocks)):
-        rows = slice(n * tok, (n + 1) * tok)
-        gate = columns[n]
+        columns.append(jnp.sum(jnp.where(pick, table.astype(f32), 0.0).T, axis=1, keepdims=True))
+
+    if last:
+        at_end = ids_ref[2] == 1
+
+        @pl.when(at_end)
+        def _():
+            load(0, blocks[0])
+            load(1, blocks[1])
+
+        @pl.when(jnp.logical_not(at_end))
+        def _():
+            load(0, blocks[2])
+            load(1, blocks[3])
+
+        for n in range(2):
+            end = blocks[n][2 * tok :, 0:tok].astype(f32)
+            mid = blocks[n + 2][2 * tok :, 0:tok].astype(f32)
+            column(jnp.where(at_end, end, mid))
+    else:
+        for n, block in enumerate(blocks):
+            load(n, block)
+            column(block[2 * tok :, 0:tok])
+    step = min(GROUP, 2 * pairs)
+    for first in range(0, 2 * pairs, step):
+        rows = slice(first * tok, (first + step) * tok)
+        gate = jnp.concatenate(columns[first : first + step], axis=0)
         both = dot(xs[rows, :], win[...], ((1,), (0,)))
         back = dot(ys[rows, :], wout[...], ((1,), (1,)))
         g = both[:, :ffn]
@@ -86,13 +111,16 @@
         dh = back * gate
         dgus[rows, :ffn] = (dh * u * s * (1.0 + g * (1.0 - s))).astype(bf16)
         dgus[rows, ffn:] = (dh * silu).astype(bf16)
-        out = keep_ref if n % 2 == 0 else give_ref
-        out[n // 2, 0:tok, :] = dot(dgus[rows, :], win[...], ((1,), (1,))).astype(bf16)
-        spread = jnp.broadcast_to(gate_grad, (tok, experts)).T
-        pick = lax.broadcasted_iota(jnp.int32, spread.shape, 0) == expert
-        spread = jnp.where(pick, spread, 0.0)
-        tail = jnp.zeros((experts, width - tok), f32)
-        out[n // 2, tok:, :] = jnp.concatenate([spread, tail], axis=1).astype(bf16)
+        row_grad = dot(dgus[rows, :], win[...], ((1,), (1,))).astype(bf16)
+        for n in range(first, first + step):
+            part = slice((n - first) * tok, (n - first + 1) * tok)
+            out = keep_ref if n % 2 == 0 else give_ref
+            out[n // 2, 0:tok, :] = row_grad[part]
+            spread = jnp.broadcast_to(gate_grad[part], (tok, experts)).T
+            pick = lax.broadcasted_iota(jnp.int32, spread.shape, 0) == expert
+            spread = jnp.where(pick, spread, 0.0)
+            tail = jnp.zeros((experts, width - tok), f32)
+            out[n // 2, tok:, :] = jnp.concatenate([spread, tail], axis=1).astype(bf16)
     if not last:
         acc_in_ref[...] = dot(xs[...], dgus[...], ((0,), (0,)))
         acc_out_ref[...] = dot(chs[...], ys[...], ((0,), (0,)))
@@ -116,8 +144,8 @@
 
 def run_experts(ids, blocks, weights, previous, tok, experts, width, ffn):
     last = previous is not None
-    pairs = len(blocks) // 2
-    shard = weights[0].shape[0]
+    pairs = 1 if last else len(blocks) // 2
+    shard = 2 * weights[0].shape[0]
     cols = weights[0].shape[1]
     both_w = 2 * ffn
     rows = 2 * pairs * tok
@@ -145,55 +173,72 @@
         + [pl.BlockSpec(memory_space=pltpu.VMEM)] * (len(operands) - 1),
         out_specs=[pl.BlockSpec(memory_space=pltpu.VMEM)] * len(outs),
         scratch_shapes=scratch,
-        compiler_params=pltpu.CompilerParams(vmem_limit_bytes=40 * 1024 * 1024),
+        compiler_params=pltpu.CompilerParams(vmem_limit_bytes=(26 if last else 24) * 1024 * 1024),
         cost_estimate=pl.CostEstimate(flops=flops, bytes_accessed=8 * 1024 * 1024, transcendentals=rows * ffn),
         name="experts_last" if last else "experts_first",
     )(*operands)
 
 
-def per_device_dense(tokens, routes, gates, output_grad, w_in, w_out, momentum_in, momentum_out):
+def finish_kernel(own_ref, t1a_ref, t1b_ref, t2a_ref, t2b_ref, min_ref, mout_ref, nin_ref, nout_ref):
+    half = t1a_ref.shape[0]
+    cols = min_ref.shape[2]
+    for lo, one, two in ((0, t1a_ref, t2a_ref), (half, t1b_ref, t2b_ref)):
+        rows = slice(lo, lo + half)
+        total = own_ref[rows, :].astype(f32) + one[...].astype(f32) + two[...].astype(f32)
+        old_in = momentum_decay * min_ref[0, rows, :].astype(f32)
+        old_out = momentum_decay * mout_ref[0, rows, :].astype(f32)
+        nin_ref[0, rows, :] = (old_in + total[:, :cols]).astype(bf16)
+        nout_ref[0, rows, :] = (old_out + total[:, cols:]).astype(bf16)
+
+
+def per_device_dense(*args):
+    return dense_step(*args)
+
+
+def dense_step(tokens, routes, gates, output_grad, w_in, w_out, momentum_in, momentum_out):
     tok, width = tokens.shape
     ffn = w_out.shape[1]
     experts = lax.axis_size("expert")
     chips = experts // 2
     rep = lax.axis_index("rep")
     expert = lax.axis_index("expert")
-    ids = jnp.stack([rep, expert]).astype(jnp.int32)
+    chip = expert // 2
+    at_end = (chip == 0) | (chip == chips - 1)
+    ids = jnp.stack([rep, expert, at_end.astype(jnp.int32)]).astype(jnp.int32)
 
     def over_rep(value, bits):
         return lax.ppermute(value, "rep", [(i, i ^ bits) for i in range(4)])
 
     def over_chips(value, chip_pairs):
-        return lax.ppermute(
-            value, "expert", [(2 * a + c, 2 * b + c) for a, b in chip_pairs for c in range(2)]
-        )
+        pairs = [(2 * a + c, 2 * b + c) for a, b in chip_pairs for c in range(2)]
+        return lax.ppermute(value, "expert", pairs)
 
     def partner(value):
         return lax.ppermute(value, "expert", [(i, i ^ 1) for i in range(experts)])
 
-    own_w = jnp.concatenate([w_in[0], w_out[0]], axis=1)
-    shard = own_w.shape[0]
-    half = shard // 2
-    one_w = over_rep(own_w, 1)
-    two_w = over_rep(own_w, 2)
+    half = w_in.shape[1] // 2
+    own_a = jnp.concatenate([w_in[0, :half], w_out[0, :half]], axis=1)
+    own_b = jnp.concatenate([w_in[0, half:], w_out[0, half:]], axis=1)
+    w1a = over_rep(own_a, 1)
+    w2b = over_rep(own_b, 2)
     block = pl.pallas_call(
         pack_kernel,
         out_shape=jax.ShapeDtypeStruct((2 * tok + experts, width), bf16),
+        compiler_params=pltpu.CompilerParams(vmem_limit_bytes=6 * 1024 * 1024),
         name="pack_block",
     )(tokens, output_grad, routes.T, gates.T)
     far = over_chips(block, [(z, z ^ 2) for z in range(chips)])
+    w1b = over_rep(own_b, 1)
+    w2a = over_rep(own_a, 2)
     near = over_chips(block, [(z, z ^ 1) for z in range(chips)])
+    block_p = partner(block)
     middle = over_chips(block, [(1, 2), (2, 1)])
-    block_p = partner(block)
-    three_a = over_rep(one_w[:half], 2)
-    three_b = over_rep(two_w[half:], 1)
-    weights = (own_w, one_w, two_w, three_a, three_b)
+    w3a = over_rep(w1a, 2)
+    w3b = over_rep(w2b, 1)
+    weights = (own_a, own_b, w1a, w1b, w2a, w2b, w3a, w3b)
+    near_p = partner(near)
     ends = over_chips(far, [(2, 3), (1, 0)])
-    near_p = partner(near)
     far_p = partner(far)
-    at_end = (expert // 2 == 0) | (expert // 2 == chips - 1)
-    cross = jnp.where(at_end, ends, middle)
-    cross_p = partner(cross)
     keep, give, acc_in, acc_out = run_experts(
         ids, [block, block_p, near, near_p, far, far_p], weights, None, tok, experts, width, ffn
     )
@@ -201,8 +246,10 @@
     both = (keep.astype(f32) + got.astype(f32)).astype(bf16)
     home_near = over_chips(both[1], [(z, z ^ 1) for z in range(chips)])
     home_far = over_chips(both[2], [(z, z ^ 2) for z in range(chips)])
+    middle_p = partner(middle)
+    ends_p = partner(ends)
     keep2, give2, mine, r1a, r1b, r2a, r2b, r3a, r3b = run_experts(
-        ids, [cross, cross_p], weights, (acc_in, acc_out), tok, experts, width, ffn
+        ids, [ends, ends_p, middle, middle_p], weights, (acc_in, acc_out), tok, experts, width, ffn
     )
     s3a = over_rep(r3a, 2)
     s3b = over_rep(r3b, 1)
@@ -211,25 +258,22 @@
     got2 = partner(give2)
     both2 = (keep2.astype(f32) + got2.astype(f32)).astype(bf16)
     home_cross = over_chips(both2[0], [(z, z ^ 3) for z in range(chips)])
-    r1a = (r1a.astype(f32) + s3a.astype(f32)).astype(bf16)
-    r2b = (r2b.astype(f32) + s3b.astype(f32)).astype(bf16)
-    t1a = over_rep(r1a, 1)
-    t2b = over_rep(r2b, 2)
-    total = (
-        both[0].astype(f32)
-        + home_near.astype(f32)
-        + home_far.astype(f32)
-        + home_cross.astype(f32)
-    )
-    token_grad = total[:tok].astype(bf16)
-    table = total[tok:, :tok]
+    t1a = over_rep((r1a.astype(f32) + s3a.astype(f32)).astype(bf16), 1)
+    t2b = over_rep((r2b.astype(f32) + s3b.astype(f32)).astype(bf16), 2)
+    parts = (both[0], home_near, home_far, home_cross)
+    token_grad = sum(p[:tok].astype(f32) for p in parts).astype(bf16)
+    table = sum(p[tok:, :tok].astype(f32) for p in parts)
     picked = routes.T[:, None, :] == jnp.arange(experts, dtype=jnp.int32)[None, :, None]
     gate_grad = jnp.sum(jnp.where(picked, table[None], 0.0), axis=1).astype(bf16).T
-    sum_a = mine[:half].astype(f32) + t1a.astype(f32) + t2a.astype(f32)
-    sum_b = mine[half:].astype(f32) + t1b.astype(f32) + t2b.astype(f32)
-    summed = jnp.concatenate([sum_a, sum_b], axis=0)
-    new_in = (momentum_decay * momentum_in.astype(f32) + summed[None, :, : 2 * ffn]).astype(bf16)
-    new_out = (momentum_decay * momentum_out.astype(f32) + summed[None, :, 2 * ffn :]).astype(bf16)
+    new_in, new_out = pl.pallas_call(
+        finish_kernel,
+        out_shape=[
+            jax.ShapeDtypeStruct(momentum_in.shape, bf16),
+            jax.ShapeDtypeStruct(momentum_out.shape, bf16),
+        ],
+        compiler_params=pltpu.CompilerParams(vmem_limit_bytes=10 * 1024 * 1024),
+        name="finish",
+    )(mine, t1a, t1b, t2a, t2b, momentum_in, momentum_out)
     return token_grad, gate_grad, new_in, new_out
 
 
@@ -372,21 +416,16 @@
         P("expert", "rep", None),
         P("expert", None, "rep"),
     )
-    def per_device(tokens, routes, *rest):
-        tok, width = tokens.shape
-        experts = mesh.shape["expert"]
-        w_in, w_out = rest[2], rest[3]
-        dense = (
-            experts == 8
-            and mesh.shape["rep"] == 4
-            and w_in.shape[0] == 1
-            and tok == 128
-            and width >= tok
-            and w_out.shape[1] == w_in.shape[1]
-            and w_in.shape[1] % 128 == 0
-        )
-        step = per_device_dense if dense else per_device_sparse
-        return step(tokens, routes, *rest)
+
+    small = mesh.shape["expert"] == 8 and mesh.shape["rep"] == 4
+
+    def per_device(*args):
+        tok, width = args[0].shape
+        w_in, w_out = args[4], args[5]
+        lanes = (tok, w_in.shape[1], w_out.shape[1], w_out.shape[2], w_in.shape[2])
+        fits = small and tok == 128 and width >= tok and all(n % 128 == 0 for n in lanes)
+        dense = fits and w_in.shape[0] == 1 and w_in.shape[1] == w_out.shape[2] == w_out.shape[1]
+        return (per_device_dense if dense else per_device_sparse)(*args)
 
     return jax.shard_map(
         per_device, mesh=mesh, in_specs=in_specs, out_specs=out_specs, check_vma=False

time: 155 us -> 144 us (0.929)
  waiting for transfers between devices: 88 us -> 78.1 us
  Pallas kernels: 26.5 us -> 18.3 us
  local copies, waits for them, and re-layouts: 3.1 us -> 10.5 us
  other arithmetic: 4.85 us -> 2.33 us
    ppermute x7, waiting for transfers between devices: 68.2 us -> 43.2 us  [over_chips(): return lax.ppermute(value, 'expert', pairs)]
    ppermute x10 -> x12, waiting for transfers between devices: 19.8 us -> 34.9 us  [over_rep(): return lax.ppermute(value, 'rep', [(i, i ^ bits) for i in range(4)])]
    unnamed x12 -> x34, local copies, waits for them, and re-layouts: 0.67 us -> 9.21 us
    pallas_call x2, Pallas kernels: 24.4 us -> 16.9 us  [run_experts(): pl.pallas_call(functools.partial(expert_kernel, pairs, last), out_shape=o...]
    slice x4 -> x0, local copies, waits for them, and re-layouts: 2.38 us -> none  [the longest x1 0.8 us: per_device_dense(): three_a = over_rep(one_w[:half], 2)]
    ppermute x10 -> x12, starting transfers between devices: 13.3 us -> 13.7 us  [over_rep(): return lax.ppermute(value, 'rep', [(i, i ^ bits) for i in range(4)])]
  transfers between devices with their start and end apart: 23 -> 26, of which waited for: 8 -> 10; matrix products, arithmetic and copies ran while one was open for 3% -> 2% of each run, Pallas kernels for 11% -> 8%
where the time goes in v2:
time: 144 us; the launch traced here: 143 us
  waiting for transfers between devices  78.1 us (54%)
  starting transfers between devices  33.1 us (23%)
  Pallas kernels  18.3 us (13%)
  local copies, waits for them, and re-layouts  10.5 us (7%)
  other arithmetic  2.33 us (2%)
    ppermute x7, waiting for transfers between devices, over_chips(): return lax.ppermute(value, 'expert', pairs)  43.2 us
    ppermute x12, waiting for transfers between devices, over_rep(): return lax.ppermute(value, 'rep', [(i, i ^ bits) for i in range(4)])  34.9 us
    ppermute x7, starting transfers between devices, over_chips(): return lax.ppermute(value, 'expert', pairs)  18.2 us
    pallas_call x2, Pallas kernels, run_experts(): pl.pallas_call(functools.partial(expert_kernel, pairs, last), out_shape=o...  16.9 us
    ppermute x12, starting transfers between devices, over_rep(): return lax.ppermute(value, 'rep', [(i, i ^ bits) for i in range(4)])  13.7 us
    unnamed x34, local copies, waits for them, and re-layouts  9.21 us
  transfers between devices with their start and end apart: 26, of which 10 were waited for; matrix products, arithmetic and copies ran while one was open for 2% of the time, Pallas kernels for 8%

profile of v2, /device:TPU:0, one launch (start us, length us, event | category | flops | bytes accessed | tf_op | source)
XLA Modules:
  0.0 143.3 jit_solution(5507286136647004608)
XLA Ops:
  0.7 1.2 slice_bitcast_fusion.4
  2.0 3.1 %collective-permute-start.8 = (bf16[192,1152]{1,0:T(8,128)(2,1)S(1)}, bf16[192,1152]{1,0:T(8,128)(2,1)S(1)}, u32[]{:S(2)}, u32[]{:S(2)}) collective-permute-start(bf16[192,1152]{1,0:T(8,128)(2,1)S(1)} %pad_maximum_fusion.1.refs_8_.refs_6_), channel_id=1, source_target_pairs={{0,16},{8,24},{16,0},{24,8},{1,17},{9,25},{17,1},{25,9},{2,18},{10... | collective-permute-start | bytes 1327112 | tf_op jit(solution)/shard_map/ppermute | solution.py:210
  5.1 2.7 %collective-permute-start.3 = (bf16[264,1536]{1,0:T(8,128)(2,1)S(1)}, bf16[264,1536]{1,0:T(8,128)(2,1)}, u32[]{:S(2)}, u32[]{:S(2)}) collective-permute-start(bf16[264,1536]{1,0:T(8,128)(2,1)S(1)} %pack_block.1.refs_1_), channel_id=1, source_target_pairs={{0,4},{1,5},{2,6},{3,7},{4,0},{5,1},{6,2},{7,3},{8,12},{9,13},{10,... | collective-permute-start | bytes 2433032 | tf_op jit(solution)/shard_map/ppermute | solution.py:214
  7.8 1.6 %collective-permute-start.5 = (bf16[192,1152]{1,0:T(8,128)(2,1)S(1)}, bf16[192,1152]{1,0:T(8,128)(2,1)}, u32[]{:S(2)}, u32[]{:S(2)}) collective-permute-start(bf16[192,1152]{1,0:T(8,128)(2,1)S(1)} %pad_maximum_fusion.refs_7_.refs_5_), channel_id=1, source_target_pairs={{0,8},{8,0},{16,24},{24,16},{1,9},{9,1},{17,25},{25,17},{2,10},{10... | collective-permute-start | bytes 1327112 | tf_op jit(solution)/shard_map/ppermute | solution.py:210
  9.3 0.5 collective-permute-start.6
  9.9 1.6 %collective-permute-start.1 = (bf16[264,1536]{1,0:T(8,128)(2,1)S(1)}, bf16[264,1536]{1,0:T(8,128)(2,1)}, u32[]{:S(2)}, u32[]{:S(2)}) collective-permute-start(bf16[264,1536]{1,0:T(8,128)(2,1)S(1)} %pack_block.1.refs_1_), channel_id=1, source_target_pairs={{0,2},{1,3},{2,0},{3,1},{4,6},{5,7},{6,4},{7,5},{8,10},{9,11},{10,... | collective-permute-start | bytes 2433032 | tf_op jit(solution)/shard_map/ppermute | solution.py:214
  11.5 3.7 %collective-permute-done.8.refs_12_.refs_10_ = bf16[192,1152]{1,0:T(8,128)(2,1)S(1)} collective-permute-done((bf16[192,1152]{1,0:T(8,128)(2,1)S(1)}, bf16[192,1152]{1,0:T(8,128)(2,1)S(1)}, u32[]{:S(2)}, u32[]{:S(2)}) %collective-permute-start.8) | collective-permute-done | bytes 442400 | tf_op jit(solution)/shard_map/ppermute | solution.py:210
  15.2 5.8 %collective-permute-done.5.refs_9_.refs_7_ = bf16[192,1152]{1,0:T(8,128)(2,1)} collective-permute-done((bf16[192,1152]{1,0:T(8,128)(2,1)S(1)}, bf16[192,1152]{1,0:T(8,128)(2,1)}, u32[]{:S(2)}, u32[]{:S(2)}) %collective-permute-start.5) | collective-permute-done | bytes 442400 | tf_op jit(solution)/shard_map/ppermute | solution.py:210
  21.0 0.5 collective-permute-start.7
  21.5 7.2 %collective-permute-done.6.refs_10_.refs_8_ = bf16[192,1152]{1,0:T(8,128)(2,1)S(1)} collective-permute-done((bf16[192,1152]{1,0:T(8,128)(2,1)S(1)}, bf16[192,1152]{1,0:T(8,128)(2,1)S(1)}, u32[]{:S(2)}, u32[]{:S(2)}) %collective-permute-start.6) | collective-permute-done | bytes 442400 | tf_op jit(solution)/shard_map/ppermute | solution.py:210
  28.7 0.8 copy-done.3
  29.4 0.7 collective-permute-start.16
  30.2 14.1 %collective-permute-done.3.refs_5_ = bf16[264,1536]{1,0:T(8,128)(2,1)} collective-permute-done((bf16[264,1536]{1,0:T(8,128)(2,1)S(1)}, bf16[264,1536]{1,0:T(8,128)(2,1)}, u32[]{:S(2)}, u32[]{:S(2)}) %collective-permute-start.3) | collective-permute-done | bytes 811040 | tf_op jit(solution)/shard_map/ppermute | solution.py:214
  44.2 1.3 collective-permute-start.14
  45.5 0.7 copy-done.5
  46.3 0.5 collective-permute-start.2
  46.8 0.9 copy-done.14
  47.7 1.5 %collective-permute-start.10 = (bf16[192,1152]{1,0:T(8,128)(2,1)S(1)}, bf16[192,1152]{1,0:T(8,128)(2,1)S(1)}, u32[]{:S(2)}, u32[]{:S(2)}) collective-permute-start(bf16[192,1152]{1,0:T(8,128)(2,1)S(1)} %collective-permute-done.8.refs_12_.refs_10_), channel_id=1, source_target_pairs={{0,8},{8,0},{16,24},{24,16},{1,9},{9,1},{17,25},{25,17},{2,10},{10... | collective-permute-start | bytes 1327112 | tf_op jit(solution)/shard_map/ppermute | solution.py:210
  49.2 0.8 copy-done.1
  50.0 0.5 collective-permute-start.9
  50.5 9.3 %collective-permute-done.10.refs_14_.refs_12_ = bf16[192,1152]{1,0:T(8,128)(2,1)S(1)} collective-permute-done((bf16[192,1152]{1,0:T(8,128)(2,1)S(1)}, bf16[192,1152]{1,0:T(8,128)(2,1)S(1)}, u32[]{:S(2)}, u32[]{:S(2)}) %collective-permute-start.10) | collective-permute-done | bytes 442400 | tf_op jit(solution)/shard_map/ppermute | solution.py:210
  59.8 0.8 copy-done.7
  60.6 3.6 %collective-permute-done.14.refs_1_ = bf16[264,1536]{1,0:T(8,128)(2,1)S(1)} collective-permute-done((bf16[264,1536]{1,0:T(8,128)(2,1)}, bf16[264,1536]{1,0:T(8,128)(2,1)S(1)}, u32[]{:S(2)}, u32[]{:S(2)}) %collective-permute-start.14) | collective-permute-done | bytes 811040 | tf_op jit(solution)/shard_map/ppermute | solution.py:214
  64.3 1.0 copy-done.2
  65.3 1.0 copy-done.4
  66.3 1.0 copy-done.6
  67.3 1.0 copy-done.8
  68.3 1.1 copy-done.15
  69.5 11.0 %experts_first.1 = (bf16[3,136,1536]{2,1,0:T(8,128)(2,1)S(1)}, bf16[3,136,1536]{2,1,0:T(8,128)(2,1)S(1)}, f32[1536,768]{1,0:T(8,128)S(1)}, f32[384,1536]{1,0:T(8,128)S(1)}) custom-call(s32[3]{0:T(128)S(1)} %pad_add_fusion.refs_0_, bf16[264,1536]{1,0:T(8,128)(2,1)S(1)} %pack_block.1.refs_1_, bf16[264,1536]{1,0:T(8,128)(2,1)S(1)} %copy-done.15, ...), custom_call_target="tpu_custom_call" | custom-call | flops 7247757312 | bytes 8388608 | tf_op jit(solution)/shard_map/experts_first/pallas_call | solution.py:169
  80.5 5.9 %experts_last.1 = (bf16[1,136,1536]{2,1,0:T(8,128)(2,1)S(1)}, bf16[1,136,1536]{2,1,0:T(8,128)(2,1)S(1)}, bf16[384,1152]{1,0:T(8,128)(2,1)S(1)}, bf16[192,1152]{1...) custom-call(s32[3]{0:T(128)S(1)} %pad_add_fusion.refs_0_, ...), custom_call_target="tpu_custom_call" | custom-call | flops 2415919104 | bytes 8388608 | tf_op jit(solution)/shard_map/experts_last/pallas_call | solution.py:169
  86.4 0.6 collective-permute-start.18
  87.1 1.5 %collective-permute-start.24 = (bf16[192,1152]{1,0:T(8,128)(2,1)S(1)}, bf16[192,1152]{1,0:T(8,128)(2,1)S(1)}, u32[]{:S(2)}, u32[]{:S(2)}) collective-permute-start(bf16[192,1152]{1,0:T(8,128)(2,1)S(1)} %get-tuple-element.31), channel_id=1, source_target_pairs={{0,8},{8,0},{16,24},{24,16},{1,9},{9,1},{17,25},{25,17},{2,10},{10... | collective-permute-start | bytes 1327112 | tf_op jit(solution)/shard_map/ppermute | solution.py:210
  88.6 0.5 collective-permute-start.20
  89.1 0.5 collective-permute-start.22
  89.6 1.6 %collective-permute-start.23 = (bf16[192,1152]{1,0:T(8,128)(2,1)S(1)}, bf16[192,1152]{1,0:T(8,128)(2,1)S(1)}, u32[]{:S(2)}, u32[]{:S(2)}) collective-permute-start(bf16[192,1152]{1,0:T(8,128)(2,1)S(1)} %get-tuple-element.29), channel_id=1, source_target_pairs={{0,16},{8,24},{16,0},{24,8},{1,17},{9,25},{17,1},{25,9},{2,18},{10... | collective-permute-start | bytes 1327112 | tf_op jit(solution)/shard_map/ppermute | solution.py:210
  91.2 8.9 %collective-permute-done.24 = bf16[192,1152]{1,0:T(8,128)(2,1)S(1)} collective-permute-done((bf16[192,1152]{1,0:T(8,128)(2,1)S(1)}, bf16[192,1152]{1,0:T(8,128)(2,1)S(1)}, u32[]{:S(2)}, u32[]{:S(2)}) %collective-permute-start.24) | collective-permute-done | bytes 442400 | tf_op jit(solution)/shard_map/ppermute | solution.py:210
  100.1 4.5 %collective-permute-start.19 = (bf16[136,1536]{1,0:T(8,128)(2,1)S(1)}, bf16[136,1536]{1,0:T(8,128)(2,1)S(1)}, u32[]{:S(2)}, u32[]{:S(2)}) collective-permute-start(bf16[136,1536]{1,0:T(8,128)(2,1)S(1)} %fusion.3), channel_id=1, source_target_pairs={{0,6},{1,7},{2,4},{3,5},{4,2},{5,3},{6,0},{7,1},{8,14},{9,15},{10,... | collective-permute-start | bytes 1253384 | tf_op jit(solution)/shard_map/ppermute | solution.py:214
  104.8 0.3 add_convert_fusion
  105.1 7.2 %collective-permute-start.12 = (bf16[136,1536]{1,0:T(8,128)(2,1)S(1)}, bf16[136,1536]{1,0:T(8,128)(2,1)S(1)}, u32[]{:S(2)}, u32[]{:S(2)}) collective-permute-start(bf16[136,1536]{1,0:T(8,128)(2,1)S(1)} %get-tuple-element.36), channel_id=1, source_target_pairs={{0,2},{1,3},{2,0},{3,1},{4,6},{5,7},{6,4},{7,5},{8,10},{9,11},{10,... | collective-permute-start | bytes 1253384 | tf_op jit(solution)/shard_map/ppermute | solution.py:214
  112.3 0.3 collective-permute-start.13
  112.8 2.1 %collective-permute-done.19 = bf16[136,1536]{1,0:T(8,128)(2,1)S(1)} collective-permute-done((bf16[136,1536]{1,0:T(8,128)(2,1)S(1)}, bf16[136,1536]{1,0:T(8,128)(2,1)S(1)}, u32[]{:S(2)}, u32[]{:S(2)}) %collective-permute-start.19) | collective-permute-done | bytes 417824 | tf_op jit(solution)/shard_map/ppermute | solution.py:214
  114.9 0.5 collective-permute-start.25
  115.4 8.3 %collective-permute-done.12 = bf16[136,1536]{1,0:T(8,128)(2,1)S(1)} collective-permute-done((bf16[136,1536]{1,0:T(8,128)(2,1)S(1)}, bf16[136,1536]{1,0:T(8,128)(2,1)S(1)}, u32[]{:S(2)}, u32[]{:S(2)}) %collective-permute-start.12) | collective-permute-done | bytes 417824 | tf_op jit(solution)/shard_map/ppermute | solution.py:214
  123.7 1.5 %collective-permute-start.21 = (bf16[192,1152]{1,0:T(8,128)(2,1)S(1)}, bf16[192,1152]{1,0:T(8,128)(2,1)S(1)}, u32[]{:S(2)}, u32[]{:S(2)}) collective-permute-start(bf16[192,1152]{1,0:T(8,128)(2,1)S(1)} %add_convert_fusion.2), channel_id=1, source_target_pairs={{0,8},{8,0},{16,24},{24,16},{1,9},{9,1},{17,25},{25,17},{2,10},{10... | collective-permute-start | bytes 1327112 | tf_op jit(solution)/shard_map/ppermute | solution.py:210
  125.1 15.2 %collective-permute-done.13 = bf16[136,1536]{1,0:T(8,128)(2,1)S(1)} collective-permute-done((bf16[136,1536]{1,0:T(8,128)(2,1)S(1)}, bf16[136,1536]{1,0:T(8,128)(2,1)S(1)}, u32[]{:S(2)}, u32[]{:S(2)}) %collective-permute-start.13) | collective-permute-done | bytes 417824 | tf_op jit(solution)/shard_map/ppermute | solution.py:214
  140.3 0.6 select_reduce_fusion
  140.9 1.0 fusion.2
  141.9 1.3 finish.1
  (55 shorter events, 0.8 us)
Async XLA Ops:
  0.6 1.2 copy-start.16
  0.6 4.4 %copy-start.12 = (s32[128,4]{0,1:T(4,128)S(1)}, s32[128,4]{0,1:T(4,128)}, u32[]{:S(2)}) copy-start(s32[128,4]{0,1:T(4,128)} %param.9) | copy-start | bytes 6148
  0.7 4.4 %copy-start.13 = (bf16[128,4]{0,1:T(4,128)(2,1)S(1)}, bf16[128,4]{0,1:T(4,128)(2,1)}, u32[]{:S(2)}) copy-start(bf16[128,4]{0,1:T(4,128)(2,1)} %param.10) | copy-start | bytes 3076
  0.7 4.4 %copy-start.10 = (bf16[128,1536]{1,0:T(8,128)(2,1)S(1)}, bf16[128,1536]{1,0:T(8,128)(2,1)}, u32[]{:S(2)}) copy-start(bf16[128,1536]{1,0:T(8,128)(2,1)} %y_ref.1) | copy-start | bytes 1179652
  0.7 4.4 %copy-start.9 = (bf16[128,1536]{1,0:T(8,128)(2,1)S(1)}, bf16[128,1536]{1,0:T(8,128)(2,1)}, u32[]{:S(2)}) copy-start(bf16[128,1536]{1,0:T(8,128)(2,1)} %x_ref.1) | copy-start | bytes 1179652
  2.0 13.2 %collective-permute-start.8 = (bf16[192,1152]{1,0:T(8,128)(2,1)S(1)}, bf16[192,1152]{1,0:T(8,128)(2,1)S(1)}, u32[]{:S(2)}, u32[]{:S(2)}) collective-permute-start(bf16[192,1152]{1,0:T(8,128)(2,1)S(1)} %pad_maximum_fusion.1.refs_8_.refs_6_), channel_id=1, source_target_pairs={{0,16},{8,24},{16,0},{24,8},{1,17},{9,25},{17,1},{25,9},{2,18},{10... | collective-permute-start | bytes 1327112 | tf_op jit(solution)/shard_map/ppermute | solution.py:210
  5.1 39.1 %collective-permute-start.3 = (bf16[264,1536]{1,0:T(8,128)(2,1)S(1)}, bf16[264,1536]{1,0:T(8,128)(2,1)}, u32[]{:S(2)}, u32[]{:S(2)}) collective-permute-start(bf16[264,1536]{1,0:T(8,128)(2,1)S(1)} %pack_block.1.refs_1_), channel_id=1, source_target_pairs={{0,4},{1,5},{2,6},{3,7},{4,0},{5,1},{6,2},{7,3},{8,12},{9,13},{10,... | collective-permute-start | bytes 2433032 | tf_op jit(solution)/shard_map/ppermute | solution.py:214
  7.8 13.2 %collective-permute-start.5 = (bf16[192,1152]{1,0:T(8,128)(2,1)S(1)}, bf16[192,1152]{1,0:T(8,128)(2,1)}, u32[]{:S(2)}, u32[]{:S(2)}) collective-permute-start(bf16[192,1152]{1,0:T(8,128)(2,1)S(1)} %pad_maximum_fusion.refs_7_.refs_5_), channel_id=1, source_target_pairs={{0,8},{8,0},{16,24},{24,16},{1,9},{9,1},{17,25},{25,17},{2,10},{10... | collective-permute-start | bytes 1327112 | tf_op jit(solution)/shard_map/ppermute | solution.py:210
  9.3 19.3 %collective-permute-start.6 = (bf16[192,1152]{1,0:T(8,128)(2,1)S(1)}, bf16[192,1152]{1,0:T(8,128)(2,1)S(1)}, u32[]{:S(2)}, u32[]{:S(2)}) collective-permute-start(bf16[192,1152]{1,0:T(8,128)(2,1)S(1)} %pad_maximum_fusion.1.refs_8_.refs_6_), channel_id=1, source_target_pairs={{0,8},{8,0},{16,24},{24,16},{1,9},{9,1},{17,25},{25,17},{2,10},{10... | collective-permute-start | bytes 1327112 | tf_op jit(solution)/shard_map/ppermute | solution.py:210
  9.9 36.4 %collective-permute-start.1 = (bf16[264,1536]{1,0:T(8,128)(2,1)S(1)}, bf16[264,1536]{1,0:T(8,128)(2,1)}, u32[]{:S(2)}, u32[]{:S(2)}) collective-permute-start(bf16[264,1536]{1,0:T(8,128)(2,1)S(1)} %pack_block.1.refs_1_), channel_id=1, source_target_pairs={{0,2},{1,3},{2,0},{3,1},{4,6},{5,7},{6,4},{7,5},{8,10},{9,11},{10,... | collective-permute-start | bytes 2433032 | tf_op jit(solution)/shard_map/ppermute | solution.py:214
  15.2 31.6 %collective-permute-start = (bf16[264,1536]{1,0:T(8,128)(2,1)S(1)}, bf16[264,1536]{1,0:T(8,128)(2,1)S(1)}, u32[]{:S(2)}, u32[]{:S(2)}) collective-permute-start(bf16[264,1536]{1,0:T(8,128)(2,1)S(1)} %pack_block.1.refs_1_), channel_id=1, source_target_pairs={{0,1},{1,0},{2,3},{3,2},{4,5},{5,4},{6,7},{7,6},{8,9},{9,8},{10,11... | collective-permute-start | bytes 2433032 | tf_op jit(solution)/shard_map/ppermute | solution.py:217
  21.0 24.5 %collective-permute-start.7 = (bf16[192,1152]{1,0:T(8,128)(2,1)S(1)}, bf16[192,1152]{1,0:T(8,128)(2,1)S(1)}, u32[]{:S(2)}, u32[]{:S(2)}) collective-permute-start(bf16[192,1152]{1,0:T(8,128)(2,1)S(1)} %pad_maximum_fusion.refs_7_.refs_5_), channel_id=1, source_target_pairs={{0,16},{8,24},{16,0},{24,8},{1,17},{9,25},{17,1},{25,9},{2,18},{10... | collective-permute-start | bytes 1327112 | tf_op jit(solution)/shard_map/ppermute | solution.py:210
  28.7 0.8 copy-start.3
  29.4 20.5 %collective-permute-start.16 = (bf16[264,1536]{1,0:T(8,128)(2,1)S(1)}, bf16[264,1536]{1,0:T(8,128)(2,1)S(1)}, u32[]{:S(2)}, u32[]{:S(2)}) collective-permute-start(bf16[264,1536]{1,0:T(8,128)(2,1)S(1)} %pack_block.1.refs_1_), channel_id=1, source_target_pairs={{2,4},{3,5},{4,2},{5,3},{10,12},{11,13},{12,10},{13,11},{18,20},{1... | collective-permute-start | bytes 2433032 | tf_op jit(solution)/shard_map/ppermute | solution.py:214
  44.2 20.0 %collective-permute-start.14 = (bf16[264,1536]{1,0:T(8,128)(2,1)}, bf16[264,1536]{1,0:T(8,128)(2,1)S(1)}, u32[]{:S(2)}, u32[]{:S(2)}) collective-permute-start(bf16[264,1536]{1,0:T(8,128)(2,1)} %collective-permute-done.3.refs_5_), channel_id=1, source_target_pairs={{4,6},{5,7},{2,0},{3,1},{12,14},{13,15},{10,8},{11,9},{20,22},{21,... | collective-permute-start | bytes 2433032 | tf_op jit(solution)/shard_map/ppermute | solution.py:214
  45.5 0.8 copy-start.5
  46.3 18.0 %collective-permute-start.4 = (bf16[264,1536]{1,0:T(8,128)(2,1)}, bf16[264,1536]{1,0:T(8,128)(2,1)}, u32[]{:S(2)}, u32[]{:S(2)}) collective-permute-start(bf16[264,1536]{1,0:T(8,128)(2,1)} %collective-permute-done.3.refs_5_), channel_id=1, source_target_pairs={{0,1},{1,0},{2,3},{3,2},{4,5},{5,4},{6,7},{7,6},{8,9},{9,8},{10,11... | collective-permute-start | bytes 2433032 | tf_op jit(solution)/shard_map/ppermute | solution.py:217
  46.3 18.0 %collective-permute-start.2 = (bf16[264,1536]{1,0:T(8,128)(2,1)}, bf16[264,1536]{1,0:T(8,128)(2,1)}, u32[]{:S(2)}, u32[]{:S(2)}) collective-permute-start(bf16[264,1536]{1,0:T(8,128)(2,1)} %collective-permute-done.1.refs_3_), channel_id=1, source_target_pairs={{0,1},{1,0},{2,3},{3,2},{4,5},{5,4},{6,7},{7,6},{8,9},{9,8},{10,11... | collective-permute-start | bytes 2433032 | tf_op jit(solution)/shard_map/ppermute | solution.py:217
  46.8 0.9 copy-start.14
  47.7 12.1 %collective-permute-start.10 = (bf16[192,1152]{1,0:T(8,128)(2,1)S(1)}, bf16[192,1152]{1,0:T(8,128)(2,1)S(1)}, u32[]{:S(2)}, u32[]{:S(2)}) collective-permute-start(bf16[192,1152]{1,0:T(8,128)(2,1)S(1)} %collective-permute-done.8.refs_12_.refs_10_), channel_id=1, source_target_pairs={{0,8},{8,0},{16,24},{24,16},{1,9},{9,1},{17,25},{25,17},{2,10},{10... | collective-permute-start | bytes 1327112 | tf_op jit(solution)/shard_map/ppermute | solution.py:210
  49.2 0.8 copy-start.1
  50.0 14.3 %collective-permute-start.9 = (bf16[192,1152]{1,0:T(8,128)(2,1)}, bf16[192,1152]{1,0:T(8,128)(2,1)}, u32[]{:S(2)}, u32[]{:S(2)}) collective-permute-start(bf16[192,1152]{1,0:T(8,128)(2,1)} %collective-permute-done.5.refs_9_.refs_7_), channel_id=1, source_target_pairs={{0,16},{8,24},{16,0},{24,8},{1,17},{9,25},{17,1},{25,9},{2,18},{10... | collective-permute-start | bytes 1327112 | tf_op jit(solution)/shard_map/ppermute | solution.py:210
  59.8 0.8 copy-start.7
  60.6 19.9 %collective-permute-start.17 = (bf16[264,1536]{1,0:T(8,128)(2,1)S(1)}, bf16[264,1536]{1,0:T(8,128)(2,1)}, u32[]{:S(2)}, u32[]{:S(2)}) collective-permute-start(bf16[264,1536]{1,0:T(8,128)(2,1)S(1)} %collective-permute-done.16.refs_3_), channel_id=1, source_target_pairs={{0,1},{1,0},{2,3},{3,2},{4,5},{5,4},{6,7},{7,6},{8,9},{9,8},{10,11... | collective-permute-start | bytes 2433032 | tf_op jit(solution)/shard_map/ppermute | solution.py:217
  64.2 16.3 %collective-permute-start.15 = (bf16[264,1536]{1,0:T(8,128)(2,1)S(1)}, bf16[264,1536]{1,0:T(8,128)(2,1)}, u32[]{:S(2)}, u32[]{:S(2)}) collective-permute-start(bf16[264,1536]{1,0:T(8,128)(2,1)S(1)} %collective-permute-done.14.refs_1_), channel_id=1, source_target_pairs={{0,1},{1,0},{2,3},{3,2},{4,5},{5,4},{6,7},{7,6},{8,9},{9,8},{10,11... | collective-permute-start | bytes 2433032 | tf_op jit(solution)/shard_map/ppermute | solution.py:217
  64.3 1.0 copy-start.2
  65.3 1.0 copy-start.4
  66.3 1.0 copy-start.6
  67.3 1.0 copy-start.8
  68.3 1.1 copy-start.15
  86.4 3.1 %collective-permute-start.18 = (bf16[1,136,1536]{2,1,0:T(8,128)(2,1)S(1)}, bf16[1,136,1536]{2,1,0:T(8,128)(2,1)S(1)}, u32[]{:S(2)}, u32[]{:S(2)}) collective-permute-start(bf16[1,136,1536]{2,1,0:T(8,128)(2,1)S(1)} %get-tuple-element.24), channel_id=1, source_target_pairs={{0,1},{1,0},{2,3},{3,2},{4,5},{5,4},{6,7},{7,6},{8,9},{9,8},{10,11... | collective-permute-start | bytes 1253384 | tf_op jit(solution)/shard_map/ppermute | solution.py:217
  87.0 17.7 %collective-permute-start.11 = (bf16[3,136,1536]{2,1,0:T(8,128)(2,1)S(1)}, bf16[3,136,1536]{2,1,0:T(8,128)(2,1)S(1)}, u32[]{:S(2)}, u32[]{:S(2)}) collective-permute-start(bf16[3,136,1536]{2,1,0:T(8,128)(2,1)S(1)} %get-tuple-element.20), channel_id=1, source_target_pairs={{0,1},{1,0},{2,3},{3,2},{4,5},{5,4},{6,7},{7,6},{8,9},{9,8},{10,11... | collective-permute-start | bytes 3760136 | tf_op jit(solution)/shard_map/ppermute | solution.py:217
  87.1 13.0 %collective-permute-start.24 = (bf16[192,1152]{1,0:T(8,128)(2,1)S(1)}, bf16[192,1152]{1,0:T(8,128)(2,1)S(1)}, u32[]{:S(2)}, u32[]{:S(2)}) collective-permute-start(bf16[192,1152]{1,0:T(8,128)(2,1)S(1)} %get-tuple-element.31), channel_id=1, source_target_pairs={{0,8},{8,0},{16,24},{24,16},{1,9},{9,1},{17,25},{25,17},{2,10},{10... | collective-permute-start | bytes 1327112 | tf_op jit(solution)/shard_map/ppermute | solution.py:210
  88.6 23.7 %collective-permute-start.20 = (bf16[192,1152]{1,0:T(8,128)(2,1)S(1)}, bf16[192,1152]{1,0:T(8,128)(2,1)S(1)}, u32[]{:S(2)}, u32[]{:S(2)}) collective-permute-start(bf16[192,1152]{1,0:T(8,128)(2,1)S(1)} %get-tuple-element.27), channel_id=1, source_target_pairs={{0,16},{8,24},{16,0},{24,8},{1,17},{9,25},{17,1},{25,9},{2,18},{10... | collective-permute-start | bytes 1327112 | tf_op jit(solution)/shard_map/ppermute | solution.py:210
  89.1 52.8 %collective-permute-start.22 = (bf16[192,1152]{1,0:T(8,128)(2,1)S(1)}, bf16[192,1152]{1,0:T(8,128)(2,1)S(1)}, u32[]{:S(2)}, u32[]{:S(2)}) collective-permute-start(bf16[192,1152]{1,0:T(8,128)(2,1)S(1)} %get-tuple-element.28), channel_id=1, source_target_pairs={{0,8},{8,0},{16,24},{24,16},{1,9},{9,1},{17,25},{25,17},{2,10},{10... | collective-permute-start | bytes 1327112 | tf_op jit(solution)/shard_map/ppermute | solution.py:210
  89.6 52.3 %collective-permute-start.23 = (bf16[192,1152]{1,0:T(8,128)(2,1)S(1)}, bf16[192,1152]{1,0:T(8,128)(2,1)S(1)}, u32[]{:S(2)}, u32[]{:S(2)}) collective-permute-start(bf16[192,1152]{1,0:T(8,128)(2,1)S(1)} %get-tuple-element.29), channel_id=1, source_target_pairs={{0,16},{8,24},{16,0},{24,8},{1,17},{9,25},{17,1},{25,9},{2,18},{10... | collective-permute-start | bytes 1327112 | tf_op jit(solution)/shard_map/ppermute | solution.py:210
  100.1 14.7 %collective-permute-start.19 = (bf16[136,1536]{1,0:T(8,128)(2,1)S(1)}, bf16[136,1536]{1,0:T(8,128)(2,1)S(1)}, u32[]{:S(2)}, u32[]{:S(2)}) collective-permute-start(bf16[136,1536]{1,0:T(8,128)(2,1)S(1)} %fusion.3), channel_id=1, source_target_pairs={{0,6},{1,7},{2,4},{3,5},{4,2},{5,3},{6,0},{7,1},{8,14},{9,15},{10,... | collective-permute-start | bytes 1253384 | tf_op jit(solution)/shard_map/ppermute | solution.py:214
  105.1 18.5 %collective-permute-start.12 = (bf16[136,1536]{1,0:T(8,128)(2,1)S(1)}, bf16[136,1536]{1,0:T(8,128)(2,1)S(1)}, u32[]{:S(2)}, u32[]{:S(2)}) collective-permute-start(bf16[136,1536]{1,0:T(8,128)(2,1)S(1)} %get-tuple-element.36), channel_id=1, source_target_pairs={{0,2},{1,3},{2,0},{3,1},{4,6},{5,7},{6,4},{7,5},{8,10},{9,11},{10,... | collective-permute-start | bytes 1253384 | tf_op jit(solution)/shard_map/ppermute | solution.py:214
  112.3 28.0 %collective-permute-start.13 = (bf16[136,1536]{1,0:T(8,128)(2,1)S(1)}, bf16[136,1536]{1,0:T(8,128)(2,1)S(1)}, u32[]{:S(2)}, u32[]{:S(2)}) collective-permute-start(bf16[136,1536]{1,0:T(8,128)(2,1)S(1)} %get-tuple-element.35), channel_id=1, source_target_pairs={{0,4},{1,5},{2,6},{3,7},{4,0},{5,1},{6,2},{7,3},{8,12},{9,13},{10,... | collective-permute-start | bytes 1253384 | tf_op jit(solution)/shard_map/ppermute | solution.py:214
  112.8 29.1 %copy-start = (bf16[1,384,768]{2,1,0:T(8,128)(2,1)S(1)}, bf16[1,384,768]{2,1,0:T(8,128)(2,1)}, u32[]{:S(2)}) copy-start(bf16[1,384,768]{2,1,0:T(8,128)(2,1)} %min_ref.1) | copy-start | bytes 1769476
  112.8 29.1 %copy-start.11 = (bf16[1,384,384]{2,1,0:T(8,128)(2,1)S(1)}, bf16[1,384,384]{2,1,0:T(8,128)(2,1)}, u32[]{:S(2)}) copy-start(bf16[1,384,384]{2,1,0:T(8,128)(2,1)} %mout_ref.1) | copy-start | bytes 884740
  114.9 27.0 %collective-permute-start.25 = (bf16[192,1152]{1,0:T(8,128)(2,1)S(1)}, bf16[192,1152]{1,0:T(8,128)(2,1)S(1)}, u32[]{:S(2)}, u32[]{:S(2)}) collective-permute-start(bf16[192,1152]{1,0:T(8,128)(2,1)S(1)} %add_convert_fusion.1), channel_id=1, source_target_pairs={{0,16},{8,24},{16,0},{24,8},{1,17},{9,25},{17,1},{25,9},{2,18},{10... | collective-permute-start | bytes 1327112 | tf_op jit(solution)/shard_map/ppermute | solution.py:210
  123.7 18.2 %collective-permute-start.21 = (bf16[192,1152]{1,0:T(8,128)(2,1)S(1)}, bf16[192,1152]{1,0:T(8,128)(2,1)S(1)}, u32[]{:S(2)}, u32[]{:S(2)}) collective-permute-start(bf16[192,1152]{1,0:T(8,128)(2,1)S(1)} %add_convert_fusion.2), channel_id=1, source_target_pairs={{0,8},{8,0},{16,24},{24,16},{1,9},{9,1},{17,25},{25,17},{2,10},{10... | collective-permute-start | bytes 1327112 | tf_op jit(solution)/shard_map/ppermute | solution.py:210

commit v3 on v0

--- a/solution.py
+++ b/solution.py
@@ -1,9 +1,383 @@
+import functools
+
 import jax
 import jax.numpy as jnp
 from jax import lax
+from jax.experimental import pallas as pl
+from jax.experimental.pallas import tpu as pltpu
 from jax.sharding import PartitionSpec as P
 
+
 momentum_decay = 0.9
+bf16 = jnp.bfloat16
+f32 = jnp.float32
+MIB = 1024 * 1024
+
+
+def dot(a, b, left, right):
+    return lax.dot_general(a, b, (((left,), (right,)), ((), ())), preferred_element_type=f32)
+
+
+def call(kernel, operands, outs, scratch=(), mib=8, scalars=0, flops=0, far=0):
+    specs = [pl.BlockSpec(memory_space=pltpu.SMEM)] * scalars
+    specs += [pl.BlockSpec(memory_space=pltpu.VMEM)] * (len(operands) - scalars - far)
+    specs += [pl.BlockSpec(memory_space=pltpu.HBM)] * far
+    return pl.pallas_call(
+        kernel,
+        out_shape=[jax.ShapeDtypeStruct(shape, dtype) for shape, dtype in outs],
+        in_specs=specs,
+        out_specs=[pl.BlockSpec(memory_space=pltpu.VMEM)] * len(outs),
+        scratch_shapes=[pltpu.VMEM(*item) if isinstance(item, tuple) else item for item in scratch],
+        compiler_params=pltpu.CompilerParams(vmem_limit_bytes=mib * MIB),
+        cost_estimate=pl.CostEstimate(flops=flops, bytes_accessed=4 * MIB, transcendentals=0),
+    )(*operands)
+
+
+def stage_kernel(routes_hbm, gates_hbm, x_hbm, y_hbm, win_hbm, wout_hbm, *refs):
+    x_ref, block_ref, win_ref, wout_ref, routes_ref, gates_ref, sems = refs
+    tok = x_ref.shape[0]
+    experts = block_ref.shape[0] - tok
+    moves = (
+        (routes_hbm, routes_ref),
+        (gates_hbm, gates_ref),
+        (y_hbm, block_ref.at[0:tok]),
+        (x_hbm, x_ref),
+        (win_hbm, win_ref),
+        (wout_hbm, wout_ref),
+    )
+    copies = [pltpu.make_async_copy(src, dst, sems.at[i]) for i, (src, dst) in enumerate(moves)]
+    for copy in copies:
+        copy.start()
+    copies[0].wait()
+    copies[1].wait()
+    ids = lax.broadcasted_iota(jnp.int32, (experts, tok), 0)
+    dense = jnp.zeros((experts, tok), f32)
+    for k in range(routes_ref.shape[0]):
+        gate = gates_ref[k : k + 1, :].astype(f32)
+        dense = dense + jnp.where(ids == routes_ref[k : k + 1, :], gate, 0.0)
+    tail = jnp.zeros((experts, block_ref.shape[1] - tok), f32)
+    block_ref[tok:, :] = jnp.concatenate([dense, tail], axis=1).astype(bf16)
+    for copy in copies[2:]:
+        copy.wait()
+
+
+def is_end(expert, chips):
+    chip = lax.shift_right_logical(expert, 1)
+    return (chip == 0) | (chip == chips - 1)
+
+
+def gate_column(table, expert):
+    pick = lax.broadcasted_iota(jnp.int32, table.shape, 0) == expert
+    return jnp.sum(jnp.where(pick, table.astype(f32), 0.0).T, axis=1, keepdims=True)
+
+
+def gate_table(column, experts, expert):
+    spread = jnp.broadcast_to(column, (column.shape[0], experts)).T
+    pick = lax.broadcasted_iota(jnp.int32, spread.shape, 0) == expert
+    return jnp.where(pick, spread, 0.0)
+
+
+def write_rows(out, row_grad, table):
+    tok = row_grad.shape[0]
+    out[0:tok, :] = row_grad
+    tail = jnp.zeros((table.shape[0], out.shape[1] - tok), f32)
+    out[tok:, :] = jnp.concatenate([table, tail], axis=1).astype(bf16)
+
+
+def activations(both):
+    ffn = both.shape[1] // 2
+    g, u = both[:, :ffn], both[:, ffn:]
+    s = 1.0 / (1.0 + jnp.exp(-g))
+    silu = g * s
+    hidden = (silu * u).astype(bf16)
+    return silu, u * s * (1.0 + g * (1.0 - s)), hidden
+
+
+def block_step(tables, expert, x, y, win, wout, keep_ref, give_ref, dgu_ref, ch_ref):
+    tok, ffn = x.shape[0] // 2, wout.shape[0]
+    experts = tables[0].shape[0]
+    gate = jnp.concatenate([gate_column(table, expert) for table in tables], axis=0)
+    silu, slope, hidden = activations(dot(x, win[...], 1, 0))
+    back = dot(y, wout[...], 1, 1)
+    gate_grad = jnp.sum(hidden.astype(f32) * back, axis=1, keepdims=True)
+    ch_ref[...] = (hidden.astype(f32) * gate).astype(bf16)
+    dh = back * gate
+    dgu_ref[:, :ffn] = (dh * slope).astype(bf16)
+    dgu_ref[:, ffn:] = (dh * silu).astype(bf16)
+    row_grad = dot(dgu_ref[...], win[...], 1, 1).astype(bf16)
+    for i, out in enumerate((keep_ref, give_ref)):
+        part = slice(i * tok, (i + 1) * tok)
+        write_rows(out, row_grad[part], gate_table(gate_grad[part], experts, expert))
+
+
+def own_kernel(ids_ref, x0, x1, y0, y1, *refs):
+    in_pieces, out_pieces = refs[0:4], refs[4:8]
+    keep_ref, give_ref, dgu_ref, ch_ref, win, wout = refs[8:]
+    rep, expert = ids_ref[0], ids_ref[1]
+    shard = wout.shape[1] // 4
+    for j in range(4):
+        at = pl.multiple_of((rep ^ j) * shard, 128)
+        win[pl.ds(at, shard), :] = in_pieces[j][0]
+        wout[:, pl.ds(at, shard)] = out_pieces[j][0]
+    tok = x0.shape[0]
+    tables = [ref[tok:, 0:tok] for ref in (y0, y1)]
+    x, y = (jnp.concatenate([ref[0:tok, :] for ref in pair], axis=0) for pair in ((x0, x1), (y0, y1)))
+    block_step(tables, expert, x, y, win, wout, keep_ref, give_ref, dgu_ref, ch_ref)
+
+
+def rest_kernel(ids_ref, *refs):
+    blocks, (own_dgu, own_ch, win, wout), refs = (refs[0:4], refs[4:8], refs[8:12]), refs[12:16], refs[16:]
+    keep_ref, give_ref, acc_in_ref, acc_out_ref, xs, ys, dgus, chs = refs
+    tok = blocks[0][0].shape[0]
+    rows = 2 * tok
+    dgus[0:rows, :] = own_dgu[...]
+    chs[0:rows, :] = own_ch[...]
+    for n, (x0, x1, y0, y1) in enumerate(blocks):
+        at = n * rows
+        for i, (xr, yr) in enumerate(((x0, y0), (x1, y1))):
+            xs[at + i * tok : at + (i + 1) * tok, :] = xr[...]
+            ys[at + i * tok : at + (i + 1) * tok, :] = yr[0:tok, :]
+    for n in (1, 2):
+        part = slice(n * rows, (n + 1) * rows)
+        outs = (keep_ref.at[n - 1], give_ref.at[n - 1], dgus.at[part], chs.at[part])
+        x, y = xs[part, :], ys[part, :]
+        tables = [ref[tok:, 0:tok] for ref in blocks[n][2:]]
+        block_step(tables, ids_ref[1], x, y, win, wout, *outs)
+    acc_in_ref[...] = dot(xs[...], dgus[...], 0, 0)
+    acc_out_ref[...] = dot(chs[...], ys[...], 0, 0)
+
+
+def forward_kernel(chips, ids_ref, e0, e1, m0, m1, win, xs, silu_ref, slope_ref, hidden_ref):
+    tok = e0.shape[0]
+    at_end = is_end(ids_ref[1], chips)
+
+    @pl.when(at_end)
+    def _():
+        xs[0:tok, :] = e0[...]
+        xs[tok:, :] = e1[...]
+
+    @pl.when(jnp.logical_not(at_end))
+    def _():
+        xs[0:tok, :] = m0[...]
+        xs[tok:, :] = m1[...]
+
+    silu_ref[...], slope_ref[...], hidden_ref[...] = activations(dot(xs[...], win[...], 1, 0))
+
+
+def shard_grads(refs, acc_in_ref, acc_out_ref, xs, ys, dgus, chs, index, half):
+    shard = 2 * half
+    at = pl.multiple_of(index * shard, 128)
+    part_in = acc_in_ref[pl.ds(at, shard), :] + dot(xs[:, pl.ds(at, shard)], dgus[...], 0, 0)
+    part_out = acc_out_ref[:, pl.ds(at, shard)] + dot(chs[...], ys[:, pl.ds(at, shard)], 0, 0)
+    cols = part_in.shape[1]
+    for n, ref in enumerate(refs):
+        rows = slice(n * ref.shape[0], (n + 1) * ref.shape[0])
+        ref[:, 0:cols] = part_in[rows].astype(bf16)
+        ref[:, cols:] = part_out[rows].astype(bf16)
+
+
+def grad_kernel(chips, ids_ref, e0, e1, m0, m1, xs, silu, slope, hidden, wout, acc_in, acc_out, *refs):
+    r3a_ref, r3b_ref, dgus, chs, ys, tab_ref = refs
+    tok = ys.shape[0] // 2
+    rep, expert = ids_ref[0], ids_ref[1]
+    at_end = is_end(ids_ref[1], chips)
+    ffn, experts = wout.shape[0], tab_ref.shape[1]
+
+    @pl.when(at_end)
+    def _():
+        ys[0:tok, :] = e0[0:tok, :]
+        ys[tok:, :] = e1[0:tok, :]
+
+    @pl.when(jnp.logical_not(at_end))
+    def _():
+        ys[0:tok, :] = m0[0:tok, :]
+        ys[tok:, :] = m1[0:tok, :]
+
+    columns = []
+    for end, mid in ((e0, m0), (e1, m1)):
+        table = jnp.where(at_end, end[tok:, 0:tok].astype(f32), mid[tok:, 0:tok].astype(f32))
+        columns.append(gate_column(table, expert))
+    gate = jnp.concatenate(columns, axis=0)
+    back = dot(ys[...], wout[...], 1, 1)
+    gate_grad = jnp.sum(hidden[...].astype(f32) * back, axis=1, keepdims=True)
+    chs[...] = (hidden[...].astype(f32) * gate).astype(bf16)
+    dh = back * gate
+    dgus[:, :ffn] = (dh * slope[...]).astype(bf16)
+    dgus[:, ffn:] = (dh * silu[...]).astype(bf16)
+    for i in range(2):
+        tab_ref[i] = gate_table(gate_grad[i * tok : (i + 1) * tok], experts, expert)
+    half = r3a_ref.shape[0]
+    shard_grads((r3a_ref, r3b_ref), acc_in, acc_out, xs, ys, dgus, chs, rep ^ 3, half)
+
+
+def other_grads_kernel(ids_ref, xs, ys, dgus, chs, acc_in, acc_out, mine_ref, r1a_ref, r1b_ref, r2a_ref, r2b_ref):
+    rep, half = ids_ref[0], r1a_ref.shape[0]
+    args = (acc_in, acc_out, xs, ys, dgus, chs)
+    shard_grads((r1a_ref, r1b_ref), *args, rep ^ 1, half)
+    shard_grads((r2a_ref, r2b_ref), *args, rep ^ 2, half)
+    shard_grads((mine_ref,), *args, rep, half)
+
+
+def rows_kernel(dgus, win, tab_ref, keep_ref, give_ref):
+    tok = dgus.shape[0] // 2
+    row_grad = dot(dgus[...], win[...], 1, 1).astype(bf16)
+    for i, out in enumerate((keep_ref, give_ref)):
+        write_rows(out, row_grad[i * tok : (i + 1) * tok], tab_ref[i])
+
+
+def finish_kernel(own_ref, t1a_ref, t1b_ref, t2a_ref, t2b_ref, min_ref, mout_ref, nin_ref, nout_ref):
+    half = t1a_ref.shape[0]
+    cols = min_ref.shape[2]
+    for lo, one, two in ((0, t1a_ref, t2a_ref), (half, t1b_ref, t2b_ref)):
+        rows = slice(lo, lo + half)
+        total = own_ref[rows, :].astype(f32) + one[...].astype(f32) + two[...].astype(f32)
+        old_in = momentum_decay * min_ref[0, rows, :].astype(f32)
+        old_out = momentum_decay * mout_ref[0, rows, :].astype(f32)
+        nin_ref[0, rows, :] = (old_in + total[:, :cols]).astype(bf16)
+        nout_ref[0, rows, :] = (old_out + total[:, cols:]).astype(bf16)
+
+
+def per_device_dense(*args):
+    return dense_step(*args)
+
+
+def dense_step(tokens, routes, gates, output_grad, w_in, w_out, momentum_in, momentum_out):
+    tok, width = tokens.shape
+    ffn, both_w = w_out.shape[1], w_in.shape[2]
+    shard = w_in.shape[1]
+    half = shard // 2
+    cols = both_w + shard
+    experts = lax.axis_size("expert")
+    chips = experts // 2
+    rep = lax.axis_index("rep")
+    expert = lax.axis_index("expert")
+    ids = jnp.stack([rep, expert]).astype(jnp.int32)
+
+    def over_rep(value, bits):
+        return lax.ppermute(value, "rep", [(i, i ^ bits) for i in range(4)])
+
+    def over_chips(value, chip_pairs):
+        pairs = [(2 * a + c, 2 * b + c) for a, b in chip_pairs for c in range(2)]
+        return lax.ppermute(value, "expert", pairs)
+
+    def partner(value):
+        return lax.ppermute(value, "expert", [(i, i ^ 1) for i in range(experts)])
+
+    to_far = [(z, z ^ 2) for z in range(chips)]
+    to_near = [(z, z ^ 1) for z in range(chips)]
+    to_cross = [(z, z ^ 3) for z in range(chips)]
+    to_middle = [(1, 2), (2, 1)]
+    to_ends = [(2, 3), (1, 0)]
+
+    far_x = over_chips(tokens, to_far)
+    w1in = over_rep(w_in, 1)
+    w2in = over_rep(w_in, 2)
+    near_x = over_chips(tokens, to_near)
+    top = routes.shape[1]
+    sources = [routes.T, gates.T, tokens, output_grad, w_in, w_out]
+    own_x, own_y, own_in, own_out = call(
+        stage_kernel,
+        sources,
+        [((tok, width), bf16), ((tok + experts, width), bf16), (w_in.shape, bf16), (w_out.shape, bf16)],
+        [((top, tok), jnp.int32), ((top, tok), bf16), pltpu.SemaphoreType.DMA((len(sources),))],
+        mib=2,
+        far=len(sources),
+    )
+    far_y = over_chips(own_y, to_far)
+    near_y = over_chips(own_y, to_near)
+    w1out = over_rep(w_out, 1)
+    w2out = over_rep(w_out, 2)
+    middle_x = over_chips(tokens, to_middle)
+    own_xp = partner(own_x)
+    own_yp = partner(own_y)
+    w3in = over_rep(w1in, 2)
+    ends_x = over_chips(far_x, to_ends)
+    w3out = over_rep(w2out, 1)
+    far_xp = partner(far_x)
+    near_xp = partner(near_x)
+    middle_y = over_chips(own_y, to_middle)
+    ends_y = over_chips(far_y, to_ends)
+    far_yp = partner(far_y)
+    near_yp = partner(near_y)
+    rows = 2 * tok
+    block = ((tok + experts, width), bf16)
+    flops = 5 * rows * width * both_w
+    own_blocks = [own_x, own_xp, own_y, own_yp]
+    keep, give_own, own_dgu, own_ch, win, wout = call(
+        own_kernel,
+        [ids, *own_blocks, own_in, w1in, w2in, w3in, own_out, w1out, w2out, w3out],
+        [block, block, ((rows, both_w), bf16), ((rows, ffn), bf16)]
+        + [((width, both_w), bf16), ((ffn, width), bf16)],
+        mib=10,
+        scalars=1,
+        flops=flops,
+    )
+    got = partner(give_own)
+    home_own = (keep.astype(f32) + got.astype(f32)).astype(bf16)
+    keep, give, acc_in, acc_out = call(
+        rest_kernel,
+        [ids, *own_blocks, near_x, near_xp, near_y, near_yp, far_x, far_xp, far_y, far_yp]
+        + [own_dgu, own_ch, win, wout],
+        [((2, tok + experts, width), bf16)] * 2 + [((width, both_w), f32), ((ffn, width), f32)],
+        [((3 * rows, n), bf16) for n in (width, width, both_w, ffn)],
+        mib=18,
+        scalars=1,
+        flops=3 * flops,
+    )
+    middle_xp = partner(middle_x)
+    ends_xp = partner(ends_x)
+    got = partner(give)
+    home_near, home_far = ((keep[i].astype(f32) + got[i].astype(f32)).astype(bf16) for i in range(2))
+    xs, silu, slope, hidden = call(
+        functools.partial(forward_kernel, chips),
+        [ids, ends_x, ends_xp, middle_x, middle_xp, win],
+        [((rows, width), bf16), ((rows, ffn), f32), ((rows, ffn), f32), ((rows, ffn), bf16)],
+        scalars=1,
+        flops=2 * rows * width * both_w,
+    )
+    middle_yp = partner(middle_y)
+    ends_yp = partner(ends_y)
+    home_near = over_chips(home_near, to_near)
+    home_far = over_chips(home_far, to_far)
+    r3a, r3b, dgus, chs, ys, table = call(
+        functools.partial(grad_kernel, chips),
+        [ids, ends_y, ends_yp, middle_y, middle_yp, xs, silu, slope, hidden, wout]
+        + [acc_in, acc_out],
+        [((half, cols), bf16)] * 2
+        + [((rows, both_w), bf16), ((rows, ffn), bf16), ((rows, width), bf16), ((2, experts, tok), f32)],
+        mib=8,
+        scalars=1,
+        flops=rows * width * both_w * 2,
+    )
+    s3a = over_rep(r3a, 2)
+    s3b = over_rep(r3b, 1)
+    mine, r1a, r1b, r2a, r2b = call(
+        other_grads_kernel,
+        [ids, xs, ys, dgus, chs, acc_in, acc_out],
+        [((shard, cols), bf16)] + [((half, cols), bf16)] * 4,
+        mib=8,
+        scalars=1,
+        flops=2 * rows * width * both_w,
+    )
+    keep2, give2 = call(rows_kernel, [dgus, win, table], [block, block])
+    got2 = partner(give2)
+    t2a = over_rep(r2a, 2)
+    t1b = over_rep(r1b, 1)
+    last = (keep2.astype(f32) + got2.astype(f32)).astype(bf16)
+    home_cross = over_chips(last, to_cross)
+    t1a = over_rep((r1a.astype(f32) + s3a.astype(f32)).astype(bf16), 1)
+    t2b = over_rep((r2b.astype(f32) + s3b.astype(f32)).astype(bf16), 2)
+    parts = (home_own, home_near, home_far, home_cross)
+    token_grad = sum(p[:tok].astype(f32) for p in parts).astype(bf16)
+    table = sum(p[tok:, :tok].astype(f32) for p in parts)
+    picked = routes.T[:, None, :] == jnp.arange(experts, dtype=jnp.int32)[None, :, None]
+    gate_grad = jnp.sum(jnp.where(picked, table[None], 0.0), axis=1).astype(bf16).T
+    new_in, new_out = call(
+        finish_kernel,
+        [mine, t1a, t1b, t2a, t2b, momentum_in, momentum_out],
+        [(momentum_in.shape, bf16), (momentum_out.shape, bf16)],
+    )
+    return token_grad, gate_grad, new_in, new_out
 
 
 def slot_positions(routes, experts):
@@ -26,7 +400,7 @@
     return (gate_pre, up_part, silu_gate, hidden, expert_out)
 
 
-def per_device(tokens, routes, gates, output_grad, w_in, w_out, momentum_in, momentum_out):
+def per_device_sparse(tokens, routes, gates, output_grad, w_in, w_out, momentum_in, momentum_out):
     tok_dev, width = tokens.shape
     top_count = routes.shape[1]
     senders = lax.axis_size("expert")
@@ -145,6 +519,17 @@
         P("expert", "rep", None),
         P("expert", None, "rep"),
     )
+
+    small = mesh.shape["expert"] == 8 and mesh.shape["rep"] == 4
+
+    def per_device(*args):
+        tok, width = args[0].shape
+        w_in, w_out = args[4], args[5]
+        lanes = (tok, w_in.shape[1], w_out.shape[1], w_out.shape[2], w_in.shape[2])
+        fits = small and tok == 128 and width >= tok and all(n % 128 == 0 for n in lanes)
+        dense = fits and w_in.shape[0] == 1 and w_in.shape[1] == w_out.shape[2] == w_out.shape[1]
+        return (per_device_dense if dense else per_device_sparse)(*args)
+
     return jax.shard_map(
         per_device, mesh=mesh, in_specs=in_specs, out_specs=out_specs, check_vma=False
     )

time: 235 us -> 169 us (0.72)
  waiting for transfers between devices: 124 us -> 88 us
  matrix products: 24.1 us -> 0 us
  Pallas kernels: 0 us -> 19.5 us
  local copies, waits for them, and re-layouts: 37.1 us -> 23.1 us
  between operations: 14 us -> 0.98 us
  starting transfers between devices: 24 us -> 34.7 us
  other arithmetic: 11 us -> 2.24 us
    all_to_all x5 -> x0, waiting for transfers between devices: 122 us -> none  [the longest x1 41.8 us: per_device(): lax.all_to_all(sent_tokens, 'expert', split_axis=0, concat_axis=0, tiled=...]
    ppermute x0 -> x36, waiting for transfers between devices: none -> 88 us  [the longest x11 53.1 us: over_chips(): return lax.ppermute(value, 'expert', pairs)]
    ppermute x0 -> x36, starting transfers between devices: none -> 34.7 us  [the longest x11 18.4 us: over_chips(): return lax.ppermute(value, 'expert', pairs)]
    dot_general x6 -> x0, matrix products: 24.1 us -> none  [the longest x1 5.68 us: forward_pass(): both = jnp.dot(x_rows, weight_in, preferred_element_type=jnp.float32)]
    all_to_all x5 -> x0, starting transfers between devices: 23.7 us -> none  [the longest x1 6.35 us: per_device(): lax.all_to_all(sent_gate, 'expert', split_axis=0, concat_axis=0, tiled=True)]
    pallas_call x0 -> x8, Pallas kernels: none -> 19.5 us  [call(): pl.pallas_call(kernel, out_shape=[jax.ShapeDtypeStruct(shape, dtype) for...]
    gather x4 -> x0, local copies, waits for them, and re-layouts: 13.1 us -> none  [the longest x1 3.75 us: per_device(): jnp.concatenate([tokens, zero_row], axis=0)[source_row]]
    unnamed x23 -> x64, local copies, waits for them, and re-layouts: 13.8 us -> 23.1 us
  transfers between devices with their start and end apart: 9 -> 36, of which waited for: 5 -> 12; matrix products, arithmetic and copies ran while one was open for 20% -> 0% of each run, Pallas kernels for 0% -> 10%
where the time goes in v3:
time: 169 us
  waiting for transfers between devices  88 us (52%)
  starting transfers between devices  34.7 us (21%)
  local copies, waits for them, and re-layouts  23.1 us (14%)
  Pallas kernels  19.5 us (12%)
  other arithmetic  2.24 us (1%)
    ppermute x11, waiting for transfers between devices, over_chips(): return lax.ppermute(value, 'expert', pairs)  53.1 us
    ppermute x12, waiting for transfers between devices, over_rep(): return lax.ppermute(value, 'rep', [(i, i ^ bits) for i in range(4)])  34.8 us
    unnamed x64, local copies, waits for them, and re-layouts  23.1 us
    pallas_call x8, Pallas kernels, call(): pl.pallas_call(kernel, out_shape=[jax.ShapeDtypeStruct(shape, dtype) for...  19.5 us
    ppermute x11, starting transfers between devices, over_chips(): return lax.ppermute(value, 'expert', pairs)  18.4 us
    ppermute x12, starting transfers between devices, over_rep(): return lax.ppermute(value, 'rep', [(i, i ^ bits) for i in range(4)])  13.5 us
  transfers between devices with their start and end apart: 36, of which 12 were waited for; matrix products, arithmetic and copies ran while one was open for 0% of the time, Pallas kernels for 10%

profile of v3, /device:TPU:0, one launch (start us, length us, event | category | flops | bytes accessed | tf_op | source)
XLA Modules:
  0.0 168.5 jit_solution(14646250987372780853)
XLA Ops:
  0.6 1.1 copy-done.1
  1.7 1.0 copy-done.2
  2.7 1.0 copy-done.3
  3.7 1.0 copy-done.5
  8.6 2.5 %collective-permute-start.6 = (bf16[1,384,384]{2,1,0:T(8,128)(2,1)S(1)}, bf16[1,384,384]{2,1,0:T(8,128)(2,1)S(1)}, u32[]{:S(2)}, u32[]{:S(2)}) collective-permute-start(bf16[1,384,384]{2,1,0:T(8,128)(2,1)S(1)} %copy-done.5), channel_id=1, source_target_pairs={{0,16},{8,24},{16,0},{24,8},{1,17},{9,25},{17,1},{25,9},{2,18},{10... | collective-permute-start | bytes 884744 | tf_op jit(solution)/shard_map/ppermute | solution.py:257
  11.1 1.5 collective-permute-start.5
  12.6 2.6 %collective-permute-start.13 = (bf16[128,1536]{1,0:T(8,128)(2,1)S(1)}, bf16[128,1536]{1,0:T(8,128)(2,1)}, u32[]{:S(2)}, u32[]{:S(2)}) collective-permute-start(bf16[128,1536]{1,0:T(8,128)(2,1)S(1)} %copy-done.3), channel_id=1, source_target_pairs={{0,4},{1,5},{2,6},{3,7},{4,0},{5,1},{6,2},{7,3},{8,12},{9,13},{10,... | collective-permute-start | bytes 1179656 | tf_op jit(solution)/shard_map/ppermute | solution.py:261
  15.2 1.6 collective-permute-start.9
  16.8 2.0 %collective-permute-done.6.refs_6_ = bf16[1,384,384]{2,1,0:T(8,128)(2,1)S(1)} collective-permute-done((bf16[1,384,384]{2,1,0:T(8,128)(2,1)S(1)}, bf16[1,384,384]{2,1,0:T(8,128)(2,1)S(1)}, u32[]{:S(2)}, u32[]{:S(2)}) %collective-permute-start.6) | collective-permute-done | bytes 294944 | tf_op jit(solution)/shard_map/ppermute | solution.py:257
  18.8 1.7 %collective-permute-start.2 = (bf16[1,384,768]{2,1,0:T(8,128)(2,1)S(1)}, bf16[1,384,768]{2,1,0:T(8,128)(2,1)S(1)}, u32[]{:S(2)}, u32[]{:S(2)}) collective-permute-start(bf16[1,384,768]{2,1,0:T(8,128)(2,1)S(1)} %copy-done.1), channel_id=1, source_target_pairs={{0,8},{8,0},{16,24},{24,16},{1,9},{9,1},{17,25},{25,17},{2,10},{10... | collective-permute-start | bytes 1769480 | tf_op jit(solution)/shard_map/ppermute | solution.py:257
  22.7 11.4 %collective-permute-done.13.refs_8_ = bf16[128,1536]{1,0:T(8,128)(2,1)} collective-permute-done((bf16[128,1536]{1,0:T(8,128)(2,1)S(1)}, bf16[128,1536]{1,0:T(8,128)(2,1)}, u32[]{:S(2)}, u32[]{:S(2)}) %collective-permute-start.13) | collective-permute-done | bytes 393248 | tf_op jit(solution)/shard_map/ppermute | solution.py:261
  34.1 3.1 %collective-permute-start.11 = (bf16[136,1536]{1,0:T(8,128)(2,1)S(1)}, bf16[136,1536]{1,0:T(8,128)(2,1)}, u32[]{:S(2)}, u32[]{:S(2)}) collective-permute-start(bf16[136,1536]{1,0:T(8,128)(2,1)S(1)} %get-tuple-element.38.y0.refs_2_), channel_id=1, source_target_pairs={{0,2},{1,3},{2,0},{3,1},{4,6},{5,7},{6,4},{7,5},{8,10},{9,11},{10,... | collective-permute-start | bytes 1253384 | tf_op jit(solution)/shard_map/ppermute | solution.py:261
  37.1 1.3 collective-permute-start.24
  39.9 20.5 %collective-permute-done.15.refs_10_ = bf16[136,1536]{1,0:T(8,128)(2,1)} collective-permute-done((bf16[136,1536]{1,0:T(8,128)(2,1)S(1)}, bf16[136,1536]{1,0:T(8,128)(2,1)}, u32[]{:S(2)}, u32[]{:S(2)}) %collective-permute-start.15) | collective-permute-done | bytes 417824 | tf_op jit(solution)/shard_map/ppermute | solution.py:261
  60.9 1.5 collective-permute-start.4
  63.3 4.4 %collective-permute-done.24.e0 = bf16[128,1536]{1,0:T(8,128)(2,1)S(1)} collective-permute-done((bf16[128,1536]{1,0:T(8,128)(2,1)}, bf16[128,1536]{1,0:T(8,128)(2,1)S(1)}, u32[]{:S(2)}, u32[]{:S(2)}) %collective-permute-start.24) | collective-permute-done | bytes 393248 | tf_op jit(solution)/shard_map/ppermute | solution.py:261
  69.0 8.1 %collective-permute-done.7.refs_7_ = bf16[1,384,384]{2,1,0:T(8,128)(2,1)S(1)} collective-permute-done((bf16[1,384,384]{2,1,0:T(8,128)(2,1)S(1)}, bf16[1,384,384]{2,1,0:T(8,128)(2,1)S(1)}, u32[]{:S(2)}, u32[]{:S(2)}) %collective-permute-start.7) | collective-permute-done | bytes 294944 | tf_op jit(solution)/shard_map/ppermute | solution.py:257
  77.9 1.3 collective-permute-start.20
  79.2 0.9 copy-done.11
  80.5 5.8 %collective-permute-done.4.refs_3_ = bf16[1,384,768]{2,1,0:T(8,128)(2,1)S(1)} collective-permute-done((bf16[1,384,768]{2,1,0:T(8,128)(2,1)S(1)}, bf16[1,384,768]{2,1,0:T(8,128)(2,1)S(1)}, u32[]{:S(2)}, u32[]{:S(2)}) %collective-permute-start.4) | collective-permute-done | bytes 589856 | tf_op jit(solution)/shard_map/ppermute | solution.py:257
  87.8 1.1 copy-done.10
  88.9 1.1 copy-done.12
  89.9 1.1 copy-done.14
  91.0 1.0 copy-done.16
  92.0 1.0 copy-done.19
  93.0 1.0 copy-done.22
  94.0 1.0 copy-done.25
  95.0 1.0 copy-done.27
  95.9 1.0 copy-done.29
  96.9 1.0 copy-done.31
  97.9 3.0 %shard_map.112 = (bf16[136,1536]{1,0:T(8,128)(2,1)S(1)}, bf16[136,1536]{1,0:T(8,128)(2,1)S(1)}, bf16[256,768]{1,0:T(8,128)(2,1)S(1)}, bf16[256,384]{1,0:T(8,128)...) custom-call(s32[2]{0:T(128)S(1)} %pad_add_fusion.ids_ref, bf16[128,1536]{1,0:T(8,128)(2,1)S(1)} %copy-done.19, ...), custom_call_target="tpu_custom_call" | custom-call | flops 1509949440 | bytes 4194304 | tf_op jit(solution)/shard_map/pallas_call | solution.py:25
  100.9 1.4 shard_map.114
  103.0 8.8 %shard_map.113 = (bf16[2,136,1536]{2,1,0:T(8,128)(2,1)S(1)}, bf16[2,136,1536]{2,1,0:T(8,128)(2,1)S(1)}, f32[1536,768]{1,0:T(8,128)S(1)}, f32[384,1536]{1,0:T(8,128)S(1)}) custom-call(s32[2]{0:T(128)S(1)} %pad_add_fusion.ids_ref, bf16[128,1536]{1,0:T(8,128)(2,1)S(1)} %copy-done.20, bf16[128,1536]{1,0:T(8,128)(2,1)S(1)} %copy-done.23, ...), custom_call_target="tpu_custom_call" | custom-call | flops 4529848320 | bytes 4194304 | tf_op jit(solution)/shard_map/pallas_call | solution.py:25
  111.9 1.9 %shard_map.115 = (bf16[192,1152]{1,0:T(8,128)(2,1)S(1)}, bf16[192,1152]{1,0:T(8,128)(2,1)S(1)}, bf16[256,768]{1,0:T(8,128)(2,1)S(1)}, bf16[256,384]{1,0:T(8,128)...) custom-call(s32[2]{0:T(128)S(1)} %pad_add_fusion.ids_ref, ...), custom_call_target="tpu_custom_call" | custom-call | flops 603979776 | bytes 4194304 | tf_op jit(solution)/shard_map/pallas_call | solution.py:25
  116.5 1.6 shard_map.117
  118.1 1.3 collective-permute-start.32
  119.5 8.8 %collective-permute-done.34 = bf16[192,1152]{1,0:T(8,128)(2,1)S(1)} collective-permute-done((bf16[192,1152]{1,0:T(8,128)(2,1)S(1)}, bf16[192,1152]{1,0:T(8,128)(2,1)S(1)}, u32[]{:S(2)}, u32[]{:S(2)}) %collective-permute-start.34) | collective-permute-done | bytes 442400 | tf_op jit(solution)/shard_map/ppermute | solution.py:257
  128.9 4.4 %collective-permute-start.29 = (bf16[136,1536]{1,0:T(8,128)(2,1)S(1)}, bf16[136,1536]{1,0:T(8,128)(2,1)S(1)}, u32[]{:S(2)}, u32[]{:S(2)}) collective-permute-start(bf16[136,1536]{1,0:T(8,128)(2,1)S(1)} %add_convert_fusion.2), channel_id=1, source_target_pairs={{0,6},{1,7},{2,4},{3,5},{4,2},{5,3},{6,0},{7,1},{8,14},{9,15},{10,... | collective-permute-start | bytes 1253384 | tf_op jit(solution)/shard_map/ppermute | solution.py:261
  133.4 1.6 collective-permute-start.35
  135.8 1.9 %collective-permute-done.32.t1b_ref = bf16[192,1152]{1,0:T(8,128)(2,1)S(1)} collective-permute-done((bf16[192,1152]{1,0:T(8,128)(2,1)S(1)}, bf16[192,1152]{1,0:T(8,128)(2,1)S(1)}, u32[]{:S(2)}, u32[]{:S(2)}) %collective-permute-start.32) | collective-permute-done | bytes 442400 | tf_op jit(solution)/shard_map/ppermute | solution.py:257
  137.7 1.4 collective-permute-start.18
  139.2 2.1 %collective-permute-done.33.t2a_ref = bf16[192,1152]{1,0:T(8,128)(2,1)S(1)} collective-permute-done((bf16[192,1152]{1,0:T(8,128)(2,1)S(1)}, bf16[192,1152]{1,0:T(8,128)(2,1)S(1)}, u32[]{:S(2)}, u32[]{:S(2)}) %collective-permute-start.33) | collective-permute-done | bytes 442400 | tf_op jit(solution)/shard_map/ppermute | solution.py:257
  141.3 1.4 collective-permute-start.19
  142.8 6.1 %collective-permute-done.35.t2b_ref = bf16[192,1152]{1,0:T(8,128)(2,1)S(1)} collective-permute-done((bf16[192,1152]{1,0:T(8,128)(2,1)S(1)}, bf16[192,1152]{1,0:T(8,128)(2,1)S(1)}, u32[]{:S(2)}, u32[]{:S(2)}) %collective-permute-start.35) | collective-permute-done | bytes 442400 | tf_op jit(solution)/shard_map/ppermute | solution.py:257
  148.8 1.3 shard_map.118
  150.2 2.7 %collective-permute-done.18 = bf16[136,1536]{1,0:T(8,128)(2,1)S(1)} collective-permute-done((bf16[136,1536]{1,0:T(8,128)(2,1)S(1)}, bf16[136,1536]{1,0:T(8,128)(2,1)S(1)}, u32[]{:S(2)}, u32[]{:S(2)}) %collective-permute-start.18) | collective-permute-done | bytes 417824 | tf_op jit(solution)/shard_map/ppermute | solution.py:261
  152.8 14.1 %collective-permute-done.19 = bf16[136,1536]{1,0:T(8,128)(2,1)S(1)} collective-permute-done((bf16[136,1536]{1,0:T(8,128)(2,1)S(1)}, bf16[136,1536]{1,0:T(8,128)(2,1)S(1)}, u32[]{:S(2)}, u32[]{:S(2)}) %collective-permute-start.19) | collective-permute-done | bytes 417824 | tf_op jit(solution)/shard_map/ppermute | solution.py:261
  167.5 1.0 add_convert_fusion.6
  (105 shorter events, 18.5 us)
Async XLA Ops:
  0.6 1.1 copy-start.1
  1.7 1.0 copy-start.2
  7.4 14.5 %collective-permute-start = (bf16[128,1536]{1,0:T(8,128)(2,1)S(1)}, bf16[128,1536]{1,0:T(8,128)(2,1)S(1)}, u32[]{:S(2)}, u32[]{:S(2)}) collective-permute-start(bf16[128,1536]{1,0:T(8,128)(2,1)S(1)} %get-tuple-element.37.x0.refs_0_), channel_id=1, source_target_pairs={{0,1},{1,0},{2,3},{3,2},{4,5},{5,4},{6,7},{7,6},{8,9},{9,8},{10,11... | collective-permute-start | bytes 1179656 | tf_op jit(solution)/shard_map/ppermute | solution.py:264
  8.6 10.2 %collective-permute-start.6 = (bf16[1,384,384]{2,1,0:T(8,128)(2,1)S(1)}, bf16[1,384,384]{2,1,0:T(8,128)(2,1)S(1)}, u32[]{:S(2)}, u32[]{:S(2)}) collective-permute-start(bf16[1,384,384]{2,1,0:T(8,128)(2,1)S(1)} %copy-done.5), channel_id=1, source_target_pairs={{0,16},{8,24},{16,0},{24,8},{1,17},{9,25},{17,1},{25,9},{2,18},{10... | collective-permute-start | bytes 884744 | tf_op jit(solution)/shard_map/ppermute | solution.py:257
  11.1 9.4 %collective-permute-start.5 = (bf16[1,384,384]{2,1,0:T(8,128)(2,1)S(1)}, bf16[1,384,384]{2,1,0:T(8,128)(2,1)S(1)}, u32[]{:S(2)}, u32[]{:S(2)}) collective-permute-start(bf16[1,384,384]{2,1,0:T(8,128)(2,1)S(1)} %copy-done.5), channel_id=1, source_target_pairs={{0,8},{8,0},{16,24},{24,16},{1,9},{9,1},{17,25},{25,17},{2,10},{10... | collective-permute-start | bytes 884744 | tf_op jit(solution)/shard_map/ppermute | solution.py:257
  12.6 21.5 %collective-permute-start.13 = (bf16[128,1536]{1,0:T(8,128)(2,1)S(1)}, bf16[128,1536]{1,0:T(8,128)(2,1)}, u32[]{:S(2)}, u32[]{:S(2)}) collective-permute-start(bf16[128,1536]{1,0:T(8,128)(2,1)S(1)} %copy-done.3), channel_id=1, source_target_pairs={{0,4},{1,5},{2,6},{3,7},{4,0},{5,1},{6,2},{7,3},{8,12},{9,13},{10,... | collective-permute-start | bytes 1179656 | tf_op jit(solution)/shard_map/ppermute | solution.py:261
  15.2 18.9 %collective-permute-start.9 = (bf16[128,1536]{1,0:T(8,128)(2,1)S(1)}, bf16[128,1536]{1,0:T(8,128)(2,1)}, u32[]{:S(2)}, u32[]{:S(2)}) collective-permute-start(bf16[128,1536]{1,0:T(8,128)(2,1)S(1)} %copy-done.3), channel_id=1, source_target_pairs={{0,2},{1,3},{2,0},{3,1},{4,6},{5,7},{6,4},{7,5},{8,10},{9,11},{10,... | collective-permute-start | bytes 1179656 | tf_op jit(solution)/shard_map/ppermute | solution.py:261
  18.8 42.2 %collective-permute-start.2 = (bf16[1,384,768]{2,1,0:T(8,128)(2,1)S(1)}, bf16[1,384,768]{2,1,0:T(8,128)(2,1)S(1)}, u32[]{:S(2)}, u32[]{:S(2)}) collective-permute-start(bf16[1,384,768]{2,1,0:T(8,128)(2,1)S(1)} %copy-done.1), channel_id=1, source_target_pairs={{0,8},{8,0},{16,24},{24,16},{1,9},{9,1},{17,25},{25,17},{2,10},{10... | collective-permute-start | bytes 1769480 | tf_op jit(solution)/shard_map/ppermute | solution.py:257
  21.2 15.9 %collective-permute-start.26 = (bf16[128,1536]{1,0:T(8,128)(2,1)S(1)}, bf16[128,1536]{1,0:T(8,128)(2,1)S(1)}, u32[]{:S(2)}, u32[]{:S(2)}) collective-permute-start(bf16[128,1536]{1,0:T(8,128)(2,1)S(1)} %copy-done.3), channel_id=1, source_target_pairs={{2,4},{3,5},{4,2},{5,3},{10,12},{11,13},{12,10},{13,11},{18,20},{1... | collective-permute-start | bytes 1179656 | tf_op jit(solution)/shard_map/ppermute | solution.py:261
  22.7 15.8 %collective-permute-start.1 = (bf16[136,1536]{1,0:T(8,128)(2,1)S(1)}, bf16[136,1536]{1,0:T(8,128)(2,1)S(1)}, u32[]{:S(2)}, u32[]{:S(2)}) collective-permute-start(bf16[136,1536]{1,0:T(8,128)(2,1)S(1)} %get-tuple-element.38.y0.refs_2_), channel_id=1, source_target_pairs={{0,1},{1,0},{2,3},{3,2},{4,5},{5,4},{6,7},{7,6},{8,9},{9,8},{10,11... | collective-permute-start | bytes 1253384 | tf_op jit(solution)/shard_map/ppermute | solution.py:264
  34.0 26.4 %collective-permute-start.15 = (bf16[136,1536]{1,0:T(8,128)(2,1)S(1)}, bf16[136,1536]{1,0:T(8,128)(2,1)}, u32[]{:S(2)}, u32[]{:S(2)}) collective-permute-start(bf16[136,1536]{1,0:T(8,128)(2,1)S(1)} %get-tuple-element.38.y0.refs_2_), channel_id=1, source_target_pairs={{0,4},{1,5},{2,6},{3,7},{4,0},{5,1},{6,2},{7,3},{8,12},{9,13},{10,... | collective-permute-start | bytes 1253384 | tf_op jit(solution)/shard_map/ppermute | solution.py:261
  34.1 29.2 %collective-permute-start.11 = (bf16[136,1536]{1,0:T(8,128)(2,1)S(1)}, bf16[136,1536]{1,0:T(8,128)(2,1)}, u32[]{:S(2)}, u32[]{:S(2)}) collective-permute-start(bf16[136,1536]{1,0:T(8,128)(2,1)S(1)} %get-tuple-element.38.y0.refs_2_), channel_id=1, source_target_pairs={{0,2},{1,3},{2,0},{3,1},{4,6},{5,7},{6,4},{7,5},{8,10},{9,11},{10,... | collective-permute-start | bytes 1253384 | tf_op jit(solution)/shard_map/ppermute | solution.py:261
  37.1 30.5 %collective-permute-start.24 = (bf16[128,1536]{1,0:T(8,128)(2,1)}, bf16[128,1536]{1,0:T(8,128)(2,1)S(1)}, u32[]{:S(2)}, u32[]{:S(2)}) collective-permute-start(bf16[128,1536]{1,0:T(8,128)(2,1)} %collective-permute-done.13.refs_8_), channel_id=1, source_target_pairs={{4,6},{5,7},{2,0},{3,1},{12,14},{13,15},{10,8},{11,9},{20,22},{21,... | collective-permute-start | bytes 1179656 | tf_op jit(solution)/shard_map/ppermute | solution.py:261
  39.2 28.5 %collective-permute-start.22 = (bf16[136,1536]{1,0:T(8,128)(2,1)S(1)}, bf16[136,1536]{1,0:T(8,128)(2,1)S(1)}, u32[]{:S(2)}, u32[]{:S(2)}) collective-permute-start(bf16[136,1536]{1,0:T(8,128)(2,1)S(1)} %get-tuple-element.38.y0.refs_2_), channel_id=1, source_target_pairs={{2,4},{3,5},{4,2},{5,3},{10,12},{11,13},{12,10},{13,11},{18,20},{1... | collective-permute-start | bytes 1253384 | tf_op jit(solution)/shard_map/ppermute | solution.py:261
  60.4 18.7 %collective-permute-start.3 = (bf16[1,384,768]{2,1,0:T(8,128)(2,1)S(1)}, bf16[1,384,768]{2,1,0:T(8,128)(2,1)S(1)}, u32[]{:S(2)}, u32[]{:S(2)}) collective-permute-start(bf16[1,384,768]{2,1,0:T(8,128)(2,1)S(1)} %copy-done.1), channel_id=1, source_target_pairs={{0,16},{8,24},{16,0},{24,8},{1,17},{9,25},{17,1},{25,9},{2,18},{10... | collective-permute-start | bytes 1769480 | tf_op jit(solution)/shard_map/ppermute | solution.py:257
  60.9 25.5 %collective-permute-start.4 = (bf16[1,384,768]{2,1,0:T(8,128)(2,1)S(1)}, bf16[1,384,768]{2,1,0:T(8,128)(2,1)S(1)}, u32[]{:S(2)}, u32[]{:S(2)}) collective-permute-start(bf16[1,384,768]{2,1,0:T(8,128)(2,1)S(1)} %collective-permute-done.2.refs_1_), channel_id=1, source_target_pairs={{0,16},{8,24},{16,0},{24,8},{1,17},{9,25},{17,1},{25,9},{2,18},{10... | collective-permute-start | bytes 1769480 | tf_op jit(solution)/shard_map/ppermute | solution.py:257
  63.3 16.8 %collective-permute-start.27 = (bf16[128,1536]{1,0:T(8,128)(2,1)S(1)}, bf16[128,1536]{1,0:T(8,128)(2,1)S(1)}, u32[]{:S(2)}, u32[]{:S(2)}) collective-permute-start(bf16[128,1536]{1,0:T(8,128)(2,1)S(1)} %collective-permute-done.26.m0), channel_id=1, source_target_pairs={{0,1},{1,0},{2,3},{3,2},{4,5},{5,4},{6,7},{7,6},{8,9},{9,8},{10,11... | collective-permute-start | bytes 1179656 | tf_op jit(solution)/shard_map/ppermute | solution.py:264
  67.7 19.5 %collective-permute-start.25 = (bf16[128,1536]{1,0:T(8,128)(2,1)S(1)}, bf16[128,1536]{1,0:T(8,128)(2,1)S(1)}, u32[]{:S(2)}, u32[]{:S(2)}) collective-permute-start(bf16[128,1536]{1,0:T(8,128)(2,1)S(1)} %collective-permute-done.24.e0), channel_id=1, source_target_pairs={{0,1},{1,0},{2,3},{3,2},{4,5},{5,4},{6,7},{7,6},{8,9},{9,8},{10,11... | collective-permute-start | bytes 1179656 | tf_op jit(solution)/shard_map/ppermute | solution.py:264
  67.7 9.4 %collective-permute-start.7 = (bf16[1,384,384]{2,1,0:T(8,128)(2,1)S(1)}, bf16[1,384,384]{2,1,0:T(8,128)(2,1)S(1)}, u32[]{:S(2)}, u32[]{:S(2)}) collective-permute-start(bf16[1,384,384]{2,1,0:T(8,128)(2,1)S(1)} %collective-permute-done.6.refs_6_), channel_id=1, source_target_pairs={{0,8},{8,0},{16,24},{24,16},{1,9},{9,1},{17,25},{25,17},{2,10},{10... | collective-permute-start | bytes 884744 | tf_op jit(solution)/shard_map/ppermute | solution.py:257
  77.9 24.6 %collective-permute-start.20 = (bf16[136,1536]{1,0:T(8,128)(2,1)}, bf16[136,1536]{1,0:T(8,128)(2,1)S(1)}, u32[]{:S(2)}, u32[]{:S(2)}) collective-permute-start(bf16[136,1536]{1,0:T(8,128)(2,1)} %collective-permute-done.15.refs_10_), channel_id=1, source_target_pairs={{4,6},{5,7},{2,0},{3,1},{12,14},{13,15},{10,8},{11,9},{20,22},{21,... | collective-permute-start | bytes 1253384 | tf_op jit(solution)/shard_map/ppermute | solution.py:261
  80.0 22.9 %collective-permute-start.16 = (bf16[136,1536]{1,0:T(8,128)(2,1)}, bf16[136,1536]{1,0:T(8,128)(2,1)}, u32[]{:S(2)}, u32[]{:S(2)}) collective-permute-start(bf16[136,1536]{1,0:T(8,128)(2,1)} %collective-permute-done.15.refs_10_), channel_id=1, source_target_pairs={{0,1},{1,0},{2,3},{3,2},{4,5},{5,4},{6,7},{7,6},{8,9},{9,8},{10,11... | collective-permute-start | bytes 1253384 | tf_op jit(solution)/shard_map/ppermute | solution.py:264
  80.0 22.9 %collective-permute-start.12 = (bf16[136,1536]{1,0:T(8,128)(2,1)}, bf16[136,1536]{1,0:T(8,128)(2,1)}, u32[]{:S(2)}, u32[]{:S(2)}) collective-permute-start(bf16[136,1536]{1,0:T(8,128)(2,1)} %collective-permute-done.11.refs_6_), channel_id=1, source_target_pairs={{0,1},{1,0},{2,3},{3,2},{4,5},{5,4},{6,7},{7,6},{8,9},{9,8},{10,11... | collective-permute-start | bytes 1253384 | tf_op jit(solution)/shard_map/ppermute | solution.py:264
  87.2 15.1 %collective-permute-start.14 = (bf16[128,1536]{1,0:T(8,128)(2,1)}, bf16[128,1536]{1,0:T(8,128)(2,1)}, u32[]{:S(2)}, u32[]{:S(2)}) collective-permute-start(bf16[128,1536]{1,0:T(8,128)(2,1)} %collective-permute-done.13.refs_8_), channel_id=1, source_target_pairs={{0,1},{1,0},{2,3},{3,2},{4,5},{5,4},{6,7},{7,6},{8,9},{9,8},{10,11... | collective-permute-start | bytes 1179656 | tf_op jit(solution)/shard_map/ppermute | solution.py:264
  87.2 15.7 %collective-permute-start.10 = (bf16[128,1536]{1,0:T(8,128)(2,1)}, bf16[128,1536]{1,0:T(8,128)(2,1)}, u32[]{:S(2)}, u32[]{:S(2)}) collective-permute-start(bf16[128,1536]{1,0:T(8,128)(2,1)} %collective-permute-done.9.refs_4_), channel_id=1, source_target_pairs={{0,1},{1,0},{2,3},{3,2},{4,5},{5,4},{6,7},{7,6},{8,9},{9,8},{10,11... | collective-permute-start | bytes 1179656 | tf_op jit(solution)/shard_map/ppermute | solution.py:264
  87.8 1.1 copy-start.10
  88.9 1.1 copy-start.12
  89.9 1.1 copy-start.14
  91.0 1.0 copy-start.16
  100.9 2.1 %copy-start.17 = (bf16[136,1536]{1,0:T(8,128)(2,1)S(1)}, bf16[136,1536]{1,0:T(8,128)(2,1)}, u32[]{:S(2)}) copy-start(bf16[136,1536]{1,0:T(8,128)(2,1)} %copy-done.15) | copy-start | bytes 1253380
  100.9 2.1 %copy-start.20 = (bf16[128,1536]{1,0:T(8,128)(2,1)S(1)}, bf16[128,1536]{1,0:T(8,128)(2,1)}, u32[]{:S(2)}) copy-start(bf16[128,1536]{1,0:T(8,128)(2,1)} %copy-done.18) | copy-start | bytes 1179652
  100.9 2.1 %copy-start.23 = (bf16[128,1536]{1,0:T(8,128)(2,1)S(1)}, bf16[128,1536]{1,0:T(8,128)(2,1)}, u32[]{:S(2)}) copy-start(bf16[128,1536]{1,0:T(8,128)(2,1)} %copy-done.21) | copy-start | bytes 1179652
  102.4 9.5 %collective-permute-start.23 = (bf16[136,1536]{1,0:T(8,128)(2,1)S(1)}, bf16[136,1536]{1,0:T(8,128)(2,1)S(1)}, u32[]{:S(2)}, u32[]{:S(2)}) collective-permute-start(bf16[136,1536]{1,0:T(8,128)(2,1)S(1)} %collective-permute-done.22.m0), channel_id=1, source_target_pairs={{0,1},{1,0},{2,3},{3,2},{4,5},{5,4},{6,7},{7,6},{8,9},{9,8},{10,11... | collective-permute-start | bytes 1253384 | tf_op jit(solution)/shard_map/ppermute | solution.py:264
  102.5 9.4 %collective-permute-start.21 = (bf16[136,1536]{1,0:T(8,128)(2,1)S(1)}, bf16[136,1536]{1,0:T(8,128)(2,1)S(1)}, u32[]{:S(2)}, u32[]{:S(2)}) collective-permute-start(bf16[136,1536]{1,0:T(8,128)(2,1)S(1)} %collective-permute-done.20.e0), channel_id=1, source_target_pairs={{0,1},{1,0},{2,3},{3,2},{4,5},{5,4},{6,7},{7,6},{8,9},{9,8},{10,11... | collective-permute-start | bytes 1253384 | tf_op jit(solution)/shard_map/ppermute | solution.py:264
  114.5 3.5 %collective-permute-start.28 = (bf16[136,1536]{1,0:T(8,128)(2,1)S(1)}, bf16[136,1536]{1,0:T(8,128)(2,1)S(1)}, u32[]{:S(2)}, u32[]{:S(2)}) collective-permute-start(bf16[136,1536]{1,0:T(8,128)(2,1)S(1)} %get-tuple-element.58), channel_id=1, source_target_pairs={{0,1},{1,0},{2,3},{3,2},{4,5},{5,4},{6,7},{7,6},{8,9},{9,8},{10,11... | collective-permute-start | bytes 1253384 | tf_op jit(solution)/shard_map/ppermute | solution.py:264
  114.7 18.7 %collective-permute-start.17 = (bf16[2,136,1536]{2,1,0:T(8,128)(2,1)S(1)}, bf16[2,136,1536]{2,1,0:T(8,128)(2,1)S(1)}, u32[]{:S(2)}, u32[]{:S(2)}) collective-permute-start(bf16[2,136,1536]{2,1,0:T(8,128)(2,1)S(1)} %get-tuple-element.48), channel_id=1, source_target_pairs={{0,1},{1,0},{2,3},{3,2},{4,5},{5,4},{6,7},{7,6},{8,9},{9,8},{10,11... | collective-permute-start | bytes 2506760 | tf_op jit(solution)/shard_map/ppermute | solution.py:264
  115.1 20.1 %collective-permute-start.8 = (bf16[136,1536]{1,0:T(8,128)(2,1)S(1)}, bf16[136,1536]{1,0:T(8,128)(2,1)S(1)}, u32[]{:S(2)}, u32[]{:S(2)}) collective-permute-start(bf16[136,1536]{1,0:T(8,128)(2,1)S(1)} %get-tuple-element.42), channel_id=1, source_target_pairs={{0,1},{1,0},{2,3},{3,2},{4,5},{5,4},{6,7},{7,6},{8,9},{9,8},{10,11... | collective-permute-start | bytes 1253384 | tf_op jit(solution)/shard_map/ppermute | solution.py:264
  115.2 13.0 %collective-permute-start.34 = (bf16[192,1152]{1,0:T(8,128)(2,1)S(1)}, bf16[192,1152]{1,0:T(8,128)(2,1)S(1)}, u32[]{:S(2)}, u32[]{:S(2)}) collective-permute-start(bf16[192,1152]{1,0:T(8,128)(2,1)S(1)} %get-tuple-element.67), channel_id=1, source_target_pairs={{0,8},{8,0},{16,24},{24,16},{1,9},{9,1},{17,25},{25,17},{2,10},{10... | collective-permute-start | bytes 1327112 | tf_op jit(solution)/shard_map/ppermute | solution.py:257
  115.7 13.1 %collective-permute-start.30 = (bf16[192,1152]{1,0:T(8,128)(2,1)S(1)}, bf16[192,1152]{1,0:T(8,128)(2,1)S(1)}, u32[]{:S(2)}, u32[]{:S(2)}) collective-permute-start(bf16[192,1152]{1,0:T(8,128)(2,1)S(1)} %get-tuple-element.63), channel_id=1, source_target_pairs={{0,16},{8,24},{16,0},{24,8},{1,17},{9,25},{17,1},{25,9},{2,18},{10... | collective-permute-start | bytes 1327112 | tf_op jit(solution)/shard_map/ppermute | solution.py:257
  118.1 19.7 %collective-permute-start.32 = (bf16[192,1152]{1,0:T(8,128)(2,1)S(1)}, bf16[192,1152]{1,0:T(8,128)(2,1)S(1)}, u32[]{:S(2)}, u32[]{:S(2)}) collective-permute-start(bf16[192,1152]{1,0:T(8,128)(2,1)S(1)} %get-tuple-element.64), channel_id=1, source_target_pairs={{0,8},{8,0},{16,24},{24,16},{1,9},{9,1},{17,25},{25,17},{2,10},{10... | collective-permute-start | bytes 1327112 | tf_op jit(solution)/shard_map/ppermute | solution.py:257
  128.2 13.0 %collective-permute-start.33 = (bf16[192,1152]{1,0:T(8,128)(2,1)S(1)}, bf16[192,1152]{1,0:T(8,128)(2,1)S(1)}, u32[]{:S(2)}, u32[]{:S(2)}) collective-permute-start(bf16[192,1152]{1,0:T(8,128)(2,1)S(1)} %get-tuple-element.65), channel_id=1, source_target_pairs={{0,16},{8,24},{16,0},{24,8},{1,17},{9,25},{17,1},{25,9},{2,18},{10... | collective-permute-start | bytes 1327112 | tf_op jit(solution)/shard_map/ppermute | solution.py:257
  128.9 21.3 %collective-permute-start.29 = (bf16[136,1536]{1,0:T(8,128)(2,1)S(1)}, bf16[136,1536]{1,0:T(8,128)(2,1)S(1)}, u32[]{:S(2)}, u32[]{:S(2)}) collective-permute-start(bf16[136,1536]{1,0:T(8,128)(2,1)S(1)} %add_convert_fusion.2), channel_id=1, source_target_pairs={{0,6},{1,7},{2,4},{3,5},{4,2},{5,3},{6,0},{7,1},{8,14},{9,15},{10,... | collective-permute-start | bytes 1253384 | tf_op jit(solution)/shard_map/ppermute | solution.py:261
  133.3 15.5 %copy-start = (bf16[1,384,768]{2,1,0:T(8,128)(2,1)S(1)}, bf16[1,384,768]{2,1,0:T(8,128)(2,1)}, u32[]{:S(2)}) copy-start(bf16[1,384,768]{2,1,0:T(8,128)(2,1)} %min_ref.1) | copy-start | bytes 1769476
  133.3 15.5 %copy-start.4 = (bf16[1,384,384]{2,1,0:T(8,128)(2,1)S(1)}, bf16[1,384,384]{2,1,0:T(8,128)(2,1)}, u32[]{:S(2)}) copy-start(bf16[1,384,384]{2,1,0:T(8,128)(2,1)} %mout_ref.1) | copy-start | bytes 884740
  133.4 15.4 %collective-permute-start.35 = (bf16[192,1152]{1,0:T(8,128)(2,1)S(1)}, bf16[192,1152]{1,0:T(8,128)(2,1)S(1)}, u32[]{:S(2)}, u32[]{:S(2)}) collective-permute-start(bf16[192,1152]{1,0:T(8,128)(2,1)S(1)} %add_convert_fusion), channel_id=1, source_target_pairs={{0,16},{8,24},{16,0},{24,8},{1,17},{9,25},{17,1},{25,9},{2,18},{10... | collective-permute-start | bytes 1327112 | tf_op jit(solution)/shard_map/ppermute | solution.py:257
  135.2 13.6 %collective-permute-start.31 = (bf16[192,1152]{1,0:T(8,128)(2,1)S(1)}, bf16[192,1152]{1,0:T(8,128)(2,1)S(1)}, u32[]{:S(2)}, u32[]{:S(2)}) collective-permute-start(bf16[192,1152]{1,0:T(8,128)(2,1)S(1)} %add_convert_fusion.1), channel_id=1, source_target_pairs={{0,8},{8,0},{16,24},{24,16},{1,9},{9,1},{17,25},{25,17},{2,10},{10... | collective-permute-start | bytes 1327112 | tf_op jit(solution)/shard_map/ppermute | solution.py:257
  137.7 15.1 %collective-permute-start.18 = (bf16[136,1536]{1,0:T(8,128)(2,1)S(1)}, bf16[136,1536]{1,0:T(8,128)(2,1)S(1)}, u32[]{:S(2)}, u32[]{:S(2)}) collective-permute-start(bf16[136,1536]{1,0:T(8,128)(2,1)S(1)} %get-tuple-element.70), channel_id=1, source_target_pairs={{0,2},{1,3},{2,0},{3,1},{4,6},{5,7},{6,4},{7,5},{8,10},{9,11},{10,... | collective-permute-start | bytes 1253384 | tf_op jit(solution)/shard_map/ppermute | solution.py:261
  141.3 25.7 %collective-permute-start.19 = (bf16[136,1536]{1,0:T(8,128)(2,1)S(1)}, bf16[136,1536]{1,0:T(8,128)(2,1)S(1)}, u32[]{:S(2)}, u32[]{:S(2)}) collective-permute-start(bf16[136,1536]{1,0:T(8,128)(2,1)S(1)} %get-tuple-element.71), channel_id=1, source_target_pairs={{0,4},{1,5},{2,6},{3,7},{4,0},{5,1},{6,2},{7,3},{8,12},{9,13},{10,... | collective-permute-start | bytes 1253384 | tf_op jit(solution)/shard_map/ppermute | solution.py:261
  142.7 24.3 %copy-start.7 = (s32[128,4]{0,1:T(4,128)S(1)}, s32[128,4]{0,1:T(4,128)}, u32[]{:S(2)}) copy-start(s32[128,4]{0,1:T(4,128)} %param.9) | copy-start | bytes 6148
  (20 other events, 16.8 us)

commit v4 on v3

--- a/solution.py
+++ b/solution.py
@@ -34,13 +34,12 @@
 
 
 def stage_kernel(routes_hbm, gates_hbm, x_hbm, y_hbm, win_hbm, wout_hbm, *refs):
-    x_ref, block_ref, win_ref, wout_ref, routes_ref, gates_ref, sems = refs
-    tok = x_ref.shape[0]
-    experts = block_ref.shape[0] - tok
+    x_ref, block_ref, win_ref, wout_ref, routes_ref, gates_ref, y_ref, sems = refs
+    tok, width = y_ref.shape
     moves = (
         (routes_hbm, routes_ref),
         (gates_hbm, gates_ref),
-        (y_hbm, block_ref.at[0:tok]),
+        (y_hbm, y_ref),
         (x_hbm, x_ref),
         (win_hbm, win_ref),
         (wout_hbm, wout_ref),
@@ -50,15 +49,28 @@
         copy.start()
     copies[0].wait()
     copies[1].wait()
+    first = width // 128 * tok
+    experts = block_ref.shape[0] - first
     ids = lax.broadcasted_iota(jnp.int32, (experts, tok), 0)
     dense = jnp.zeros((experts, tok), f32)
     for k in range(routes_ref.shape[0]):
         gate = gates_ref[k : k + 1, :].astype(f32)
         dense = dense + jnp.where(ids == routes_ref[k : k + 1, :], gate, 0.0)
-    tail = jnp.zeros((experts, block_ref.shape[1] - tok), f32)
-    block_ref[tok:, :] = jnp.concatenate([dense, tail], axis=1).astype(bf16)
-    for copy in copies[2:]:
+    block_ref[first:, :] = dense.astype(bf16)
+    copies[2].wait()
+    for j in range(width // 128):
+        block_ref[j * tok : (j + 1) * tok, :] = y_ref[:, j * 128 : (j + 1) * 128]
+    for copy in copies[3:]:
         copy.wait()
+
+
+def stacked(width, tok, experts):
+    return (width // 128 * tok + experts, 128)
+
+
+def unstack(ref, width):
+    tok = 128
+    return jnp.concatenate([ref[j * tok : (j + 1) * tok, :] for j in range(width // 128)], axis=1)
 
 
 def is_end(expert, chips):
@@ -93,11 +105,10 @@
     return silu, u * s * (1.0 + g * (1.0 - s)), hidden
 
 
-def block_step(tables, expert, x, y, win, wout, keep_ref, give_ref, dgu_ref, ch_ref):
-    tok, ffn = x.shape[0] // 2, wout.shape[0]
-    experts = tables[0].shape[0]
+def back_step(tables, expert, y, acts, win, wout, keep_ref, give_ref, dgu_ref, ch_ref):
+    silu, slope, hidden = acts
+    tok, ffn, experts = y.shape[0] // 2, wout.shape[0], tables[0].shape[0]
     gate = jnp.concatenate([gate_column(table, expert) for table in tables], axis=0)
-    silu, slope, hidden = activations(dot(x, win[...], 1, 0))
     back = dot(y, wout[...], 1, 1)
     gate_grad = jnp.sum(hidden.astype(f32) * back, axis=1, keepdims=True)
     ch_ref[...] = (hidden.astype(f32) * gate).astype(bf16)
@@ -111,38 +122,60 @@
 
 
 def own_kernel(ids_ref, x0, x1, y0, y1, *refs):
-    in_pieces, out_pieces = refs[0:4], refs[4:8]
-    keep_ref, give_ref, dgu_ref, ch_ref, win, wout = refs[8:]
+    in_pieces, out_pieces, refs = refs[0:5], refs[5:9], refs[9:]
+    keep_ref, give_ref, dgu_ref, ch_ref, win, wout = refs
     rep, expert = ids_ref[0], ids_ref[1]
-    shard = wout.shape[1] // 4
+    shard, (tok, width) = wout.shape[1] // 4, x0.shape
+    cut = in_pieces[3].shape[1]
     for j in range(4):
         at = pl.multiple_of((rep ^ j) * shard, 128)
-        win[pl.ds(at, shard), :] = in_pieces[j][0]
         wout[:, pl.ds(at, shard)] = out_pieces[j][0]
-    tok = x0.shape[0]
-    tables = [ref[tok:, 0:tok] for ref in (y0, y1)]
-    x, y = (jnp.concatenate([ref[0:tok, :] for ref in pair], axis=0) for pair in ((x0, x1), (y0, y1)))
-    block_step(tables, expert, x, y, win, wout, keep_ref, give_ref, dgu_ref, ch_ref)
+        if j < 3:
+            win[pl.ds(at, shard), :] = in_pieces[j][0]
+        else:
+            win[pl.ds(at, cut), :] = in_pieces[3][0]
+            win[pl.ds(at + cut, shard - cut), :] = in_pieces[4][0]
+    tables = [ref[width // 128 * tok :, :] for ref in (y0, y1)]
+    x = jnp.concatenate([x0[...], x1[...]], axis=0)
+    y = jnp.concatenate([unstack(y0, width), unstack(y1, width)], axis=0)
+    acts = activations(dot(x, win[...], 1, 0))
+    back_step(tables, expert, y, acts, win, wout, keep_ref, give_ref, dgu_ref, ch_ref)
+
+
+def early_kernel(n0, n1, f0, f1, win, xs, silu_ref, slope_ref, hidden_ref):
+    tok = n0.shape[0]
+    for n, ref in enumerate((n0, n1, f0, f1)):
+        xs[n * tok : (n + 1) * tok, :] = ref[...]
+    silu_ref[...], slope_ref[...], hidden_ref[...] = activations(dot(xs[...], win[...], 1, 0))
 
 
 def rest_kernel(ids_ref, *refs):
-    blocks, (own_dgu, own_ch, win, wout), refs = (refs[0:4], refs[4:8], refs[8:12]), refs[12:16], refs[16:]
-    keep_ref, give_ref, acc_in_ref, acc_out_ref, xs, ys, dgus, chs = refs
-    tok = blocks[0][0].shape[0]
+    blocks, (silu, slope, hidden, win, wout), refs = refs[0:4], refs[4:9], refs[9:]
+    keep_ref, give_ref, ys, dgus, chs = refs
+    rows, width = ys.shape[0] // 2, ys.shape[1]
+    tok = rows // 2
+    for n in range(2):
+        part, pair = slice(n * rows, (n + 1) * rows), blocks[2 * n : 2 * n + 2]
+        for i, ref in enumerate(pair):
+            ys[n * rows + i * tok : n * rows + (i + 1) * tok, :] = unstack(ref, width)
+        tables = [ref[width // 128 * tok :, :] for ref in pair]
+        acts = (silu[part, :], slope[part, :], hidden[part, :])
+        outs = (keep_ref.at[n], give_ref.at[n], dgus.at[part], chs.at[part])
+        back_step(tables, ids_ref[1], ys[part, :], acts, win, wout, *outs)
+
+
+def sum_kernel(x0, x1, y0, y1, own_dgu, own_ch, more_xs, more_ys, more_dgu, more_ch, *refs):
+    acc_in_ref, acc_out_ref, xs, ys, dgus, chs = refs
+    tok, width = x0.shape
     rows = 2 * tok
-    dgus[0:rows, :] = own_dgu[...]
-    chs[0:rows, :] = own_ch[...]
-    for n, (x0, x1, y0, y1) in enumerate(blocks):
-        at = n * rows
-        for i, (xr, yr) in enumerate(((x0, y0), (x1, y1))):
-            xs[at + i * tok : at + (i + 1) * tok, :] = xr[...]
-            ys[at + i * tok : at + (i + 1) * tok, :] = yr[0:tok, :]
-    for n in (1, 2):
-        part = slice(n * rows, (n + 1) * rows)
-        outs = (keep_ref.at[n - 1], give_ref.at[n - 1], dgus.at[part], chs.at[part])
-        x, y = xs[part, :], ys[part, :]
-        tables = [ref[tok:, 0:tok] for ref in blocks[n][2:]]
-        block_step(tables, ids_ref[1], x, y, win, wout, *outs)
+    for i, (x, y) in enumerate(((x0, y0), (x1, y1))):
+        xs[i * tok : (i + 1) * tok, :] = x[...]
+        ys[i * tok : (i + 1) * tok, :] = unstack(y, width)
+    for whole, first, more in ((dgus, own_dgu, more_dgu), (chs, own_ch, more_ch)):
+        whole[0:rows, :] = first[...]
+        whole[rows:, :] = more[...]
+    xs[rows:, :] = more_xs[...]
+    ys[rows:, :] = more_ys[...]
     acc_in_ref[...] = dot(xs[...], dgus[...], 0, 0)
     acc_out_ref[...] = dot(chs[...], ys[...], 0, 0)
 
@@ -183,19 +216,21 @@
     at_end = is_end(ids_ref[1], chips)
     ffn, experts = wout.shape[0], tab_ref.shape[1]
 
+    width = ys.shape[1]
+
     @pl.when(at_end)
     def _():
-        ys[0:tok, :] = e0[0:tok, :]
-        ys[tok:, :] = e1[0:tok, :]
+        ys[0:tok, :] = unstack(e0, width)
+        ys[tok:, :] = unstack(e1, width)
 
     @pl.when(jnp.logical_not(at_end))
     def _():
-        ys[0:tok, :] = m0[0:tok, :]
-        ys[tok:, :] = m1[0:tok, :]
-
-    columns = []
+        ys[0:tok, :] = unstack(m0, width)
+        ys[tok:, :] = unstack(m1, width)
+
+    columns, first = [], width // 128 * tok
     for end, mid in ((e0, m0), (e1, m1)):
-        table = jnp.where(at_end, end[tok:, 0:tok].astype(f32), mid[tok:, 0:tok].astype(f32))
+        table = jnp.where(at_end, end[first:, :].astype(f32), mid[first:, :].astype(f32))
         columns.append(gate_column(table, expert))
     gate = jnp.concatenate(columns, axis=0)
     back = dot(ys[...], wout[...], 1, 1)
@@ -278,9 +313,11 @@
     own_x, own_y, own_in, own_out = call(
         stage_kernel,
         sources,
-        [((tok, width), bf16), ((tok + experts, width), bf16), (w_in.shape, bf16), (w_out.shape, bf16)],
-        [((top, tok), jnp.int32), ((top, tok), bf16), pltpu.SemaphoreType.DMA((len(sources),))],
-        mib=2,
+        [((tok, width), bf16), (stacked(width, tok, experts), bf16)]
+        + [(w_in.shape, bf16), (w_out.shape, bf16)],
+        [((top, tok), jnp.int32), ((top, tok), bf16), ((tok, width), bf16)]
+        + [pltpu.SemaphoreType.DMA((len(sources),))],
+        mib=4,
         far=len(sources),
     )
     far_y = over_chips(own_y, to_far)
@@ -290,42 +327,58 @@
     middle_x = over_chips(tokens, to_middle)
     own_xp = partner(own_x)
     own_yp = partner(own_y)
-    w3in = over_rep(w1in, 2)
+    cut = shard * 3 // 4
+    w3ina = over_rep(w1in[:, :cut], 2)
     ends_x = over_chips(far_x, to_ends)
+    w3inb = over_rep(w2in[:, cut:], 1)
     w3out = over_rep(w2out, 1)
     far_xp = partner(far_x)
     near_xp = partner(near_x)
     middle_y = over_chips(own_y, to_middle)
-    ends_y = over_chips(far_y, to_ends)
-    far_yp = partner(far_y)
-    near_yp = partner(near_y)
     rows = 2 * tok
     block = ((tok + experts, width), bf16)
     flops = 5 * rows * width * both_w
     own_blocks = [own_x, own_xp, own_y, own_yp]
     keep, give_own, own_dgu, own_ch, win, wout = call(
         own_kernel,
-        [ids, *own_blocks, own_in, w1in, w2in, w3in, own_out, w1out, w2out, w3out],
+        [ids, *own_blocks, own_in, w1in, w2in, w3ina, w3inb, own_out, w1out, w2out, w3out],
         [block, block, ((rows, both_w), bf16), ((rows, ffn), bf16)]
         + [((width, both_w), bf16), ((ffn, width), bf16)],
         mib=10,
         scalars=1,
         flops=flops,
     )
+    ends_y = over_chips(far_y, to_ends)
+    far_yp = partner(far_y)
+    near_yp = partner(near_y)
+    middle_xp = partner(middle_x)
+    ends_xp = partner(ends_x)
     got = partner(give_own)
     home_own = (keep.astype(f32) + got.astype(f32)).astype(bf16)
-    keep, give, acc_in, acc_out = call(
+    more_xs, *early = call(
+        early_kernel,
+        [near_x, near_xp, far_x, far_xp, win],
+        [((2 * rows, width), bf16), ((2 * rows, ffn), f32), ((2 * rows, ffn), f32), ((2 * rows, ffn), bf16)],
+        mib=6,
+        flops=2 * flops // 5 * 2,
+    )
+    keep, give, *more = call(
         rest_kernel,
-        [ids, *own_blocks, near_x, near_xp, near_y, near_yp, far_x, far_xp, far_y, far_yp]
-        + [own_dgu, own_ch, win, wout],
-        [((2, tok + experts, width), bf16)] * 2 + [((width, both_w), f32), ((ffn, width), f32)],
+        [ids, near_y, near_yp, far_y, far_yp, *early, win, wout],
+        [((2, tok + experts, width), bf16)] * 2
+        + [((2 * rows, width), bf16), ((2 * rows, both_w), bf16), ((2 * rows, ffn), bf16)],
+        mib=8,
+        scalars=1,
+        flops=flops,
+    )
+    acc_in, acc_out = call(
+        sum_kernel,
+        [*own_blocks, own_dgu, own_ch, more_xs, *more],
+        [((width, both_w), f32), ((ffn, width), f32)],
         [((3 * rows, n), bf16) for n in (width, width, both_w, ffn)],
-        mib=18,
-        scalars=1,
-        flops=3 * flops,
-    )
-    middle_xp = partner(middle_x)
-    ends_xp = partner(ends_x)
+        mib=16,
+        flops=2 * flops,
+    )
     got = partner(give)
     home_near, home_far = ((keep[i].astype(f32) + got[i].astype(f32)).astype(bf16) for i in range(2))
     xs, silu, slope, hidden = call(

time: 169 us -> 163 us (0.964)
  waiting for transfers between devices: 88 us -> 75.8 us
  Pallas kernels: 19.5 us -> 22.5 us
  starting transfers between devices: 34.7 us -> 36.9 us
    ppermute x11, waiting for transfers between devices: 53.1 us -> 42.2 us  [over_chips(): return lax.ppermute(value, 'expert', pairs)]
    pallas_call x8 -> x10, Pallas kernels: 19.5 us -> 22.5 us  [call(): pl.pallas_call(kernel, out_shape=[jax.ShapeDtypeStruct(shape, dtype) for...]
    ppermute x11, starting transfers between devices: 18.4 us -> 20.3 us  [over_chips(): return lax.ppermute(value, 'expert', pairs)]
    ppermute x12 -> x13, waiting for transfers between devices: 34.8 us -> 33.5 us  [over_rep(): return lax.ppermute(value, 'rep', [(i, i ^ bits) for i in range(4)])]
    unnamed x64 -> x76, local copies, waits for them, and re-layouts: 23.1 us -> 24 us
    ppermute x12 -> x13, starting transfers between devices: 13.5 us -> 14.4 us  [over_rep(): return lax.ppermute(value, 'rep', [(i, i ^ bits) for i in range(4)])]
  transfers between devices with their start and end apart: 36 -> 37, of which waited for: 12 -> 13; matrix products, arithmetic and copies ran while one was open for 0% -> 0% of each run, Pallas kernels for 10% -> 12%
where the time goes in v4:
time: 163 us; the launch traced here: 162 us
  waiting for transfers between devices  75.8 us (47%)
  starting transfers between devices  36.9 us (23%)
  local copies, waits for them, and re-layouts  24.1 us (15%)
  Pallas kernels  22.5 us (14%)
  other arithmetic  2.23 us (1%)
    ppermute x11, waiting for transfers between devices, over_chips(): return lax.ppermute(value, 'expert', pairs)  42.2 us
    ppermute x13, waiting for transfers between devices, over_rep(): return lax.ppermute(value, 'rep', [(i, i ^ bits) for i in range(4)])  33.5 us
    unnamed x76, local copies, waits for them, and re-layouts  24 us
    pallas_call x10, Pallas kernels, call(): pl.pallas_call(kernel, out_shape=[jax.ShapeDtypeStruct(shape, dtype) for...  22.5 us
    ppermute x11, starting transfers between devices, over_chips(): return lax.ppermute(value, 'expert', pairs)  20.3 us
    ppermute x13, starting transfers between devices, over_rep(): return lax.ppermute(value, 'rep', [(i, i ^ bits) for i in range(4)])  14.4 us
  transfers between devices with their start and end apart: 37, of which 13 were waited for; matrix products, arithmetic and copies ran while one was open for 0% of the time, Pallas kernels for 12%

profile of v4, /device:TPU:0, one launch (start us, length us, event | category | flops | bytes accessed | tf_op | source)
XLA Modules:
  0.0 162.5 jit_solution(3548359738240225228)
XLA Ops:
  0.6 3.1 %collective-permute-start.7 = (bf16[1,384,384]{2,1,0:T(8,128)(2,1)}, bf16[1,384,384]{2,1,0:T(8,128)(2,1)S(1)}, u32[]{:S(2)}, u32[]{:S(2)}) collective-permute-start(bf16[1,384,384]{2,1,0:T(8,128)(2,1)} %wout_hbm.1), channel_id=1, source_target_pairs={{0,16},{8,24},{16,0},{24,8},{1,17},{9,25},{17,1},{25,9},{2,18},{10... | collective-permute-start | bytes 884744 | tf_op jit(solution)/shard_map/ppermute | solution.py:292
  3.7 1.0 copy-done.1
  4.7 1.0 copy-done.5
  7.0 2.2 %shard_map.111 = (bf16[128,1536]{1,0:T(8,128)(2,1)S(1)}, bf16[1544,128]{1,0:T(8,128)(2,1)}, bf16[1,384,768]{2,1,0:T(8,128)(2,1)S(1)}, bf16[1,384,384]{2,1,0:T(8,128)(2,1)S(1)}) custom-call(s32[4,128]{1,0:T(4,128)S(1)} %bitcast.11, bf16[4,128]{1,0:T(4,128)(2,1)S(1)} %bitcast.13, bf16[128,1536]{1,0:T(8,128)(2,1)} %x_hbm.1, bf16[128,1536]{1,0:T(8,128)(2,1)S(1)} %copy-done.1, ...), custom_call_target="tpu_custom_call" | custom-call | bytes 4194304 | tf_op jit(solution)/shard_map/pallas_call | solution.py:25
  11.5 2.6 %collective-permute-start.16 = (bf16[128,1536]{1,0:T(8,128)(2,1)}, bf16[128,1536]{1,0:T(8,128)(2,1)}, u32[]{:S(2)}, u32[]{:S(2)}) collective-permute-start(bf16[128,1536]{1,0:T(8,128)(2,1)} %x_hbm.1), channel_id=1, source_target_pairs={{0,4},{1,5},{2,6},{3,7},{4,0},{5,1},{6,2},{7,3},{8,12},{9,13},{10,... | collective-permute-start | bytes 1179656 | tf_op jit(solution)/shard_map/ppermute | solution.py:296
  14.1 1.6 collective-permute-start.14
  15.7 1.5 collective-permute-start.6
  17.7 7.8 %collective-permute-done.6.refs_6_ = bf16[1,384,384]{2,1,0:T(8,128)(2,1)S(1)} collective-permute-done((bf16[1,384,384]{2,1,0:T(8,128)(2,1)S(1)}, bf16[1,384,384]{2,1,0:T(8,128)(2,1)S(1)}, u32[]{:S(2)}, u32[]{:S(2)}) %collective-permute-start.6) | collective-permute-done | bytes 294944 | tf_op jit(solution)/shard_map/ppermute | solution.py:292
  28.2 5.0 %collective-permute-done.16.f0 = bf16[128,1536]{1,0:T(8,128)(2,1)} collective-permute-done((bf16[128,1536]{1,0:T(8,128)(2,1)}, bf16[128,1536]{1,0:T(8,128)(2,1)}, u32[]{:S(2)}, u32[]{:S(2)}) %collective-permute-start.16) | collective-permute-done | bytes 393248 | tf_op jit(solution)/shard_map/ppermute | solution.py:296
  33.2 1.0 collective-permute-start.12
  34.2 3.0 %collective-permute-done.2.refs_1_ = bf16[1,384,768]{2,1,0:T(8,128)(2,1)S(1)} collective-permute-done((bf16[1,384,768]{2,1,0:T(8,128)(2,1)}, bf16[1,384,768]{2,1,0:T(8,128)(2,1)S(1)}, u32[]{:S(2)}, u32[]{:S(2)}) %collective-permute-start.2) | collective-permute-done | bytes 589856 | tf_op jit(solution)/shard_map/ppermute | solution.py:292
  39.0 19.0 %collective-permute-done.12.refs_2_ = bf16[1544,128]{1,0:T(8,128)(2,1)S(1)} collective-permute-done((bf16[1544,128]{1,0:T(8,128)(2,1)}, bf16[1544,128]{1,0:T(8,128)(2,1)S(1)}, u32[]{:S(2)}, u32[]{:S(2)}) %collective-permute-start.12) | collective-permute-done | bytes 395296 | tf_op jit(solution)/shard_map/ppermute | solution.py:296
  58.7 1.5 collective-permute-start.8
  61.6 7.0 %collective-permute-done.8.refs_8_ = bf16[1,384,384]{2,1,0:T(8,128)(2,1)S(1)} collective-permute-done((bf16[1,384,384]{2,1,0:T(8,128)(2,1)S(1)}, bf16[1,384,384]{2,1,0:T(8,128)(2,1)S(1)}, u32[]{:S(2)}, u32[]{:S(2)}) %collective-permute-start.8) | collective-permute-done | bytes 294944 | tf_op jit(solution)/shard_map/ppermute | solution.py:292
  70.0 1.3 collective-permute-done.5.refs_4_
  72.7 1.3 collective-permute-start.21
  76.1 1.3 collective-permute-start.25
  77.4 1.1 copy-done.3
  78.5 1.1 copy-done.7
  79.6 1.1 copy-done.12
  80.6 1.0 copy-done.14
  81.6 1.0 copy-done.16
  82.6 1.0 copy-done.19
  83.6 1.0 copy-done.22
  84.6 1.0 copy-done.31
  85.6 1.0 copy-done.33
  86.5 1.0 copy-done.35
  87.5 0.9 copy-done.37
  88.4 3.6 %shard_map.112 = (bf16[136,1536]{1,0:T(8,128)(2,1)S(1)}, bf16[136,1536]{1,0:T(8,128)(2,1)S(1)}, bf16[256,768]{1,0:T(8,128)(2,1)S(1)}, bf16[256,384]{1,0:T(8,128)...) custom-call(s32[2]{0:T(128)S(1)} %pad_add_fusion.ids_ref, bf16[128,1536]{1,0:T(8,128)(2,1)S(1)} %copy-done.19, ...), custom_call_target="tpu_custom_call" | custom-call | flops 1509949440 | bytes 4194304 | tf_op jit(solution)/shard_map/pallas_call | solution.py:25
  92.1 2.5 %shard_map.113 = (bf16[512,1536]{1,0:T(8,128)(2,1)S(1)}, f32[512,384]{1,0:T(8,128)S(1)}, f32[512,384]{1,0:T(8,128)S(1)}, bf16[512,384]{1,0:T(8,128)(2,1)S(1)}) custom-call(bf16[128,1536]{1,0:T(8,128)(2,1)S(1)} %copy-done.25, bf16[128,1536]{1,0:T(8,128)(2,1)S(1)} %copy-done.29, bf16[128,1536]{1,0:T(8,128)(2,1)} %collective-permute-done.16.f0, ...), custom_call_target="tpu_custom_call" | custom-call | flops 1207959552 | bytes 4194304 | tf_op jit(solution)/shard_map/pallas_call | solution.py:25
  95.7 3.1 %shard_map.114 = (bf16[2,136,1536]{2,1,0:T(8,128)(2,1)S(1)}, bf16[2,136,1536]{2,1,0:T(8,128)(2,1)S(1)}, bf16[512,1536]{1,0:T(8,128)(2,1)S(1)}, bf16[512,768]{1,0:T(8,128)(2,1)S(1)}, bf16[512,384]{1,0:T(8,128)(2,1)S(1)}) custom-call(s32[2]{0:T(128)S(1)} %pad_add_fusion.ids_ref, bf16[1544,128]{1,0:T(8,128)(2,1)S(1)} %collective-permute-done.10.refs_0_, ...), custom_call_target="tpu_custom_call" | custom-call | flops 1509949440 | bytes 4194304 | tf_op jit(solution)/shard_map/pallas_call | solution.py:25
  98.9 4.0 %shard_map.116 = (f32[1536,768]{1,0:T(8,128)S(1)}, f32[384,1536]{1,0:T(8,128)S(1)}) custom-call(bf16[128,1536]{1,0:T(8,128)(2,1)S(1)} %copy-done.20, bf16[128,1536]{1,0:T(8,128)(2,1)S(1)} %copy-done.23, bf16[1544,128]{1,0:T(8,128)(2,1)} %get-tuple-element.45.y0, bf16[1544,128]{1,0:T(8,128)(2,1)S(1)} %copy-done.17, ...), custom_call_target="tpu_custom_call" | custom-call | flops 3019898880 | bytes 4194304 | tf_op jit(solution)/shard_map/pallas_call | solution.py:25
  102.9 1.4 shard_map.115
  104.3 1.9 %shard_map.117 = (bf16[192,1152]{1,0:T(8,128)(2,1)S(1)}, bf16[192,1152]{1,0:T(8,128)(2,1)S(1)}, bf16[256,768]{1,0:T(8,128)(2,1)S(1)}, bf16[256,384]{1,0:T(8,128)...) custom-call(s32[2]{0:T(128)S(1)} %pad_add_fusion.ids_ref, ...), custom_call_target="tpu_custom_call" | custom-call | flops 603979776 | bytes 4194304 | tf_op jit(solution)/shard_map/pallas_call | solution.py:25
  107.7 1.5 collective-permute-start.35
  109.7 1.6 shard_map.119
  112.0 8.7 %collective-permute-done.35 = bf16[192,1152]{1,0:T(8,128)(2,1)S(1)} collective-permute-done((bf16[192,1152]{1,0:T(8,128)(2,1)S(1)}, bf16[192,1152]{1,0:T(8,128)(2,1)S(1)}, u32[]{:S(2)}, u32[]{:S(2)}) %collective-permute-start.35) | collective-permute-done | bytes 442400 | tf_op jit(solution)/shard_map/ppermute | solution.py:292
  121.5 3.5 %collective-permute-start.30 = (bf16[136,1536]{1,0:T(8,128)(2,1)S(1)}, bf16[136,1536]{1,0:T(8,128)(2,1)S(1)}, u32[]{:S(2)}, u32[]{:S(2)}) collective-permute-start(bf16[136,1536]{1,0:T(8,128)(2,1)S(1)} %add_convert_fusion.2), channel_id=1, source_target_pairs={{0,6},{1,7},{2,4},{3,5},{4,2},{5,3},{6,0},{7,1},{8,14},{9,15},{10,... | collective-permute-start | bytes 1253384 | tf_op jit(solution)/shard_map/ppermute | solution.py:296
  125.1 1.6 collective-permute-start.36
  126.9 1.6 collective-permute-start.32
  128.4 1.9 %collective-permute-done.33.t1b_ref = bf16[192,1152]{1,0:T(8,128)(2,1)S(1)} collective-permute-done((bf16[192,1152]{1,0:T(8,128)(2,1)S(1)}, bf16[192,1152]{1,0:T(8,128)(2,1)S(1)}, u32[]{:S(2)}, u32[]{:S(2)}) %collective-permute-start.33) | collective-permute-done | bytes 442400 | tf_op jit(solution)/shard_map/ppermute | solution.py:292
  130.3 2.7 %collective-permute-start.19 = (bf16[136,1536]{1,0:T(8,128)(2,1)S(1)}, bf16[136,1536]{1,0:T(8,128)(2,1)S(1)}, u32[]{:S(2)}, u32[]{:S(2)}) collective-permute-start(bf16[136,1536]{1,0:T(8,128)(2,1)S(1)} %get-tuple-element.84), channel_id=1, source_target_pairs={{0,2},{1,3},{2,0},{3,1},{4,6},{5,7},{6,4},{7,5},{8,10},{9,11},{10,... | collective-permute-start | bytes 1253384 | tf_op jit(solution)/shard_map/ppermute | solution.py:296
  132.9 0.9 collective-permute-done.34.t2a_ref
  133.8 4.6 %collective-permute-start.20 = (bf16[136,1536]{1,0:T(8,128)(2,1)S(1)}, bf16[136,1536]{1,0:T(8,128)(2,1)S(1)}, u32[]{:S(2)}, u32[]{:S(2)}) collective-permute-start(bf16[136,1536]{1,0:T(8,128)(2,1)S(1)} %get-tuple-element.85), channel_id=1, source_target_pairs={{0,4},{1,5},{2,6},{3,7},{4,0},{5,1},{6,2},{7,3},{8,12},{9,13},{10,... | collective-permute-start | bytes 1253384 | tf_op jit(solution)/shard_map/ppermute | solution.py:296
  138.6 2.8 %collective-permute-done.36.t2b_ref = bf16[192,1152]{1,0:T(8,128)(2,1)S(1)} collective-permute-done((bf16[192,1152]{1,0:T(8,128)(2,1)S(1)}, bf16[192,1152]{1,0:T(8,128)(2,1)S(1)}, u32[]{:S(2)}, u32[]{:S(2)}) %collective-permute-start.36) | collective-permute-done | bytes 442400 | tf_op jit(solution)/shard_map/ppermute | solution.py:292
  141.4 1.3 shard_map.120
  143.5 17.5 %collective-permute-done.20 = bf16[136,1536]{1,0:T(8,128)(2,1)S(1)} collective-permute-done((bf16[136,1536]{1,0:T(8,128)(2,1)S(1)}, bf16[136,1536]{1,0:T(8,128)(2,1)S(1)}, u32[]{:S(2)}, u32[]{:S(2)}) %collective-permute-start.20) | collective-permute-done | bytes 417824 | tf_op jit(solution)/shard_map/ppermute | solution.py:296
  161.5 1.0 add_convert_fusion.6
  (123 shorter events, 21.9 us)
Async XLA Ops:
  0.6 16.5 %collective-permute-start.7 = (bf16[1,384,384]{2,1,0:T(8,128)(2,1)}, bf16[1,384,384]{2,1,0:T(8,128)(2,1)S(1)}, u32[]{:S(2)}, u32[]{:S(2)}) collective-permute-start(bf16[1,384,384]{2,1,0:T(8,128)(2,1)} %wout_hbm.1), channel_id=1, source_target_pairs={{0,16},{8,24},{16,0},{24,8},{1,17},{9,25},{17,1},{25,9},{2,18},{10... | collective-permute-start | bytes 884744 | tf_op jit(solution)/shard_map/ppermute | solution.py:292
  10.7 16.0 %collective-permute-start = (bf16[128,1536]{1,0:T(8,128)(2,1)S(1)}, bf16[128,1536]{1,0:T(8,128)(2,1)S(1)}, u32[]{:S(2)}, u32[]{:S(2)}) collective-permute-start(bf16[128,1536]{1,0:T(8,128)(2,1)S(1)} %get-tuple-element.44.x0), channel_id=1, source_target_pairs={{0,1},{1,0},{2,3},{3,2},{4,5},{5,4},{6,7},{7,6},{8,9},{9,8},{10,11... | collective-permute-start | bytes 1179656 | tf_op jit(solution)/shard_map/ppermute | solution.py:299
  11.5 21.7 %collective-permute-start.16 = (bf16[128,1536]{1,0:T(8,128)(2,1)}, bf16[128,1536]{1,0:T(8,128)(2,1)}, u32[]{:S(2)}, u32[]{:S(2)}) collective-permute-start(bf16[128,1536]{1,0:T(8,128)(2,1)} %x_hbm.1), channel_id=1, source_target_pairs={{0,4},{1,5},{2,6},{3,7},{4,0},{5,1},{6,2},{7,3},{8,12},{9,13},{10,... | collective-permute-start | bytes 1179656 | tf_op jit(solution)/shard_map/ppermute | solution.py:296
  14.1 19.1 %collective-permute-start.14 = (bf16[128,1536]{1,0:T(8,128)(2,1)}, bf16[128,1536]{1,0:T(8,128)(2,1)S(1)}, u32[]{:S(2)}, u32[]{:S(2)}) collective-permute-start(bf16[128,1536]{1,0:T(8,128)(2,1)} %x_hbm.1), channel_id=1, source_target_pairs={{0,2},{1,3},{2,0},{3,1},{4,6},{5,7},{6,4},{7,5},{8,10},{9,11},{10,... | collective-permute-start | bytes 1179656 | tf_op jit(solution)/shard_map/ppermute | solution.py:296
  15.7 9.9 %collective-permute-start.6 = (bf16[1,384,384]{2,1,0:T(8,128)(2,1)S(1)}, bf16[1,384,384]{2,1,0:T(8,128)(2,1)S(1)}, u32[]{:S(2)}, u32[]{:S(2)}) collective-permute-start(bf16[1,384,384]{2,1,0:T(8,128)(2,1)S(1)} %copy-done.5), channel_id=1, source_target_pairs={{0,8},{8,0},{16,24},{24,16},{1,9},{9,1},{17,25},{25,17},{2,10},{10... | collective-permute-start | bytes 884744 | tf_op jit(solution)/shard_map/ppermute | solution.py:292
  17.1 20.0 %collective-permute-start.2 = (bf16[1,384,768]{2,1,0:T(8,128)(2,1)}, bf16[1,384,768]{2,1,0:T(8,128)(2,1)S(1)}, u32[]{:S(2)}, u32[]{:S(2)}) collective-permute-start(bf16[1,384,768]{2,1,0:T(8,128)(2,1)} %win_hbm.1), channel_id=1, source_target_pairs={{0,8},{8,0},{16,24},{24,16},{1,9},{9,1},{17,25},{25,17},{2,10},{10... | collective-permute-start | bytes 1769480 | tf_op jit(solution)/shard_map/ppermute | solution.py:292
  26.3 32.5 %collective-permute-start.3 = (bf16[1,384,768]{2,1,0:T(8,128)(2,1)}, bf16[1,384,768]{2,1,0:T(8,128)(2,1)S(1)}, u32[]{:S(2)}, u32[]{:S(2)}) collective-permute-start(bf16[1,384,768]{2,1,0:T(8,128)(2,1)} %win_hbm.1), channel_id=1, source_target_pairs={{0,16},{8,24},{16,0},{24,8},{1,17},{9,25},{17,1},{25,9},{2,18},{10... | collective-permute-start | bytes 1769480 | tf_op jit(solution)/shard_map/ppermute | solution.py:292
  27.5 10.1 %collective-permute-start.27 = (bf16[128,1536]{1,0:T(8,128)(2,1)}, bf16[128,1536]{1,0:T(8,128)(2,1)S(1)}, u32[]{:S(2)}, u32[]{:S(2)}) collective-permute-start(bf16[128,1536]{1,0:T(8,128)(2,1)} %x_hbm.1), channel_id=1, source_target_pairs={{2,4},{3,5},{4,2},{5,3},{10,12},{11,13},{12,10},{13,11},{18,20},{1... | collective-permute-start | bytes 1179656 | tf_op jit(solution)/shard_map/ppermute | solution.py:296
  33.2 5.1 %collective-permute-start.1 = (bf16[1544,128]{1,0:T(8,128)(2,1)}, bf16[1544,128]{1,0:T(8,128)(2,1)S(1)}, u32[]{:S(2)}, u32[]{:S(2)}) collective-permute-start(bf16[1544,128]{1,0:T(8,128)(2,1)} %get-tuple-element.45.y0), channel_id=1, source_target_pairs={{0,1},{1,0},{2,3},{3,2},{4,5},{5,4},{6,7},{7,6},{8,9},{9,8},{10,11... | collective-permute-start | bytes 1185800 | tf_op jit(solution)/shard_map/ppermute | solution.py:299
  33.2 24.8 %collective-permute-start.12 = (bf16[1544,128]{1,0:T(8,128)(2,1)}, bf16[1544,128]{1,0:T(8,128)(2,1)S(1)}, u32[]{:S(2)}, u32[]{:S(2)}) collective-permute-start(bf16[1544,128]{1,0:T(8,128)(2,1)} %get-tuple-element.45.y0), channel_id=1, source_target_pairs={{0,4},{1,5},{2,6},{3,7},{4,0},{5,1},{6,2},{7,3},{8,12},{9,13},{10,... | collective-permute-start | bytes 1185800 | tf_op jit(solution)/shard_map/ppermute | solution.py:296
  37.2 32.8 %copy-start.2 = (bf16[1,384,768]{2,1,0:T(8,128)(2,1)}, bf16[1,384,768]{2,1,0:T(8,128)(2,1)S(1)}, u32[]{:S(2)}) copy-start(bf16[1,384,768]{2,1,0:T(8,128)(2,1)S(1)} %collective-permute-done.2.refs_1_) | copy-start | bytes 1769476
  37.2 23.9 %collective-permute-start.10 = (bf16[1544,128]{1,0:T(8,128)(2,1)}, bf16[1544,128]{1,0:T(8,128)(2,1)S(1)}, u32[]{:S(2)}, u32[]{:S(2)}) collective-permute-start(bf16[1544,128]{1,0:T(8,128)(2,1)} %get-tuple-element.45.y0), channel_id=1, source_target_pairs={{0,2},{1,3},{2,0},{3,1},{4,6},{5,7},{6,4},{7,5},{8,10},{9,11},{10,... | collective-permute-start | bytes 1185800 | tf_op jit(solution)/shard_map/ppermute | solution.py:296
  37.6 37.6 %collective-permute-start.4 = (bf16[1,288,768]{2,1,0:T(8,128)(2,1)S(1)}, bf16[1,288,768]{2,1,0:T(8,128)(2,1)S(1)}, u32[]{:S(2)}, u32[]{:S(2)}) collective-permute-start(bf16[1,288,768]{2,1,0:T(8,128)(2,1)S(1)} %slice.56), channel_id=1, source_target_pairs={{0,16},{8,24},{16,0},{24,8},{1,17},{9,25},{17,1},{25,9},{2,18},{10... | collective-permute-start | bytes 1327112 | tf_op jit(solution)/shard_map/ppermute | solution.py:292
  39.0 33.0 %collective-permute-start.17 = (bf16[128,1536]{1,0:T(8,128)(2,1)}, bf16[128,1536]{1,0:T(8,128)(2,1)S(1)}, u32[]{:S(2)}, u32[]{:S(2)}) collective-permute-start(bf16[128,1536]{1,0:T(8,128)(2,1)} %collective-permute-done.16.f0), channel_id=1, source_target_pairs={{0,1},{1,0},{2,3},{3,2},{4,5},{5,4},{6,7},{7,6},{8,9},{9,8},{10,11... | collective-permute-start | bytes 1179656 | tf_op jit(solution)/shard_map/ppermute | solution.py:299
  58.0 16.1 %collective-permute-start.15 = (bf16[128,1536]{1,0:T(8,128)(2,1)S(1)}, bf16[128,1536]{1,0:T(8,128)(2,1)S(1)}, u32[]{:S(2)}, u32[]{:S(2)}) collective-permute-start(bf16[128,1536]{1,0:T(8,128)(2,1)S(1)} %collective-permute-done.14.n0), channel_id=1, source_target_pairs={{0,1},{1,0},{2,3},{3,2},{4,5},{5,4},{6,7},{7,6},{8,9},{9,8},{10,11... | collective-permute-start | bytes 1179656 | tf_op jit(solution)/shard_map/ppermute | solution.py:299
  58.7 9.9 %collective-permute-start.8 = (bf16[1,384,384]{2,1,0:T(8,128)(2,1)S(1)}, bf16[1,384,384]{2,1,0:T(8,128)(2,1)S(1)}, u32[]{:S(2)}, u32[]{:S(2)}) collective-permute-start(bf16[1,384,384]{2,1,0:T(8,128)(2,1)S(1)} %collective-permute-done.7.refs_7_), channel_id=1, source_target_pairs={{0,8},{8,0},{16,24},{24,16},{1,9},{9,1},{17,25},{25,17},{2,10},{10... | collective-permute-start | bytes 884744 | tf_op jit(solution)/shard_map/ppermute | solution.py:292
  61.0 10.3 %collective-permute-start.5 = (bf16[1,96,768]{2,1,0:T(8,128)(2,1)S(1)}, bf16[1,96,768]{2,1,0:T(8,128)(2,1)S(1)}, u32[]{:S(2)}, u32[]{:S(2)}) collective-permute-start(bf16[1,96,768]{2,1,0:T(8,128)(2,1)S(1)} %slice.57), channel_id=1, source_target_pairs={{0,8},{8,0},{16,24},{24,16},{1,9},{9,1},{17,25},{25,17},{2,10},{10... | collective-permute-start | bytes 442376 | tf_op jit(solution)/shard_map/ppermute | solution.py:292
  69.3 25.3 %collective-permute-start.23 = (bf16[1544,128]{1,0:T(8,128)(2,1)}, bf16[1544,128]{1,0:T(8,128)(2,1)S(1)}, u32[]{:S(2)}, u32[]{:S(2)}) collective-permute-start(bf16[1544,128]{1,0:T(8,128)(2,1)} %get-tuple-element.45.y0), channel_id=1, source_target_pairs={{2,4},{3,5},{4,2},{5,3},{10,12},{11,13},{12,10},{13,11},{18,20},{1... | collective-permute-start | bytes 1185800 | tf_op jit(solution)/shard_map/ppermute | solution.py:296
  72.0 23.2 %collective-permute-start.13 = (bf16[1544,128]{1,0:T(8,128)(2,1)S(1)}, bf16[1544,128]{1,0:T(8,128)(2,1)S(1)}, u32[]{:S(2)}, u32[]{:S(2)}) collective-permute-start(bf16[1544,128]{1,0:T(8,128)(2,1)S(1)} %collective-permute-done.12.refs_2_), channel_id=1, source_target_pairs={{0,1},{1,0},{2,3},{3,2},{4,5},{5,4},{6,7},{7,6},{8,9},{9,8},{10,11... | collective-permute-start | bytes 1185800 | tf_op jit(solution)/shard_map/ppermute | solution.py:299
  72.7 22.5 %collective-permute-start.21 = (bf16[1544,128]{1,0:T(8,128)(2,1)S(1)}, bf16[1544,128]{1,0:T(8,128)(2,1)S(1)}, u32[]{:S(2)}, u32[]{:S(2)}) collective-permute-start(bf16[1544,128]{1,0:T(8,128)(2,1)S(1)} %collective-permute-done.12.refs_2_), channel_id=1, source_target_pairs={{4,6},{5,7},{2,0},{3,1},{12,14},{13,15},{10,8},{11,9},{20,22},{21,... | collective-permute-start | bytes 1185800 | tf_op jit(solution)/shard_map/ppermute | solution.py:296
  74.8 20.9 %collective-permute-start.11 = (bf16[1544,128]{1,0:T(8,128)(2,1)S(1)}, bf16[1544,128]{1,0:T(8,128)(2,1)S(1)}, u32[]{:S(2)}, u32[]{:S(2)}) collective-permute-start(bf16[1544,128]{1,0:T(8,128)(2,1)S(1)} %collective-permute-done.10.refs_0_), channel_id=1, source_target_pairs={{0,1},{1,0},{2,3},{3,2},{4,5},{5,4},{6,7},{7,6},{8,9},{9,8},{10,11... | collective-permute-start | bytes 1185800 | tf_op jit(solution)/shard_map/ppermute | solution.py:299
  76.1 18.6 %collective-permute-start.25 = (bf16[128,1536]{1,0:T(8,128)(2,1)}, bf16[128,1536]{1,0:T(8,128)(2,1)S(1)}, u32[]{:S(2)}, u32[]{:S(2)}) collective-permute-start(bf16[128,1536]{1,0:T(8,128)(2,1)} %collective-permute-done.16.f0), channel_id=1, source_target_pairs={{4,6},{5,7},{2,0},{3,1},{12,14},{13,15},{10,8},{11,9},{20,22},{21,... | collective-permute-start | bytes 1179656 | tf_op jit(solution)/shard_map/ppermute | solution.py:296
  77.4 1.1 copy-start.3
  88.4 3.6 %copy-start.25 = (bf16[128,1536]{1,0:T(8,128)(2,1)S(1)}, bf16[128,1536]{1,0:T(8,128)(2,1)}, u32[]{:S(2)}) copy-start(bf16[128,1536]{1,0:T(8,128)(2,1)} %copy-done.24) | copy-start | bytes 1179652
  88.4 3.6 %copy-start.27 = (bf16[128,1536]{1,0:T(8,128)(2,1)S(1)}, bf16[128,1536]{1,0:T(8,128)(2,1)}, u32[]{:S(2)}) copy-start(bf16[128,1536]{1,0:T(8,128)(2,1)} %copy-done.26) | copy-start | bytes 1179652
  88.4 3.6 %copy-start.29 = (bf16[128,1536]{1,0:T(8,128)(2,1)S(1)}, bf16[128,1536]{1,0:T(8,128)(2,1)}, u32[]{:S(2)}) copy-start(bf16[128,1536]{1,0:T(8,128)(2,1)} %copy-done.28) | copy-start | bytes 1179652
  94.6 8.3 %collective-permute-start.28 = (bf16[128,1536]{1,0:T(8,128)(2,1)S(1)}, bf16[128,1536]{1,0:T(8,128)(2,1)S(1)}, u32[]{:S(2)}, u32[]{:S(2)}) collective-permute-start(bf16[128,1536]{1,0:T(8,128)(2,1)S(1)} %collective-permute-done.27.m0), channel_id=1, source_target_pairs={{0,1},{1,0},{2,3},{3,2},{4,5},{5,4},{6,7},{7,6},{8,9},{9,8},{10,11... | collective-permute-start | bytes 1179656 | tf_op jit(solution)/shard_map/ppermute | solution.py:299
  94.7 9.6 %collective-permute-start.24 = (bf16[1544,128]{1,0:T(8,128)(2,1)S(1)}, bf16[1544,128]{1,0:T(8,128)(2,1)S(1)}, u32[]{:S(2)}, u32[]{:S(2)}) collective-permute-start(bf16[1544,128]{1,0:T(8,128)(2,1)S(1)} %collective-permute-done.23.m0), channel_id=1, source_target_pairs={{0,1},{1,0},{2,3},{3,2},{4,5},{5,4},{6,7},{7,6},{8,9},{9,8},{10,11... | collective-permute-start | bytes 1185800 | tf_op jit(solution)/shard_map/ppermute | solution.py:299
  95.2 7.7 %collective-permute-start.26 = (bf16[128,1536]{1,0:T(8,128)(2,1)S(1)}, bf16[128,1536]{1,0:T(8,128)(2,1)S(1)}, u32[]{:S(2)}, u32[]{:S(2)}) collective-permute-start(bf16[128,1536]{1,0:T(8,128)(2,1)S(1)} %collective-permute-done.25.e0), channel_id=1, source_target_pairs={{0,1},{1,0},{2,3},{3,2},{4,5},{5,4},{6,7},{7,6},{8,9},{9,8},{10,11... | collective-permute-start | bytes 1179656 | tf_op jit(solution)/shard_map/ppermute | solution.py:299
  95.3 9.1 %collective-permute-start.22 = (bf16[1544,128]{1,0:T(8,128)(2,1)S(1)}, bf16[1544,128]{1,0:T(8,128)(2,1)S(1)}, u32[]{:S(2)}, u32[]{:S(2)}) collective-permute-start(bf16[1544,128]{1,0:T(8,128)(2,1)S(1)} %collective-permute-done.21.e0), channel_id=1, source_target_pairs={{0,1},{1,0},{2,3},{3,2},{4,5},{5,4},{6,7},{7,6},{8,9},{9,8},{10,11... | collective-permute-start | bytes 1185800 | tf_op jit(solution)/shard_map/ppermute | solution.py:299
  95.7 3.1 %copy-start.17 = (bf16[1544,128]{1,0:T(8,128)(2,1)S(1)}, bf16[1544,128]{1,0:T(8,128)(2,1)}, u32[]{:S(2)}) copy-start(bf16[1544,128]{1,0:T(8,128)(2,1)} %copy-done.15) | copy-start | bytes 1185796
  95.7 3.1 %copy-start.20 = (bf16[128,1536]{1,0:T(8,128)(2,1)S(1)}, bf16[128,1536]{1,0:T(8,128)(2,1)}, u32[]{:S(2)}) copy-start(bf16[128,1536]{1,0:T(8,128)(2,1)} %copy-done.18) | copy-start | bytes 1179652
  95.7 3.1 %copy-start.23 = (bf16[128,1536]{1,0:T(8,128)(2,1)S(1)}, bf16[128,1536]{1,0:T(8,128)(2,1)}, u32[]{:S(2)}) copy-start(bf16[128,1536]{1,0:T(8,128)(2,1)} %copy-done.21) | copy-start | bytes 1179652
  107.1 4.3 %collective-permute-start.29 = (bf16[136,1536]{1,0:T(8,128)(2,1)S(1)}, bf16[136,1536]{1,0:T(8,128)(2,1)S(1)}, u32[]{:S(2)}, u32[]{:S(2)}) collective-permute-start(bf16[136,1536]{1,0:T(8,128)(2,1)S(1)} %get-tuple-element.72), channel_id=1, source_target_pairs={{0,1},{1,0},{2,3},{3,2},{4,5},{5,4},{6,7},{7,6},{8,9},{9,8},{10,11... | collective-permute-start | bytes 1253384 | tf_op jit(solution)/shard_map/ppermute | solution.py:299
  107.2 17.8 %collective-permute-start.18 = (bf16[2,136,1536]{2,1,0:T(8,128)(2,1)S(1)}, bf16[2,136,1536]{2,1,0:T(8,128)(2,1)S(1)}, u32[]{:S(2)}, u32[]{:S(2)}) collective-permute-start(bf16[2,136,1536]{2,1,0:T(8,128)(2,1)S(1)} %get-tuple-element.56), channel_id=1, source_target_pairs={{0,1},{1,0},{2,3},{3,2},{4,5},{5,4},{6,7},{7,6},{8,9},{9,8},{10,11... | collective-permute-start | bytes 2506760 | tf_op jit(solution)/shard_map/ppermute | solution.py:299
  107.7 19.2 %collective-permute-start.9 = (bf16[136,1536]{1,0:T(8,128)(2,1)S(1)}, bf16[136,1536]{1,0:T(8,128)(2,1)S(1)}, u32[]{:S(2)}, u32[]{:S(2)}) collective-permute-start(bf16[136,1536]{1,0:T(8,128)(2,1)S(1)} %get-tuple-element.49), channel_id=1, source_target_pairs={{0,1},{1,0},{2,3},{3,2},{4,5},{5,4},{6,7},{7,6},{8,9},{9,8},{10,11... | collective-permute-start | bytes 1253384 | tf_op jit(solution)/shard_map/ppermute | solution.py:299
  107.7 13.0 %collective-permute-start.35 = (bf16[192,1152]{1,0:T(8,128)(2,1)S(1)}, bf16[192,1152]{1,0:T(8,128)(2,1)S(1)}, u32[]{:S(2)}, u32[]{:S(2)}) collective-permute-start(bf16[192,1152]{1,0:T(8,128)(2,1)S(1)} %get-tuple-element.81), channel_id=1, source_target_pairs={{0,8},{8,0},{16,24},{24,16},{1,9},{9,1},{17,25},{25,17},{2,10},{10... | collective-permute-start | bytes 1327112 | tf_op jit(solution)/shard_map/ppermute | solution.py:292
  109.2 12.2 %collective-permute-start.31 = (bf16[192,1152]{1,0:T(8,128)(2,1)S(1)}, bf16[192,1152]{1,0:T(8,128)(2,1)S(1)}, u32[]{:S(2)}, u32[]{:S(2)}) collective-permute-start(bf16[192,1152]{1,0:T(8,128)(2,1)S(1)} %get-tuple-element.77), channel_id=1, source_target_pairs={{0,16},{8,24},{16,0},{24,8},{1,17},{9,25},{17,1},{25,9},{2,18},{10... | collective-permute-start | bytes 1327112 | tf_op jit(solution)/shard_map/ppermute | solution.py:292
  111.4 18.9 %collective-permute-start.33 = (bf16[192,1152]{1,0:T(8,128)(2,1)S(1)}, bf16[192,1152]{1,0:T(8,128)(2,1)S(1)}, u32[]{:S(2)}, u32[]{:S(2)}) collective-permute-start(bf16[192,1152]{1,0:T(8,128)(2,1)S(1)} %get-tuple-element.78), channel_id=1, source_target_pairs={{0,8},{8,0},{16,24},{24,16},{1,9},{9,1},{17,25},{25,17},{2,10},{10... | collective-permute-start | bytes 1327112 | tf_op jit(solution)/shard_map/ppermute | solution.py:292
  120.8 13.0 %collective-permute-start.34 = (bf16[192,1152]{1,0:T(8,128)(2,1)S(1)}, bf16[192,1152]{1,0:T(8,128)(2,1)S(1)}, u32[]{:S(2)}, u32[]{:S(2)}) collective-permute-start(bf16[192,1152]{1,0:T(8,128)(2,1)S(1)} %get-tuple-element.79), channel_id=1, source_target_pairs={{0,16},{8,24},{16,0},{24,8},{1,17},{9,25},{17,1},{25,9},{2,18},{10... | collective-permute-start | bytes 1327112 | tf_op jit(solution)/shard_map/ppermute | solution.py:292
  121.5 21.2 %collective-permute-start.30 = (bf16[136,1536]{1,0:T(8,128)(2,1)S(1)}, bf16[136,1536]{1,0:T(8,128)(2,1)S(1)}, u32[]{:S(2)}, u32[]{:S(2)}) collective-permute-start(bf16[136,1536]{1,0:T(8,128)(2,1)S(1)} %add_convert_fusion.2), channel_id=1, source_target_pairs={{0,6},{1,7},{2,4},{3,5},{4,2},{5,3},{6,0},{7,1},{8,14},{9,15},{10,... | collective-permute-start | bytes 1253384 | tf_op jit(solution)/shard_map/ppermute | solution.py:296
  124.9 16.4 %copy-start = (bf16[1,384,768]{2,1,0:T(8,128)(2,1)S(1)}, bf16[1,384,768]{2,1,0:T(8,128)(2,1)}, u32[]{:S(2)}) copy-start(bf16[1,384,768]{2,1,0:T(8,128)(2,1)} %min_ref.1) | copy-start | bytes 1769476
  124.9 16.4 %copy-start.4 = (bf16[1,384,384]{2,1,0:T(8,128)(2,1)S(1)}, bf16[1,384,384]{2,1,0:T(8,128)(2,1)}, u32[]{:S(2)}) copy-start(bf16[1,384,384]{2,1,0:T(8,128)(2,1)} %mout_ref.1) | copy-start | bytes 884740
  125.1 16.3 %collective-permute-start.36 = (bf16[192,1152]{1,0:T(8,128)(2,1)S(1)}, bf16[192,1152]{1,0:T(8,128)(2,1)S(1)}, u32[]{:S(2)}, u32[]{:S(2)}) collective-permute-start(bf16[192,1152]{1,0:T(8,128)(2,1)S(1)} %add_convert_fusion), channel_id=1, source_target_pairs={{0,16},{8,24},{16,0},{24,8},{1,17},{9,25},{17,1},{25,9},{2,18},{10... | collective-permute-start | bytes 1327112 | tf_op jit(solution)/shard_map/ppermute | solution.py:292
  126.9 14.5 %collective-permute-start.32 = (bf16[192,1152]{1,0:T(8,128)(2,1)S(1)}, bf16[192,1152]{1,0:T(8,128)(2,1)S(1)}, u32[]{:S(2)}, u32[]{:S(2)}) collective-permute-start(bf16[192,1152]{1,0:T(8,128)(2,1)S(1)} %add_convert_fusion.1), channel_id=1, source_target_pairs={{0,8},{8,0},{16,24},{24,16},{1,9},{9,1},{17,25},{25,17},{2,10},{10... | collective-permute-start | bytes 1327112 | tf_op jit(solution)/shard_map/ppermute | solution.py:292
  130.3 13.2 %collective-permute-start.19 = (bf16[136,1536]{1,0:T(8,128)(2,1)S(1)}, bf16[136,1536]{1,0:T(8,128)(2,1)S(1)}, u32[]{:S(2)}, u32[]{:S(2)}) collective-permute-start(bf16[136,1536]{1,0:T(8,128)(2,1)S(1)} %get-tuple-element.84), channel_id=1, source_target_pairs={{0,2},{1,3},{2,0},{3,1},{4,6},{5,7},{6,4},{7,5},{8,10},{9,11},{10,... | collective-permute-start | bytes 1253384 | tf_op jit(solution)/shard_map/ppermute | solution.py:296
  133.8 27.1 %collective-permute-start.20 = (bf16[136,1536]{1,0:T(8,128)(2,1)S(1)}, bf16[136,1536]{1,0:T(8,128)(2,1)S(1)}, u32[]{:S(2)}, u32[]{:S(2)}) collective-permute-start(bf16[136,1536]{1,0:T(8,128)(2,1)S(1)} %get-tuple-element.85), channel_id=1, source_target_pairs={{0,4},{1,5},{2,6},{3,7},{4,0},{5,1},{6,2},{7,3},{8,12},{9,13},{10,... | collective-permute-start | bytes 1253384 | tf_op jit(solution)/shard_map/ppermute | solution.py:296
  138.5 22.5 %copy-start.9 = (s32[128,4]{0,1:T(4,128)S(1)}, s32[128,4]{0,1:T(4,128)}, u32[]{:S(2)}) copy-start(s32[128,4]{0,1:T(4,128)} %param.9) | copy-start | bytes 6148
  (27 other events, 23.0 us)

commit v5 on v4

--- a/solution.py
+++ b/solution.py
@@ -1,5 +1,3 @@
-import functools
-
 import jax
 import jax.numpy as jnp
 from jax import lax
@@ -71,11 +69,6 @@
 def unstack(ref, width):
     tok = 128
     return jnp.concatenate([ref[j * tok : (j + 1) * tok, :] for j in range(width // 128)], axis=1)
-
-
-def is_end(expert, chips):
-    chip = lax.shift_right_logical(expert, 1)
-    return (chip == 0) | (chip == chips - 1)
 
 
 def gate_column(table, expert):
@@ -180,59 +173,36 @@
     acc_out_ref[...] = dot(chs[...], ys[...], 0, 0)
 
 
-def forward_kernel(chips, ids_ref, e0, e1, m0, m1, win, xs, silu_ref, slope_ref, hidden_ref):
-    tok = e0.shape[0]
-    at_end = is_end(ids_ref[1], chips)
-
-    @pl.when(at_end)
-    def _():
-        xs[0:tok, :] = e0[...]
-        xs[tok:, :] = e1[...]
-
-    @pl.when(jnp.logical_not(at_end))
-    def _():
-        xs[0:tok, :] = m0[...]
-        xs[tok:, :] = m1[...]
-
+def forward_kernel(x0, x1, win, xs, silu_ref, slope_ref, hidden_ref):
+    tok = x0.shape[0]
+    xs[0:tok, :] = x0[...]
+    xs[tok:, :] = x1[...]
     silu_ref[...], slope_ref[...], hidden_ref[...] = activations(dot(xs[...], win[...], 1, 0))
 
 
-def shard_grads(refs, acc_in_ref, acc_out_ref, xs, ys, dgus, chs, index, half):
-    shard = 2 * half
+def shard_grads(refs, acc_in_ref, acc_out_ref, xs, ys, dgus, chs, index):
+    shard = sum(ref.shape[0] for ref in refs)
     at = pl.multiple_of(index * shard, 128)
     part_in = acc_in_ref[pl.ds(at, shard), :] + dot(xs[:, pl.ds(at, shard)], dgus[...], 0, 0)
     part_out = acc_out_ref[:, pl.ds(at, shard)] + dot(chs[...], ys[:, pl.ds(at, shard)], 0, 0)
     cols = part_in.shape[1]
-    for n, ref in enumerate(refs):
-        rows = slice(n * ref.shape[0], (n + 1) * ref.shape[0])
+    at = 0
+    for ref in refs:
+        rows = slice(at, at + ref.shape[0])
         ref[:, 0:cols] = part_in[rows].astype(bf16)
         ref[:, cols:] = part_out[rows].astype(bf16)
-
-
-def grad_kernel(chips, ids_ref, e0, e1, m0, m1, xs, silu, slope, hidden, wout, acc_in, acc_out, *refs):
+        at = rows.stop
+
+
+def grad_kernel(ids_ref, y0, y1, xs, silu, slope, hidden, wout, acc_in, acc_out, *refs):
     r3a_ref, r3b_ref, dgus, chs, ys, tab_ref = refs
-    tok = ys.shape[0] // 2
     rep, expert = ids_ref[0], ids_ref[1]
-    at_end = is_end(ids_ref[1], chips)
+    tok, width = ys.shape[0] // 2, ys.shape[1]
     ffn, experts = wout.shape[0], tab_ref.shape[1]
-
-    width = ys.shape[1]
-
-    @pl.when(at_end)
-    def _():
-        ys[0:tok, :] = unstack(e0, width)
-        ys[tok:, :] = unstack(e1, width)
-
-    @pl.when(jnp.logical_not(at_end))
-    def _():
-        ys[0:tok, :] = unstack(m0, width)
-        ys[tok:, :] = unstack(m1, width)
-
-    columns, first = [], width // 128 * tok
-    for end, mid in ((e0, m0), (e1, m1)):
-        table = jnp.where(at_end, end[first:, :].astype(f32), mid[first:, :].astype(f32))
-        columns.append(gate_column(table, expert))
-    gate = jnp.concatenate(columns, axis=0)
+    ys[0:tok, :] = unstack(y0, width)
+    ys[tok:, :] = unstack(y1, width)
+    first = width // 128 * tok
+    gate = jnp.concatenate([gate_column(ref[first:, :], expert) for ref in (y0, y1)], axis=0)
     back = dot(ys[...], wout[...], 1, 1)
     gate_grad = jnp.sum(hidden[...].astype(f32) * back, axis=1, keepdims=True)
     chs[...] = (hidden[...].astype(f32) * gate).astype(bf16)
@@ -241,16 +211,15 @@
     dgus[:, ffn:] = (dh * silu[...]).astype(bf16)
     for i in range(2):
         tab_ref[i] = gate_table(gate_grad[i * tok : (i + 1) * tok], experts, expert)
-    half = r3a_ref.shape[0]
-    shard_grads((r3a_ref, r3b_ref), acc_in, acc_out, xs, ys, dgus, chs, rep ^ 3, half)
+    shard_grads((r3a_ref, r3b_ref), acc_in, acc_out, xs, ys, dgus, chs, rep ^ 3)
 
 
 def other_grads_kernel(ids_ref, xs, ys, dgus, chs, acc_in, acc_out, mine_ref, r1a_ref, r1b_ref, r2a_ref, r2b_ref):
-    rep, half = ids_ref[0], r1a_ref.shape[0]
+    rep = ids_ref[0]
     args = (acc_in, acc_out, xs, ys, dgus, chs)
-    shard_grads((r1a_ref, r1b_ref), *args, rep ^ 1, half)
-    shard_grads((r2a_ref, r2b_ref), *args, rep ^ 2, half)
-    shard_grads((mine_ref,), *args, rep, half)
+    shard_grads((r1a_ref, r1b_ref), *args, rep ^ 1)
+    shard_grads((r2a_ref, r2b_ref), *args, rep ^ 2)
+    shard_grads((mine_ref,), *args, rep)
 
 
 def rows_kernel(dgus, win, tab_ref, keep_ref, give_ref):
@@ -260,16 +229,20 @@
         write_rows(out, row_grad[i * tok : (i + 1) * tok], tab_ref[i])
 
 
-def finish_kernel(own_ref, t1a_ref, t1b_ref, t2a_ref, t2b_ref, min_ref, mout_ref, nin_ref, nout_ref):
-    half = t1a_ref.shape[0]
-    cols = min_ref.shape[2]
-    for lo, one, two in ((0, t1a_ref, t2a_ref), (half, t1b_ref, t2b_ref)):
-        rows = slice(lo, lo + half)
-        total = own_ref[rows, :].astype(f32) + one[...].astype(f32) + two[...].astype(f32)
-        old_in = momentum_decay * min_ref[0, rows, :].astype(f32)
-        old_out = momentum_decay * mout_ref[0, rows, :].astype(f32)
-        nin_ref[0, rows, :] = (old_in + total[:, :cols]).astype(bf16)
-        nout_ref[0, rows, :] = (old_out + total[:, cols:]).astype(bf16)
+def mix_kernel(own_ref, t1b_ref, t2a_ref, min_ref, mout_ref, base_ref):
+    cut, cols = t2a_ref.shape[0], min_ref.shape[2]
+    for rows, part in ((slice(0, cut), t2a_ref), (slice(cut, own_ref.shape[0]), t1b_ref)):
+        total = own_ref[rows, :].astype(f32) + part[...].astype(f32)
+        base_ref[rows, 0:cols] = total[:, :cols] + momentum_decay * min_ref[0, rows, :].astype(f32)
+        base_ref[rows, cols:] = total[:, cols:] + momentum_decay * mout_ref[0, rows, :].astype(f32)
+
+
+def finish_kernel(base_ref, t1a_ref, t2b_ref, nin_ref, nout_ref):
+    cut, cols = t1a_ref.shape[0], nin_ref.shape[2]
+    for rows, part in ((slice(0, cut), t1a_ref), (slice(cut, base_ref.shape[0]), t2b_ref)):
+        total = (base_ref[rows, :] + part[...].astype(f32)).astype(bf16)
+        nin_ref[0, rows, :] = total[:, :cols]
+        nout_ref[0, rows, :] = total[:, cols:]
 
 
 def per_device_dense(*args):
@@ -280,7 +253,6 @@
     tok, width = tokens.shape
     ffn, both_w = w_out.shape[1], w_in.shape[2]
     shard = w_in.shape[1]
-    half = shard // 2
     cols = both_w + shard
     experts = lax.axis_size("expert")
     chips = experts // 2
@@ -351,8 +323,6 @@
     ends_y = over_chips(far_y, to_ends)
     far_yp = partner(far_y)
     near_yp = partner(near_y)
-    middle_xp = partner(middle_x)
-    ends_xp = partner(ends_x)
     got = partner(give_own)
     home_own = (keep.astype(f32) + got.astype(f32)).astype(bf16)
     more_xs, *early = call(
@@ -381,22 +351,25 @@
     )
     got = partner(give)
     home_near, home_far = ((keep[i].astype(f32) + got[i].astype(f32)).astype(bf16) for i in range(2))
+    cross_x = ends_x + middle_x
+    cross_xp = partner(cross_x)
     xs, silu, slope, hidden = call(
-        functools.partial(forward_kernel, chips),
-        [ids, ends_x, ends_xp, middle_x, middle_xp, win],
+        forward_kernel,
+        [cross_x, cross_xp, win],
         [((rows, width), bf16), ((rows, ffn), f32), ((rows, ffn), f32), ((rows, ffn), bf16)],
-        scalars=1,
         flops=2 * rows * width * both_w,
     )
-    middle_yp = partner(middle_y)
-    ends_yp = partner(ends_y)
+    cross_y = ends_y + middle_y
+    cross_yp = partner(cross_y)
     home_near = over_chips(home_near, to_near)
     home_far = over_chips(home_far, to_far)
+    part_a = shard * 13 // 24 // 16 * 16
+    part_b = shard - part_a
     r3a, r3b, dgus, chs, ys, table = call(
-        functools.partial(grad_kernel, chips),
-        [ids, ends_y, ends_yp, middle_y, middle_yp, xs, silu, slope, hidden, wout]
+        grad_kernel,
+        [ids, cross_y, cross_yp, xs, silu, slope, hidden, wout]
         + [acc_in, acc_out],
-        [((half, cols), bf16)] * 2
+        [((part_a, cols), bf16), ((part_b, cols), bf16)]
         + [((rows, both_w), bf16), ((rows, ffn), bf16), ((rows, width), bf16), ((2, experts, tok), f32)],
         mib=8,
         scalars=1,
@@ -407,7 +380,7 @@
     mine, r1a, r1b, r2a, r2b = call(
         other_grads_kernel,
         [ids, xs, ys, dgus, chs, acc_in, acc_out],
-        [((shard, cols), bf16)] + [((half, cols), bf16)] * 4,
+        [((shard, cols), bf16)] + [((part_a, cols), bf16), ((part_b, cols), bf16)] * 2,
         mib=8,
         scalars=1,
         flops=2 * rows * width * both_w,
@@ -425,10 +398,9 @@
     table = sum(p[tok:, :tok].astype(f32) for p in parts)
     picked = routes.T[:, None, :] == jnp.arange(experts, dtype=jnp.int32)[None, :, None]
     gate_grad = jnp.sum(jnp.where(picked, table[None], 0.0), axis=1).astype(bf16).T
+    (base,) = call(mix_kernel, [mine, t1b, t2a, momentum_in, momentum_out], [((shard, cols), f32)])
     new_in, new_out = call(
-        finish_kernel,
-        [mine, t1a, t1b, t2a, t2b, momentum_in, momentum_out],
-        [(momentum_in.shape, bf16), (momentum_out.shape, bf16)],
+        finish_kernel, [base, t1a, t2b], [(momentum_in.shape, bf16), (momentum_out.shape, bf16)]
     )
     return token_grad, gate_grad, new_in, new_out
 

time: 163 us -> 164 us (level)
  local copies, waits for them, and re-layouts: 24.1 us -> 11.5 us
  starting transfers between devices: 36.9 us -> 47.7 us
  other arithmetic: 2.23 us -> 4.8 us
  Pallas kernels: 22.5 us -> 20.2 us
  waiting for transfers between devices: 75.8 us -> 78 us
    unnamed x76 -> x52, local copies, waits for them, and re-layouts: 24 us -> 10.7 us
    ppermute x11, starting transfers between devices: 20.3 us -> 32.5 us  [over_chips(): return lax.ppermute(value, 'expert', pairs)]
    ppermute x11, waiting for transfers between devices: 42.2 us -> 52.7 us  [over_chips(): return lax.ppermute(value, 'expert', pairs)]
    ppermute x13, waiting for transfers between devices: 33.5 us -> 23.7 us  [over_rep(): return lax.ppermute(value, 'rep', [(i, i ^ bits) for i in range(4)])]
    add x0 -> x2, other arithmetic: none -> 2.56 us  [the longest x1 1.34 us: dense_step(): cross_x = ends_x + middle_x]
    pallas_call x10 -> x11, Pallas kernels: 22.5 us -> 20.2 us  [call(): pl.pallas_call(kernel, out_shape=[jax.ShapeDtypeStruct(shape, dtype) for...]
    ppermute x13 -> x11, waiting for transfers between devices: 0.03 us -> 1.67 us  [partner(): return lax.ppermute(value, 'expert', [(i, i ^ 1) for i in range(experts)])]
  transfers between devices with their start and end apart: 37 -> 35, of which waited for: 13 -> 14; matrix products, arithmetic and copies ran while one was open for 0% -> 2% of each run, Pallas kernels for 12% -> 11%
where the time goes in v5:
time: 164 us; the launch traced here: 163 us
  waiting for transfers between devices  78 us (48%)
  starting transfers between devices  47.7 us (29%)
  Pallas kernels  20.2 us (12%)
  local copies, waits for them, and re-layouts  11.5 us (7%)
  other arithmetic  4.8 us (3%)
    ppermute x11, waiting for transfers between devices, over_chips(): return lax.ppermute(value, 'expert', pairs)  52.7 us
    ppermute x11, starting transfers between devices, over_chips(): return lax.ppermute(value, 'expert', pairs)  32.5 us
    ppermute x13, waiting for transfers between devices, over_rep(): return lax.ppermute(value, 'rep', [(i, i ^ bits) for i in range(4)])  23.7 us
    pallas_call x11, Pallas kernels, call(): pl.pallas_call(kernel, out_shape=[jax.ShapeDtypeStruct(shape, dtype) for...  20.2 us
    ppermute x13, starting transfers between devices, over_rep(): return lax.ppermute(value, 'rep', [(i, i ^ bits) for i in range(4)])  13.4 us
    unnamed x52, local copies, waits for them, and re-layouts  10.7 us
  transfers between devices with their start and end apart: 35, of which 14 were waited for; matrix products, arithmetic and copies ran while one was open for 2% of the time, Pallas kernels for 11%

profile of v5, /device:TPU:0, one launch (start us, length us, event | category | flops | bytes accessed | tf_op | source)
XLA Modules:
  0.0 163.2 jit_solution(481173397308618865)
XLA Ops:
  0.6 3.1 %collective-permute-start.7 = (bf16[1,384,384]{2,1,0:T(8,128)(2,1)}, bf16[1,384,384]{2,1,0:T(8,128)(2,1)S(1)}, u32[]{:S(2)}, u32[]{:S(2)}) collective-permute-start(bf16[1,384,384]{2,1,0:T(8,128)(2,1)} %wout_hbm.1), channel_id=1, source_target_pairs={{0,16},{8,24},{16,0},{24,8},{1,17},{9,25},{17,1},{25,9},{2,18},{10... | collective-permute-start | bytes 884744 | tf_op jit(solution)/shard_map/ppermute | solution.py:264
  3.7 1.0 copy-done.1
  4.7 1.0 copy-done.2
  5.7 1.0 copy-done.4
  8.0 1.5 shard_map.111
  10.2 0.8 copy-done.12
  11.0 1.5 collective-permute-start.6
  12.5 2.6 %collective-permute-start.16 = (bf16[128,1536]{1,0:T(8,128)(2,1)S(1)}, bf16[128,1536]{1,0:T(8,128)(2,1)}, u32[]{:S(2)}, u32[]{:S(2)}) collective-permute-start(bf16[128,1536]{1,0:T(8,128)(2,1)S(1)} %copy-done.2), channel_id=1, source_target_pairs={{0,4},{1,5},{2,6},{3,7},{4,0},{5,1},{6,2},{7,3},{8,12},{9,13},{10,... | collective-permute-start | bytes 1179656 | tf_op jit(solution)/shard_map/ppermute | solution.py:268
  15.1 1.6 collective-permute-start.14
  17.3 3.0 %collective-permute-done.6.refs_6_ = bf16[1,384,384]{2,1,0:T(8,128)(2,1)S(1)} collective-permute-done((bf16[1,384,384]{2,1,0:T(8,128)(2,1)S(1)}, bf16[1,384,384]{2,1,0:T(8,128)(2,1)S(1)}, u32[]{:S(2)}, u32[]{:S(2)}) %collective-permute-start.6) | collective-permute-done | bytes 294944 | tf_op jit(solution)/shard_map/ppermute | solution.py:264
  21.1 0.8 copy-done.14
  21.9 1.5 collective-permute-start.2
  23.4 10.6 %collective-permute-done.16.f0 = bf16[128,1536]{1,0:T(8,128)(2,1)} collective-permute-done((bf16[128,1536]{1,0:T(8,128)(2,1)S(1)}, bf16[128,1536]{1,0:T(8,128)(2,1)}, u32[]{:S(2)}, u32[]{:S(2)}) %collective-permute-start.16) | collective-permute-done | bytes 393248 | tf_op jit(solution)/shard_map/ppermute | solution.py:268
  34.8 16.5 %collective-permute-start.10 = (bf16[1544,128]{1,0:T(8,128)(2,1)S(1)}, bf16[1544,128]{1,0:T(8,128)(2,1)S(1)}, u32[]{:S(2)}, u32[]{:S(2)}) collective-permute-start(bf16[1544,128]{1,0:T(8,128)(2,1)S(1)} %get-tuple-element.45.y0), channel_id=1, source_target_pairs={{0,2},{1,3},{2,0},{3,1},{4,6},{5,7},{6,4},{7,5},{8,10},{9,11},{10,... | collective-permute-start | bytes 1185800 | tf_op jit(solution)/shard_map/ppermute | solution.py:268
  52.0 7.3 %collective-permute-done.12.refs_2_ = bf16[1544,128]{1,0:T(8,128)(2,1)S(1)} collective-permute-done((bf16[1544,128]{1,0:T(8,128)(2,1)S(1)}, bf16[1544,128]{1,0:T(8,128)(2,1)S(1)}, u32[]{:S(2)}, u32[]{:S(2)}) %collective-permute-start.12) | collective-permute-done | bytes 395296 | tf_op jit(solution)/shard_map/ppermute | solution.py:268
  59.8 0.7 copy-done.16
  60.5 6.4 %collective-permute-done.10.refs_0_ = bf16[1544,128]{1,0:T(8,128)(2,1)S(1)} collective-permute-done((bf16[1544,128]{1,0:T(8,128)(2,1)S(1)}, bf16[1544,128]{1,0:T(8,128)(2,1)S(1)}, u32[]{:S(2)}, u32[]{:S(2)}) %collective-permute-start.10) | collective-permute-done | bytes 395296 | tf_op jit(solution)/shard_map/ppermute | solution.py:268
  66.9 1.3 collective-permute-start.21
  68.2 1.3 collective-permute-start.24
  69.5 0.8 slice.56
  72.1 4.3 %collective-permute-done.5.refs_4_ = bf16[1,96,768]{2,1,0:T(8,128)(2,1)S(1)} collective-permute-done((bf16[1,96,768]{2,1,0:T(8,128)(2,1)S(1)}, bf16[1,96,768]{2,1,0:T(8,128)(2,1)S(1)}, u32[]{:S(2)}, u32[]{:S(2)}) %collective-permute-start.5) | collective-permute-done | bytes 147488 | tf_op jit(solution)/shard_map/ppermute | solution.py:264
  76.4 12.0 %collective-permute-done.24 = bf16[128,1536]{1,0:T(8,128)(2,1)} collective-permute-done((bf16[128,1536]{1,0:T(8,128)(2,1)}, bf16[128,1536]{1,0:T(8,128)(2,1)}, u32[]{:S(2)}, u32[]{:S(2)}) %collective-permute-start.24) | collective-permute-done | bytes 393248 | tf_op jit(solution)/shard_map/ppermute | solution.py:268
  89.1 1.3 add.50.x0
  90.5 1.2 add.49.y0
  91.8 1.0 copy-done.21
  92.8 1.0 copy-done.23
  93.8 3.5 %shard_map.112 = (bf16[136,1536]{1,0:T(8,128)(2,1)S(1)}, bf16[136,1536]{1,0:T(8,128)(2,1)S(1)}, bf16[256,768]{1,0:T(8,128)(2,1)S(1)}, bf16[256,384]{1,0:T(8,128)...) custom-call(s32[2]{0:T(128)S(1)} %pad_add_fusion.ids_ref, bf16[128,1536]{1,0:T(8,128)(2,1)S(1)} %copy-done.13, ...), custom_call_target="tpu_custom_call" | custom-call | flops 1509949440 | bytes 4194304 | tf_op jit(solution)/shard_map/pallas_call | solution.py:23
  97.8 2.9 %shard_map.113 = (bf16[512,1536]{1,0:T(8,128)(2,1)S(1)}, f32[512,384]{1,0:T(8,128)S(1)}, f32[512,384]{1,0:T(8,128)S(1)}, bf16[512,384]{1,0:T(8,128)(2,1)S(1)}) custom-call(bf16[128,1536]{1,0:T(8,128)(2,1)} %collective-permute-done.14.n0, bf16[128,1536]{1,0:T(8,128)(2,1)} %collective-permute-done.15.n1, bf16[128,1536]{1,0:T(8,128)(2,1)} %collective-permute-done.16.f0, ...), custom_call_target="tpu_custom_call" | custom-call | flops 1207959552 | bytes 4194304 | tf_op jit(solution)/shard_map/pallas_call | solution.py:23
  100.7 3.1 %shard_map.114 = (bf16[2,136,1536]{2,1,0:T(8,128)(2,1)S(1)}, bf16[2,136,1536]{2,1,0:T(8,128)(2,1)S(1)}, bf16[512,1536]{1,0:T(8,128)(2,1)S(1)}, bf16[512,768]{1,0:T(8,128)(2,1)S(1)}, bf16[512,384]{1,0:T(8,128)(2,1)S(1)}) custom-call(s32[2]{0:T(128)S(1)} %pad_add_fusion.ids_ref, bf16[1544,128]{1,0:T(8,128)(2,1)S(1)} %collective-permute-done.10.refs_0_, ...), custom_call_target="tpu_custom_call" | custom-call | flops 1509949440 | bytes 4194304 | tf_op jit(solution)/shard_map/pallas_call | solution.py:23
  103.8 3.0 %shard_map.116 = (f32[1536,768]{1,0:T(8,128)S(1)}, f32[384,1536]{1,0:T(8,128)S(1)}) custom-call(bf16[128,1536]{1,0:T(8,128)(2,1)S(1)} %copy-done.13, bf16[128,1536]{1,0:T(8,128)(2,1)S(1)} %copy-done.15, bf16[1544,128]{1,0:T(8,128)(2,1)S(1)} %copy-done.9, bf16[1544,128]{1,0:T(8,128)(2,1)S(1)} %copy-done.11, bf16[256,768]{1,0:T(8,128)(2,1)S(1)} %get-tuple-element.61.own_dgu, ...), custom_call_target="tpu_custom_call" | custom-call | flops 3019898880 | bytes 4194304 | tf_op jit(solution)/shard_map/pallas_call | solution.py:23
  106.8 0.9 shard_map.115
  107.7 1.6 shard_map.117
  110.9 1.6 shard_map.119
  112.5 1.6 collective-permute-start.30
  114.1 0.8 shard_map.118
  114.9 5.8 %collective-permute-done.33 = bf16[176,1152]{1,0:T(8,128)(2,1)S(1)} collective-permute-done((bf16[176,1152]{1,0:T(8,128)(2,1)S(1)}, bf16[176,1152]{1,0:T(8,128)(2,1)S(1)}, u32[]{:S(2)}, u32[]{:S(2)}) %collective-permute-start.33) | collective-permute-done | bytes 405536 | tf_op jit(solution)/shard_map/ppermute | solution.py:264
  120.8 1.6 %collective-permute-done.27 = bf16[136,1536]{1,0:T(8,128)(2,1)S(1)} collective-permute-done((bf16[136,1536]{1,0:T(8,128)(2,1)S(1)}, bf16[136,1536]{1,0:T(8,128)(2,1)S(1)}, u32[]{:S(2)}, u32[]{:S(2)}) %collective-permute-start.27) | collective-permute-done | bytes 417824 | tf_op jit(solution)/shard_map/ppermute | solution.py:271
  123.1 1.1 collective-permute-done.31
  124.8 3.6 %collective-permute-start.28 = (bf16[136,1536]{1,0:T(8,128)(2,1)S(1)}, bf16[136,1536]{1,0:T(8,128)(2,1)S(1)}, u32[]{:S(2)}, u32[]{:S(2)}) collective-permute-start(bf16[136,1536]{1,0:T(8,128)(2,1)S(1)} %add_convert_fusion.1), channel_id=1, source_target_pairs={{0,6},{1,7},{2,4},{3,5},{4,2},{5,3},{6,0},{7,1},{8,14},{9,15},{10,... | collective-permute-start | bytes 1253384 | tf_op jit(solution)/shard_map/ppermute | solution.py:268
  128.6 1.6 collective-permute-start.32
  130.2 4.5 %collective-permute-done.29.t1b_ref = bf16[176,1152]{1,0:T(8,128)(2,1)S(1)} collective-permute-done((bf16[176,1152]{1,0:T(8,128)(2,1)S(1)}, bf16[176,1152]{1,0:T(8,128)(2,1)S(1)}, u32[]{:S(2)}, u32[]{:S(2)}) %collective-permute-start.29) | collective-permute-done | bytes 405536 | tf_op jit(solution)/shard_map/ppermute | solution.py:264
  134.7 4.0 %collective-permute-start.20 = (bf16[136,1536]{1,0:T(8,128)(2,1)S(1)}, bf16[136,1536]{1,0:T(8,128)(2,1)S(1)}, u32[]{:S(2)}, u32[]{:S(2)}) collective-permute-start(bf16[136,1536]{1,0:T(8,128)(2,1)S(1)} %get-tuple-element.85), channel_id=1, source_target_pairs={{0,4},{1,5},{2,6},{3,7},{4,0},{5,1},{6,2},{7,3},{8,12},{9,13},{10,... | collective-permute-start | bytes 1253384 | tf_op jit(solution)/shard_map/ppermute | solution.py:268
  139.2 3.0 %collective-permute-done.34.t2b_ref = bf16[176,1152]{1,0:T(8,128)(2,1)S(1)} collective-permute-done((bf16[176,1152]{1,0:T(8,128)(2,1)S(1)}, bf16[176,1152]{1,0:T(8,128)(2,1)S(1)}, u32[]{:S(2)}, u32[]{:S(2)}) %collective-permute-start.34) | collective-permute-done | bytes 405536 | tf_op jit(solution)/shard_map/ppermute | solution.py:264
  142.2 1.9 %collective-permute-done.32.t1a_ref = bf16[208,1152]{1,0:T(8,128)(2,1)S(1)} collective-permute-done((bf16[208,1152]{1,0:T(8,128)(2,1)S(1)}, bf16[208,1152]{1,0:T(8,128)(2,1)S(1)}, u32[]{:S(2)}, u32[]{:S(2)}) %collective-permute-start.32) | collective-permute-done | bytes 479264 | tf_op jit(solution)/shard_map/ppermute | solution.py:264
  144.1 1.1 shard_map.121
  145.2 3.1 %collective-permute-done.19 = bf16[136,1536]{1,0:T(8,128)(2,1)S(1)} collective-permute-done((bf16[136,1536]{1,0:T(8,128)(2,1)S(1)}, bf16[136,1536]{1,0:T(8,128)(2,1)S(1)}, u32[]{:S(2)}, u32[]{:S(2)}) %collective-permute-start.19) | collective-permute-done | bytes 417824 | tf_op jit(solution)/shard_map/ppermute | solution.py:268
  148.3 13.4 %collective-permute-done.20 = bf16[136,1536]{1,0:T(8,128)(2,1)S(1)} collective-permute-done((bf16[136,1536]{1,0:T(8,128)(2,1)S(1)}, bf16[136,1536]{1,0:T(8,128)(2,1)S(1)}, u32[]{:S(2)}, u32[]{:S(2)}) %collective-permute-start.20) | collective-permute-done | bytes 417824 | tf_op jit(solution)/shard_map/ppermute | solution.py:268
  162.3 1.0 add_convert_fusion.6
  (98 shorter events, 12.8 us)
Async XLA Ops:
  0.6 16.0 %collective-permute-start.7 = (bf16[1,384,384]{2,1,0:T(8,128)(2,1)}, bf16[1,384,384]{2,1,0:T(8,128)(2,1)S(1)}, u32[]{:S(2)}, u32[]{:S(2)}) collective-permute-start(bf16[1,384,384]{2,1,0:T(8,128)(2,1)} %wout_hbm.1), channel_id=1, source_target_pairs={{0,16},{8,24},{16,0},{24,8},{1,17},{9,25},{17,1},{25,9},{2,18},{10... | collective-permute-start | bytes 884744 | tf_op jit(solution)/shard_map/ppermute | solution.py:264
  10.2 66.2 %copy-start.8 = (bf16[1544,128]{1,0:T(8,128)(2,1)}, bf16[1544,128]{1,0:T(8,128)(2,1)S(1)}, u32[]{:S(2)}) copy-start(bf16[1544,128]{1,0:T(8,128)(2,1)S(1)} %get-tuple-element.45.y0) | copy-start | bytes 1185796
  10.2 10.9 %collective-permute-start = (bf16[128,1536]{1,0:T(8,128)(2,1)S(1)}, bf16[128,1536]{1,0:T(8,128)(2,1)S(1)}, u32[]{:S(2)}, u32[]{:S(2)}) collective-permute-start(bf16[128,1536]{1,0:T(8,128)(2,1)S(1)} %get-tuple-element.44.x0), channel_id=1, source_target_pairs={{0,1},{1,0},{2,3},{3,2},{4,5},{5,4},{6,7},{7,6},{8,9},{9,8},{10,11... | collective-permute-start | bytes 1179656 | tf_op jit(solution)/shard_map/ppermute | solution.py:271
  11.0 9.4 %collective-permute-start.6 = (bf16[1,384,384]{2,1,0:T(8,128)(2,1)S(1)}, bf16[1,384,384]{2,1,0:T(8,128)(2,1)S(1)}, u32[]{:S(2)}, u32[]{:S(2)}) collective-permute-start(bf16[1,384,384]{2,1,0:T(8,128)(2,1)S(1)} %copy-done.4), channel_id=1, source_target_pairs={{0,8},{8,0},{16,24},{24,16},{1,9},{9,1},{17,25},{25,17},{2,10},{10... | collective-permute-start | bytes 884744 | tf_op jit(solution)/shard_map/ppermute | solution.py:264
  12.5 21.5 %collective-permute-start.16 = (bf16[128,1536]{1,0:T(8,128)(2,1)S(1)}, bf16[128,1536]{1,0:T(8,128)(2,1)}, u32[]{:S(2)}, u32[]{:S(2)}) collective-permute-start(bf16[128,1536]{1,0:T(8,128)(2,1)S(1)} %copy-done.2), channel_id=1, source_target_pairs={{0,4},{1,5},{2,6},{3,7},{4,0},{5,1},{6,2},{7,3},{8,12},{9,13},{10,... | collective-permute-start | bytes 1179656 | tf_op jit(solution)/shard_map/ppermute | solution.py:268
  15.1 19.4 %collective-permute-start.14 = (bf16[128,1536]{1,0:T(8,128)(2,1)S(1)}, bf16[128,1536]{1,0:T(8,128)(2,1)}, u32[]{:S(2)}, u32[]{:S(2)}) collective-permute-start(bf16[128,1536]{1,0:T(8,128)(2,1)S(1)} %copy-done.2), channel_id=1, source_target_pairs={{0,2},{1,3},{2,0},{3,1},{4,6},{5,7},{6,4},{7,5},{8,10},{9,11},{10,... | collective-permute-start | bytes 1179656 | tf_op jit(solution)/shard_map/ppermute | solution.py:268
  16.7 18.1 %collective-permute-start.25 = (bf16[128,1536]{1,0:T(8,128)(2,1)S(1)}, bf16[128,1536]{1,0:T(8,128)(2,1)S(1)}, u32[]{:S(2)}, u32[]{:S(2)}) collective-permute-start(bf16[128,1536]{1,0:T(8,128)(2,1)S(1)} %copy-done.2), channel_id=1, source_target_pairs={{2,4},{3,5},{4,2},{5,3},{10,12},{11,13},{12,10},{13,11},{18,20},{1... | collective-permute-start | bytes 1179656 | tf_op jit(solution)/shard_map/ppermute | solution.py:268
  21.1 30.2 %collective-permute-start.1 = (bf16[1544,128]{1,0:T(8,128)(2,1)S(1)}, bf16[1544,128]{1,0:T(8,128)(2,1)S(1)}, u32[]{:S(2)}, u32[]{:S(2)}) collective-permute-start(bf16[1544,128]{1,0:T(8,128)(2,1)S(1)} %get-tuple-element.45.y0), channel_id=1, source_target_pairs={{0,1},{1,0},{2,3},{3,2},{4,5},{5,4},{6,7},{7,6},{8,9},{9,8},{10,11... | collective-permute-start | bytes 1185800 | tf_op jit(solution)/shard_map/ppermute | solution.py:271
  21.9 46.3 %collective-permute-start.2 = (bf16[1,384,768]{2,1,0:T(8,128)(2,1)}, bf16[1,384,768]{2,1,0:T(8,128)(2,1)S(1)}, u32[]{:S(2)}, u32[]{:S(2)}) collective-permute-start(bf16[1,384,768]{2,1,0:T(8,128)(2,1)} %win_hbm.1), channel_id=1, source_target_pairs={{0,8},{8,0},{16,24},{24,16},{1,9},{9,1},{17,25},{25,17},{2,10},{10... | collective-permute-start | bytes 1769480 | tf_op jit(solution)/shard_map/ppermute | solution.py:264
  34.0 36.4 %collective-permute-start.3 = (bf16[1,384,768]{2,1,0:T(8,128)(2,1)}, bf16[1,384,768]{2,1,0:T(8,128)(2,1)S(1)}, u32[]{:S(2)}, u32[]{:S(2)}) collective-permute-start(bf16[1,384,768]{2,1,0:T(8,128)(2,1)} %win_hbm.1), channel_id=1, source_target_pairs={{0,16},{8,24},{16,0},{24,8},{1,17},{9,25},{17,1},{25,9},{2,18},{10... | collective-permute-start | bytes 1769480 | tf_op jit(solution)/shard_map/ppermute | solution.py:264
  34.5 24.8 %collective-permute-start.12 = (bf16[1544,128]{1,0:T(8,128)(2,1)S(1)}, bf16[1544,128]{1,0:T(8,128)(2,1)S(1)}, u32[]{:S(2)}, u32[]{:S(2)}) collective-permute-start(bf16[1544,128]{1,0:T(8,128)(2,1)S(1)} %get-tuple-element.45.y0), channel_id=1, source_target_pairs={{0,4},{1,5},{2,6},{3,7},{4,0},{5,1},{6,2},{7,3},{8,12},{9,13},{10,... | collective-permute-start | bytes 1185800 | tf_op jit(solution)/shard_map/ppermute | solution.py:268
  34.8 33.5 %copy-start.25 = (bf16[128,1536]{1,0:T(8,128)(2,1)}, bf16[128,1536]{1,0:T(8,128)(2,1)S(1)}, u32[]{:S(2)}) copy-start(bf16[128,1536]{1,0:T(8,128)(2,1)S(1)} %collective-permute-done.25) | copy-start | bytes 1179652
  34.8 32.1 %collective-permute-start.10 = (bf16[1544,128]{1,0:T(8,128)(2,1)S(1)}, bf16[1544,128]{1,0:T(8,128)(2,1)S(1)}, u32[]{:S(2)}, u32[]{:S(2)}) collective-permute-start(bf16[1544,128]{1,0:T(8,128)(2,1)S(1)} %get-tuple-element.45.y0), channel_id=1, source_target_pairs={{0,2},{1,3},{2,0},{3,1},{4,6},{5,7},{6,4},{7,5},{8,10},{9,11},{10,... | collective-permute-start | bytes 1185800 | tf_op jit(solution)/shard_map/ppermute | solution.py:268
  51.3 37.1 %copy-start.10 = (bf16[1544,128]{1,0:T(8,128)(2,1)}, bf16[1544,128]{1,0:T(8,128)(2,1)S(1)}, u32[]{:S(2)}) copy-start(bf16[1544,128]{1,0:T(8,128)(2,1)S(1)} %collective-permute-done.1.y1) | copy-start | bytes 1185796
  51.3 19.5 %collective-permute-start.22 = (bf16[1544,128]{1,0:T(8,128)(2,1)S(1)}, bf16[1544,128]{1,0:T(8,128)(2,1)S(1)}, u32[]{:S(2)}, u32[]{:S(2)}) collective-permute-start(bf16[1544,128]{1,0:T(8,128)(2,1)S(1)} %get-tuple-element.45.y0), channel_id=1, source_target_pairs={{2,4},{3,5},{4,2},{5,3},{10,12},{11,13},{12,10},{13,11},{18,20},{1... | collective-permute-start | bytes 1185800 | tf_op jit(solution)/shard_map/ppermute | solution.py:268
  59.3 12.2 %collective-permute-start.8 = (bf16[1,384,384]{2,1,0:T(8,128)(2,1)S(1)}, bf16[1,384,384]{2,1,0:T(8,128)(2,1)S(1)}, u32[]{:S(2)}, u32[]{:S(2)}) collective-permute-start(bf16[1,384,384]{2,1,0:T(8,128)(2,1)S(1)} %collective-permute-done.7.refs_7_), channel_id=1, source_target_pairs={{0,8},{8,0},{16,24},{24,16},{1,9},{9,1},{17,25},{25,17},{2,10},{10... | collective-permute-start | bytes 884744 | tf_op jit(solution)/shard_map/ppermute | solution.py:264
  66.9 21.5 %collective-permute-start.21 = (bf16[1544,128]{1,0:T(8,128)(2,1)S(1)}, bf16[1544,128]{1,0:T(8,128)(2,1)}, u32[]{:S(2)}, u32[]{:S(2)}) collective-permute-start(bf16[1544,128]{1,0:T(8,128)(2,1)S(1)} %collective-permute-done.12.refs_2_), channel_id=1, source_target_pairs={{4,6},{5,7},{2,0},{3,1},{12,14},{13,15},{10,8},{11,9},{20,22},{21,... | collective-permute-start | bytes 1185800 | tf_op jit(solution)/shard_map/ppermute | solution.py:268
  68.2 20.2 %collective-permute-start.24 = (bf16[128,1536]{1,0:T(8,128)(2,1)}, bf16[128,1536]{1,0:T(8,128)(2,1)}, u32[]{:S(2)}, u32[]{:S(2)}) collective-permute-start(bf16[128,1536]{1,0:T(8,128)(2,1)} %collective-permute-done.16.f0), channel_id=1, source_target_pairs={{4,6},{5,7},{2,0},{3,1},{12,14},{13,15},{10,8},{11,9},{20,22},{21,... | collective-permute-start | bytes 1179656 | tf_op jit(solution)/shard_map/ppermute | solution.py:268
  70.3 21.4 %collective-permute-start.4 = (bf16[1,288,768]{2,1,0:T(8,128)(2,1)}, bf16[1,288,768]{2,1,0:T(8,128)(2,1)}, u32[]{:S(2)}, u32[]{:S(2)}) collective-permute-start(bf16[1,288,768]{2,1,0:T(8,128)(2,1)} %slice.56), channel_id=1, source_target_pairs={{0,16},{8,24},{16,0},{24,8},{1,17},{9,25},{17,1},{25,9},{2,18},{10... | collective-permute-start | bytes 1327112 | tf_op jit(solution)/shard_map/ppermute | solution.py:264
  70.9 17.6 %copy-start.24 = (bf16[1544,128]{1,0:T(8,128)(2,1)}, bf16[1544,128]{1,0:T(8,128)(2,1)S(1)}, u32[]{:S(2)}) copy-start(bf16[1544,128]{1,0:T(8,128)(2,1)S(1)} %collective-permute-done.22) | copy-start | bytes 1185796
  70.9 5.6 %collective-permute-start.5 = (bf16[1,96,768]{2,1,0:T(8,128)(2,1)S(1)}, bf16[1,96,768]{2,1,0:T(8,128)(2,1)S(1)}, u32[]{:S(2)}, u32[]{:S(2)}) collective-permute-start(bf16[1,96,768]{2,1,0:T(8,128)(2,1)S(1)} %slice.57), channel_id=1, source_target_pairs={{0,8},{8,0},{16,24},{24,16},{1,9},{9,1},{17,25},{25,17},{2,10},{10... | collective-permute-start | bytes 442376 | tf_op jit(solution)/shard_map/ppermute | solution.py:264
  72.1 25.1 %collective-permute-start.17 = (bf16[128,1536]{1,0:T(8,128)(2,1)}, bf16[128,1536]{1,0:T(8,128)(2,1)}, u32[]{:S(2)}, u32[]{:S(2)}) collective-permute-start(bf16[128,1536]{1,0:T(8,128)(2,1)} %collective-permute-done.16.f0), channel_id=1, source_target_pairs={{0,1},{1,0},{2,3},{3,2},{4,5},{5,4},{6,7},{7,6},{8,9},{9,8},{10,11... | collective-permute-start | bytes 1179656 | tf_op jit(solution)/shard_map/ppermute | solution.py:271
  76.4 21.4 %collective-permute-start.15 = (bf16[128,1536]{1,0:T(8,128)(2,1)}, bf16[128,1536]{1,0:T(8,128)(2,1)}, u32[]{:S(2)}, u32[]{:S(2)}) collective-permute-start(bf16[128,1536]{1,0:T(8,128)(2,1)} %collective-permute-done.14.n0), channel_id=1, source_target_pairs={{0,1},{1,0},{2,3},{3,2},{4,5},{5,4},{6,7},{7,6},{8,9},{9,8},{10,11... | collective-permute-start | bytes 1179656 | tf_op jit(solution)/shard_map/ppermute | solution.py:271
  88.4 12.3 %collective-permute-start.13 = (bf16[1544,128]{1,0:T(8,128)(2,1)S(1)}, bf16[1544,128]{1,0:T(8,128)(2,1)S(1)}, u32[]{:S(2)}, u32[]{:S(2)}) collective-permute-start(bf16[1544,128]{1,0:T(8,128)(2,1)S(1)} %collective-permute-done.12.refs_2_), channel_id=1, source_target_pairs={{0,1},{1,0},{2,3},{3,2},{4,5},{5,4},{6,7},{7,6},{8,9},{9,8},{10,11... | collective-permute-start | bytes 1185800 | tf_op jit(solution)/shard_map/ppermute | solution.py:271
  88.4 12.3 %collective-permute-start.11 = (bf16[1544,128]{1,0:T(8,128)(2,1)S(1)}, bf16[1544,128]{1,0:T(8,128)(2,1)S(1)}, u32[]{:S(2)}, u32[]{:S(2)}) collective-permute-start(bf16[1544,128]{1,0:T(8,128)(2,1)S(1)} %collective-permute-done.10.refs_0_), channel_id=1, source_target_pairs={{0,1},{1,0},{2,3},{3,2},{4,5},{5,4},{6,7},{7,6},{8,9},{9,8},{10,11... | collective-permute-start | bytes 1185800 | tf_op jit(solution)/shard_map/ppermute | solution.py:271
  89.0 2.8 %copy-start.9 = (bf16[1544,128]{1,0:T(8,128)(2,1)S(1)}, bf16[1544,128]{1,0:T(8,128)(2,1)}, u32[]{:S(2)}) copy-start(bf16[1544,128]{1,0:T(8,128)(2,1)} %copy-done.8) | copy-start | bytes 1185796
  89.0 2.8 %copy-start.11 = (bf16[1544,128]{1,0:T(8,128)(2,1)S(1)}, bf16[1544,128]{1,0:T(8,128)(2,1)}, u32[]{:S(2)}) copy-start(bf16[1544,128]{1,0:T(8,128)(2,1)} %copy-done.10) | copy-start | bytes 1185796
  89.0 2.8 %copy-start.13 = (bf16[128,1536]{1,0:T(8,128)(2,1)S(1)}, bf16[128,1536]{1,0:T(8,128)(2,1)}, u32[]{:S(2)}) copy-start(bf16[128,1536]{1,0:T(8,128)(2,1)} %copy-done.12) | copy-start | bytes 1179652
  89.0 2.8 %copy-start.15 = (bf16[128,1536]{1,0:T(8,128)(2,1)S(1)}, bf16[128,1536]{1,0:T(8,128)(2,1)}, u32[]{:S(2)}) copy-start(bf16[128,1536]{1,0:T(8,128)(2,1)} %copy-done.14) | copy-start | bytes 1179652
  89.0 2.8 %copy-start.17 = (bf16[1,384,384]{2,1,0:T(8,128)(2,1)S(1)}, bf16[1,384,384]{2,1,0:T(8,128)(2,1)}, u32[]{:S(2)}) copy-start(bf16[1,384,384]{2,1,0:T(8,128)(2,1)} %copy-done.16) | copy-start | bytes 884740
  89.0 2.8 %copy-start.19 = (bf16[1,384,384]{2,1,0:T(8,128)(2,1)S(1)}, bf16[1,384,384]{2,1,0:T(8,128)(2,1)}, u32[]{:S(2)}) copy-start(bf16[1,384,384]{2,1,0:T(8,128)(2,1)} %copy-done.18) | copy-start | bytes 884740
  91.7 15.1 %collective-permute-start.26 = (bf16[128,1536]{1,0:T(8,128)(2,1)S(1)}, bf16[128,1536]{1,0:T(8,128)(2,1)S(1)}, u32[]{:S(2)}, u32[]{:S(2)}) collective-permute-start(bf16[128,1536]{1,0:T(8,128)(2,1)S(1)} %add.50.x0), channel_id=1, source_target_pairs={{0,1},{1,0},{2,3},{3,2},{4,5},{5,4},{6,7},{7,6},{8,9},{9,8},{10,11... | collective-permute-start | bytes 1179656 | tf_op jit(solution)/shard_map/ppermute | solution.py:271
  97.3 10.4 %collective-permute-start.23 = (bf16[1544,128]{1,0:T(8,128)(2,1)S(1)}, bf16[1544,128]{1,0:T(8,128)(2,1)S(1)}, u32[]{:S(2)}, u32[]{:S(2)}) collective-permute-start(bf16[1544,128]{1,0:T(8,128)(2,1)S(1)} %add.49.y0), channel_id=1, source_target_pairs={{0,1},{1,0},{2,3},{3,2},{4,5},{5,4},{6,7},{7,6},{8,9},{9,8},{10,11... | collective-permute-start | bytes 1185800 | tf_op jit(solution)/shard_map/ppermute | solution.py:271
  109.3 11.4 %collective-permute-start.33 = (bf16[176,1152]{1,0:T(8,128)(2,1)S(1)}, bf16[176,1152]{1,0:T(8,128)(2,1)S(1)}, u32[]{:S(2)}, u32[]{:S(2)}) collective-permute-start(bf16[176,1152]{1,0:T(8,128)(2,1)S(1)} %get-tuple-element.81), channel_id=1, source_target_pairs={{0,8},{8,0},{16,24},{24,16},{1,9},{9,1},{17,25},{25,17},{2,10},{10... | collective-permute-start | bytes 1216520 | tf_op jit(solution)/shard_map/ppermute | solution.py:264
  109.9 14.9 %collective-permute-start.18 = (bf16[2,136,1536]{2,1,0:T(8,128)(2,1)S(1)}, bf16[2,136,1536]{2,1,0:T(8,128)(2,1)S(1)}, u32[]{:S(2)}, u32[]{:S(2)}) collective-permute-start(bf16[2,136,1536]{2,1,0:T(8,128)(2,1)S(1)} %get-tuple-element.56), channel_id=1, source_target_pairs={{0,1},{1,0},{2,3},{3,2},{4,5},{5,4},{6,7},{7,6},{8,9},{9,8},{10,11... | collective-permute-start | bytes 2506760 | tf_op jit(solution)/shard_map/ppermute | solution.py:271
  109.9 18.7 %collective-permute-start.9 = (bf16[136,1536]{1,0:T(8,128)(2,1)S(1)}, bf16[136,1536]{1,0:T(8,128)(2,1)S(1)}, u32[]{:S(2)}, u32[]{:S(2)}) collective-permute-start(bf16[136,1536]{1,0:T(8,128)(2,1)S(1)} %get-tuple-element.49), channel_id=1, source_target_pairs={{0,1},{1,0},{2,3},{3,2},{4,5},{5,4},{6,7},{7,6},{8,9},{9,8},{10,11... | collective-permute-start | bytes 1253384 | tf_op jit(solution)/shard_map/ppermute | solution.py:271
  110.4 13.8 %collective-permute-start.31 = (bf16[208,1152]{1,0:T(8,128)(2,1)S(1)}, bf16[208,1152]{1,0:T(8,128)(2,1)S(1)}, u32[]{:S(2)}, u32[]{:S(2)}) collective-permute-start(bf16[208,1152]{1,0:T(8,128)(2,1)S(1)} %get-tuple-element.79), channel_id=1, source_target_pairs={{0,16},{8,24},{16,0},{24,8},{1,17},{9,25},{17,1},{25,9},{2,18},{10... | collective-permute-start | bytes 1437704 | tf_op jit(solution)/shard_map/ppermute | solution.py:264
  112.5 22.2 %collective-permute-start.30 = (bf16[208,1152]{1,0:T(8,128)(2,1)S(1)}, bf16[208,1152]{1,0:T(8,128)(2,1)S(1)}, u32[]{:S(2)}, u32[]{:S(2)}) collective-permute-start(bf16[208,1152]{1,0:T(8,128)(2,1)S(1)} %get-tuple-element.77), channel_id=1, source_target_pairs={{0,16},{8,24},{16,0},{24,8},{1,17},{9,25},{17,1},{25,9},{2,18},{10... | collective-permute-start | bytes 1437704 | tf_op jit(solution)/shard_map/ppermute | solution.py:264
  120.7 1.8 %collective-permute-start.27 = (bf16[136,1536]{1,0:T(8,128)(2,1)S(1)}, bf16[136,1536]{1,0:T(8,128)(2,1)S(1)}, u32[]{:S(2)}, u32[]{:S(2)}) collective-permute-start(bf16[136,1536]{1,0:T(8,128)(2,1)S(1)} %get-tuple-element.72), channel_id=1, source_target_pairs={{0,1},{1,0},{2,3},{3,2},{4,5},{5,4},{6,7},{7,6},{8,9},{9,8},{10,11... | collective-permute-start | bytes 1253384 | tf_op jit(solution)/shard_map/ppermute | solution.py:271
  122.5 12.2 %collective-permute-start.29 = (bf16[176,1152]{1,0:T(8,128)(2,1)S(1)}, bf16[176,1152]{1,0:T(8,128)(2,1)S(1)}, u32[]{:S(2)}, u32[]{:S(2)}) collective-permute-start(bf16[176,1152]{1,0:T(8,128)(2,1)S(1)} %get-tuple-element.76), channel_id=1, source_target_pairs={{0,8},{8,0},{16,24},{24,16},{1,9},{9,1},{17,25},{25,17},{2,10},{10... | collective-permute-start | bytes 1216520 | tf_op jit(solution)/shard_map/ppermute | solution.py:264
  124.3 18.0 %collective-permute-start.34 = (bf16[176,1152]{1,0:T(8,128)(2,1)S(1)}, bf16[176,1152]{1,0:T(8,128)(2,1)S(1)}, u32[]{:S(2)}, u32[]{:S(2)}) collective-permute-start(bf16[176,1152]{1,0:T(8,128)(2,1)S(1)} %add_convert_fusion.5), channel_id=1, source_target_pairs={{0,16},{8,24},{16,0},{24,8},{1,17},{9,25},{17,1},{25,9},{2,18},{10... | collective-permute-start | bytes 1216520 | tf_op jit(solution)/shard_map/ppermute | solution.py:264
  124.8 20.4 %collective-permute-start.28 = (bf16[136,1536]{1,0:T(8,128)(2,1)S(1)}, bf16[136,1536]{1,0:T(8,128)(2,1)S(1)}, u32[]{:S(2)}, u32[]{:S(2)}) collective-permute-start(bf16[136,1536]{1,0:T(8,128)(2,1)S(1)} %add_convert_fusion.1), channel_id=1, source_target_pairs={{0,6},{1,7},{2,4},{3,5},{4,2},{5,3},{6,0},{7,1},{8,14},{9,15},{10,... | collective-permute-start | bytes 1253384 | tf_op jit(solution)/shard_map/ppermute | solution.py:268
  128.4 10.4 %copy-start = (bf16[1,384,768]{2,1,0:T(8,128)(2,1)S(1)}, bf16[1,384,768]{2,1,0:T(8,128)(2,1)}, u32[]{:S(2)}) copy-start(bf16[1,384,768]{2,1,0:T(8,128)(2,1)} %min_ref.1) | copy-start | bytes 1769476
  128.4 10.4 %copy-start.3 = (bf16[1,384,384]{2,1,0:T(8,128)(2,1)S(1)}, bf16[1,384,384]{2,1,0:T(8,128)(2,1)}, u32[]{:S(2)}) copy-start(bf16[1,384,384]{2,1,0:T(8,128)(2,1)} %mout_ref.1) | copy-start | bytes 884740
  128.6 15.5 %collective-permute-start.32 = (bf16[208,1152]{1,0:T(8,128)(2,1)S(1)}, bf16[208,1152]{1,0:T(8,128)(2,1)S(1)}, u32[]{:S(2)}, u32[]{:S(2)}) collective-permute-start(bf16[208,1152]{1,0:T(8,128)(2,1)S(1)} %add_convert_fusion), channel_id=1, source_target_pairs={{0,8},{8,0},{16,24},{24,16},{1,9},{9,1},{17,25},{25,17},{2,10},{10... | collective-permute-start | bytes 1437704 | tf_op jit(solution)/shard_map/ppermute | solution.py:264
  134.7 13.6 %collective-permute-start.19 = (bf16[136,1536]{1,0:T(8,128)(2,1)S(1)}, bf16[136,1536]{1,0:T(8,128)(2,1)S(1)}, u32[]{:S(2)}, u32[]{:S(2)}) collective-permute-start(bf16[136,1536]{1,0:T(8,128)(2,1)S(1)} %get-tuple-element.84), channel_id=1, source_target_pairs={{0,2},{1,3},{2,0},{3,1},{4,6},{5,7},{6,4},{7,5},{8,10},{9,11},{10,... | collective-permute-start | bytes 1253384 | tf_op jit(solution)/shard_map/ppermute | solution.py:268
  134.7 27.0 %collective-permute-start.20 = (bf16[136,1536]{1,0:T(8,128)(2,1)S(1)}, bf16[136,1536]{1,0:T(8,128)(2,1)S(1)}, u32[]{:S(2)}, u32[]{:S(2)}) collective-permute-start(bf16[136,1536]{1,0:T(8,128)(2,1)S(1)} %get-tuple-element.85), channel_id=1, source_target_pairs={{0,4},{1,5},{2,6},{3,7},{4,0},{5,1},{6,2},{7,3},{8,12},{9,13},{10,... | collective-permute-start | bytes 1253384 | tf_op jit(solution)/shard_map/ppermute | solution.py:268
  139.2 22.5 %copy-start.6 = (s32[128,4]{0,1:T(4,128)S(1)}, s32[128,4]{0,1:T(4,128)}, u32[]{:S(2)}) copy-start(s32[128,4]{0,1:T(4,128)} %param.9) | copy-start | bytes 6148
  (13 other events, 10.7 us)

commit v6 on v5

--- a/solution.py
+++ b/solution.py
@@ -83,10 +83,10 @@
 
 
 def write_rows(out, row_grad, table):
-    tok = row_grad.shape[0]
-    out[0:tok, :] = row_grad
-    tail = jnp.zeros((table.shape[0], out.shape[1] - tok), f32)
-    out[tok:, :] = jnp.concatenate([table, tail], axis=1).astype(bf16)
+    tok, width = row_grad.shape
+    for j in range(width // 128):
+        out[j * tok : (j + 1) * tok, :] = row_grad[:, j * 128 : (j + 1) * 128]
+    out[width // 128 * tok :, :] = table.astype(bf16)
 
 
 def activations(both):
@@ -195,10 +195,10 @@
 
 
 def grad_kernel(ids_ref, y0, y1, xs, silu, slope, hidden, wout, acc_in, acc_out, *refs):
-    r3a_ref, r3b_ref, dgus, chs, ys, tab_ref = refs
+    r3a_ref, r3b_ref, dgus, chs, ys, gate_ref = refs
     rep, expert = ids_ref[0], ids_ref[1]
     tok, width = ys.shape[0] // 2, ys.shape[1]
-    ffn, experts = wout.shape[0], tab_ref.shape[1]
+    ffn = wout.shape[0]
     ys[0:tok, :] = unstack(y0, width)
     ys[tok:, :] = unstack(y1, width)
     first = width // 128 * tok
@@ -209,8 +209,7 @@
     dh = back * gate
     dgus[:, :ffn] = (dh * slope[...]).astype(bf16)
     dgus[:, ffn:] = (dh * silu[...]).astype(bf16)
-    for i in range(2):
-        tab_ref[i] = gate_table(gate_grad[i * tok : (i + 1) * tok], experts, expert)
+    gate_ref[...] = gate_grad
     shard_grads((r3a_ref, r3b_ref), acc_in, acc_out, xs, ys, dgus, chs, rep ^ 3)
 
 
@@ -222,11 +221,27 @@
     shard_grads((mine_ref,), *args, rep)
 
 
-def rows_kernel(dgus, win, tab_ref, keep_ref, give_ref):
-    tok = dgus.shape[0] // 2
+def rows_kernel(ids_ref, dgus, win, gate_ref, keep_ref, give_ref):
+    tok, width = dgus.shape[0] // 2, win.shape[0]
+    experts = keep_ref.shape[0] - width // 128 * tok
     row_grad = dot(dgus[...], win[...], 1, 1).astype(bf16)
     for i, out in enumerate((keep_ref, give_ref)):
-        write_rows(out, row_grad[i * tok : (i + 1) * tok], tab_ref[i])
+        part = slice(i * tok, (i + 1) * tok)
+        write_rows(out, row_grad[part], gate_table(gate_ref[part, :], experts, ids_ref[1]))
+
+
+def combine_kernel(routes_ref, p0, p1, p2, p3, token_ref, gate_ref):
+    tok, width = token_ref.shape
+    parts = (p0, p1, p2, p3)
+    for j in range(width // 128):
+        rows = slice(j * tok, (j + 1) * tok)
+        total = sum(p[rows, :].astype(f32) for p in parts)
+        token_ref[:, j * 128 : (j + 1) * 128] = total.astype(bf16)
+    table = sum(p[width // 128 * tok :, :].astype(f32) for p in parts)
+    ids = lax.broadcasted_iota(jnp.int32, table.shape, 0)
+    for k in range(routes_ref.shape[0]):
+        mine = jnp.where(ids == routes_ref[k : k + 1, :], table, 0.0)
+        gate_ref[k : k + 1, :] = jnp.sum(mine, axis=0, keepdims=True).astype(bf16)
 
 
 def mix_kernel(own_ref, t1b_ref, t2a_ref, min_ref, mout_ref, base_ref):
@@ -308,7 +323,7 @@
     near_xp = partner(near_x)
     middle_y = over_chips(own_y, to_middle)
     rows = 2 * tok
-    block = ((tok + experts, width), bf16)
+    block = (stacked(width, tok, experts), bf16)
     flops = 5 * rows * width * both_w
     own_blocks = [own_x, own_xp, own_y, own_yp]
     keep, give_own, own_dgu, own_ch, win, wout = call(
@@ -335,7 +350,7 @@
     keep, give, *more = call(
         rest_kernel,
         [ids, near_y, near_yp, far_y, far_yp, *early, win, wout],
-        [((2, tok + experts, width), bf16)] * 2
+        [((2, *stacked(width, tok, experts)), bf16)] * 2
         + [((2 * rows, width), bf16), ((2 * rows, both_w), bf16), ((2 * rows, ffn), bf16)],
         mib=8,
         scalars=1,
@@ -361,16 +376,16 @@
     )
     cross_y = ends_y + middle_y
     cross_yp = partner(cross_y)
+    home_far = over_chips(home_far, to_far)
     home_near = over_chips(home_near, to_near)
-    home_far = over_chips(home_far, to_far)
     part_a = shard * 13 // 24 // 16 * 16
     part_b = shard - part_a
-    r3a, r3b, dgus, chs, ys, table = call(
+    r3a, r3b, dgus, chs, ys, gate_last = call(
         grad_kernel,
         [ids, cross_y, cross_yp, xs, silu, slope, hidden, wout]
         + [acc_in, acc_out],
         [((part_a, cols), bf16), ((part_b, cols), bf16)]
-        + [((rows, both_w), bf16), ((rows, ffn), bf16), ((rows, width), bf16), ((2, experts, tok), f32)],
+        + [((rows, both_w), bf16), ((rows, ffn), bf16), ((rows, width), bf16), ((rows, 1), f32)],
         mib=8,
         scalars=1,
         flops=rows * width * both_w * 2,
@@ -385,7 +400,7 @@
         scalars=1,
         flops=2 * rows * width * both_w,
     )
-    keep2, give2 = call(rows_kernel, [dgus, win, table], [block, block])
+    keep2, give2 = call(rows_kernel, [ids, dgus, win, gate_last], [block, block], scalars=1)
     got2 = partner(give2)
     t2a = over_rep(r2a, 2)
     t1b = over_rep(r1b, 1)
@@ -393,16 +408,17 @@
     home_cross = over_chips(last, to_cross)
     t1a = over_rep((r1a.astype(f32) + s3a.astype(f32)).astype(bf16), 1)
     t2b = over_rep((r2b.astype(f32) + s3b.astype(f32)).astype(bf16), 2)
-    parts = (home_own, home_near, home_far, home_cross)
-    token_grad = sum(p[:tok].astype(f32) for p in parts).astype(bf16)
-    table = sum(p[tok:, :tok].astype(f32) for p in parts)
-    picked = routes.T[:, None, :] == jnp.arange(experts, dtype=jnp.int32)[None, :, None]
-    gate_grad = jnp.sum(jnp.where(picked, table[None], 0.0), axis=1).astype(bf16).T
+    token_grad, gate_grad = call(
+        combine_kernel,
+        [routes.T, home_own, home_near, home_far, home_cross],
+        [((tok, width), bf16), ((top, tok), bf16)],
+        mib=4,
+    )
     (base,) = call(mix_kernel, [mine, t1b, t2a, momentum_in, momentum_out], [((shard, cols), f32)])
     new_in, new_out = call(
         finish_kernel, [base, t1a, t2b], [(momentum_in.shape, bf16), (momentum_out.shape, bf16)]
     )
-    return token_grad, gate_grad, new_in, new_out
+    return token_grad, gate_grad.T, new_in, new_out
 
 
 def slot_positions(routes, experts):

time: 164 us -> 162 us (0.988)
    ppermute x13, waiting for transfers between devices: 23.7 us -> 25.4 us  [over_rep(): return lax.ppermute(value, 'rep', [(i, i ^ bits) for i in range(4)])]
    ppermute x11, waiting for transfers between devices: 1.67 us -> 0.03 us  [partner(): return lax.ppermute(value, 'expert', [(i, i ^ 1) for i in range(experts)])]
    pallas_call x11 -> x12, Pallas kernels: 20.2 us -> 21.8 us  [call(): pl.pallas_call(kernel, out_shape=[jax.ShapeDtypeStruct(shape, dtype) for...]
  transfers between devices with their start and end apart: 35 -> 35, of which waited for: 14 -> 14; matrix products, arithmetic and copies ran while one was open for 2% -> 3% of each run, Pallas kernels for 11% -> 11%
where the time goes in v6:
time: 162 us
  waiting for transfers between devices  76.9 us (47%)
  starting transfers between devices  47.1 us (29%)
  Pallas kernels  21.8 us (13%)
  local copies, waits for them, and re-layouts  11.5 us (7%)
  other arithmetic  3.28 us (2%)
    ppermute x11, waiting for transfers between devices, over_chips(): return lax.ppermute(value, 'expert', pairs)  51.5 us
    ppermute x11, starting transfers between devices, over_chips(): return lax.ppermute(value, 'expert', pairs)  31.8 us
    ppermute x13, waiting for transfers between devices, over_rep(): return lax.ppermute(value, 'rep', [(i, i ^ bits) for i in range(4)])  25.4 us
    pallas_call x12, Pallas kernels, call(): pl.pallas_call(kernel, out_shape=[jax.ShapeDtypeStruct(shape, dtype) for...  21.8 us
    ppermute x13, starting transfers between devices, over_rep(): return lax.ppermute(value, 'rep', [(i, i ^ bits) for i in range(4)])  13.4 us
    unnamed x52, local copies, waits for them, and re-layouts  10.7 us
  transfers between devices with their start and end apart: 35, of which 14 were waited for; matrix products, arithmetic and copies ran while one was open for 3% of the time, Pallas kernels for 11%

profile of v6, /device:TPU:0, one launch (start us, length us, event | category | flops | bytes accessed | tf_op | source)
XLA Modules:
  0.0 161.5 jit_solution(1969084563032626023)
XLA Ops:
  0.6 3.1 %collective-permute-start.7 = (bf16[1,384,384]{2,1,0:T(8,128)(2,1)}, bf16[1,384,384]{2,1,0:T(8,128)(2,1)S(1)}, u32[]{:S(2)}, u32[]{:S(2)}) collective-permute-start(bf16[1,384,384]{2,1,0:T(8,128)(2,1)} %wout_hbm.1), channel_id=1, source_target_pairs={{0,16},{8,24},{16,0},{24,8},{1,17},{9,25},{17,1},{25,9},{2,18},{10... | collective-permute-start | bytes 884744 | tf_op jit(solution)/shard_map/ppermute | solution.py:279
  3.7 1.0 copy-done.1
  4.7 1.0 copy-done.2
  5.7 1.0 copy-done.4
  8.0 1.5 shard_map.111
  10.2 0.8 copy-done.12
  11.0 1.5 collective-permute-start.6
  12.5 2.6 %collective-permute-start.16 = (bf16[128,1536]{1,0:T(8,128)(2,1)S(1)}, bf16[128,1536]{1,0:T(8,128)(2,1)}, u32[]{:S(2)}, u32[]{:S(2)}) collective-permute-start(bf16[128,1536]{1,0:T(8,128)(2,1)S(1)} %copy-done.2), channel_id=1, source_target_pairs={{0,4},{1,5},{2,6},{3,7},{4,0},{5,1},{6,2},{7,3},{8,12},{9,13},{10,... | collective-permute-start | bytes 1179656 | tf_op jit(solution)/shard_map/ppermute | solution.py:283
  15.1 1.6 collective-permute-start.14
  17.3 3.1 %collective-permute-done.6.refs_6_ = bf16[1,384,384]{2,1,0:T(8,128)(2,1)S(1)} collective-permute-done((bf16[1,384,384]{2,1,0:T(8,128)(2,1)S(1)}, bf16[1,384,384]{2,1,0:T(8,128)(2,1)S(1)}, u32[]{:S(2)}, u32[]{:S(2)}) %collective-permute-start.6) | collective-permute-done | bytes 294944 | tf_op jit(solution)/shard_map/ppermute | solution.py:279
  20.4 0.7 copy-done.20
  21.1 0.7 copy-done.14
  21.9 1.5 collective-permute-start.2
  23.4 10.6 %collective-permute-done.16.f0 = bf16[128,1536]{1,0:T(8,128)(2,1)} collective-permute-done((bf16[128,1536]{1,0:T(8,128)(2,1)S(1)}, bf16[128,1536]{1,0:T(8,128)(2,1)}, u32[]{:S(2)}, u32[]{:S(2)}) %collective-permute-start.16) | collective-permute-done | bytes 393248 | tf_op jit(solution)/shard_map/ppermute | solution.py:283
  34.8 16.5 %collective-permute-start.10 = (bf16[1544,128]{1,0:T(8,128)(2,1)S(1)}, bf16[1544,128]{1,0:T(8,128)(2,1)S(1)}, u32[]{:S(2)}, u32[]{:S(2)}) collective-permute-start(bf16[1544,128]{1,0:T(8,128)(2,1)S(1)} %get-tuple-element.47.y0), channel_id=1, source_target_pairs={{0,2},{1,3},{2,0},{3,1},{4,6},{5,7},{6,4},{7,5},{8,10},{9,11},{10,... | collective-permute-start | bytes 1185800 | tf_op jit(solution)/shard_map/ppermute | solution.py:283
  52.0 7.3 %collective-permute-done.12.refs_2_ = bf16[1544,128]{1,0:T(8,128)(2,1)S(1)} collective-permute-done((bf16[1544,128]{1,0:T(8,128)(2,1)S(1)}, bf16[1544,128]{1,0:T(8,128)(2,1)S(1)}, u32[]{:S(2)}, u32[]{:S(2)}) %collective-permute-start.12) | collective-permute-done | bytes 395296 | tf_op jit(solution)/shard_map/ppermute | solution.py:283
  59.8 0.7 copy-done.16
  60.5 6.4 %collective-permute-done.10.refs_0_ = bf16[1544,128]{1,0:T(8,128)(2,1)S(1)} collective-permute-done((bf16[1544,128]{1,0:T(8,128)(2,1)S(1)}, bf16[1544,128]{1,0:T(8,128)(2,1)S(1)}, u32[]{:S(2)}, u32[]{:S(2)}) %collective-permute-start.10) | collective-permute-done | bytes 395296 | tf_op jit(solution)/shard_map/ppermute | solution.py:283
  66.9 1.3 collective-permute-start.21
  68.2 1.3 collective-permute-start.24
  69.5 0.8 slice.24
  71.4 0.7 copy-done.22
  72.1 4.3 %collective-permute-done.5.refs_4_ = bf16[1,96,768]{2,1,0:T(8,128)(2,1)S(1)} collective-permute-done((bf16[1,96,768]{2,1,0:T(8,128)(2,1)S(1)}, bf16[1,96,768]{2,1,0:T(8,128)(2,1)S(1)}, u32[]{:S(2)}, u32[]{:S(2)}) %collective-permute-start.5) | collective-permute-done | bytes 147488 | tf_op jit(solution)/shard_map/ppermute | solution.py:279
  76.4 12.0 %collective-permute-done.24 = bf16[128,1536]{1,0:T(8,128)(2,1)} collective-permute-done((bf16[128,1536]{1,0:T(8,128)(2,1)}, bf16[128,1536]{1,0:T(8,128)(2,1)}, u32[]{:S(2)}, u32[]{:S(2)}) %collective-permute-start.24) | collective-permute-done | bytes 393248 | tf_op jit(solution)/shard_map/ppermute | solution.py:283
  89.1 1.3 add.30.x0
  90.5 1.2 add.29.y0
  91.8 1.0 copy-done.21
  92.8 1.0 copy-done.23
  93.8 3.5 %shard_map.112 = (bf16[1544,128]{1,0:T(8,128)(2,1)S(1)}, bf16[1544,128]{1,0:T(8,128)(2,1)S(1)}, bf16[256,768]{1,0:T(8,128)(2,1)S(1)}, bf16[256,384]{1,0:T(8,128)...) custom-call(s32[2]{0:T(128)S(1)} %pad_add_fusion.ids_ref, bf16[128,1536]{1,0:T(8,128)(2,1)S(1)} %copy-done.13, ...), custom_call_target="tpu_custom_call" | custom-call | flops 1509949440 | bytes 4194304 | tf_op jit(solution)/shard_map/pallas_call | solution.py:23
  97.8 2.9 %shard_map.113 = (bf16[512,1536]{1,0:T(8,128)(2,1)S(1)}, f32[512,384]{1,0:T(8,128)S(1)}, f32[512,384]{1,0:T(8,128)S(1)}, bf16[512,384]{1,0:T(8,128)(2,1)S(1)}) custom-call(bf16[128,1536]{1,0:T(8,128)(2,1)} %collective-permute-done.14.n0, bf16[128,1536]{1,0:T(8,128)(2,1)} %collective-permute-done.15.n1, bf16[128,1536]{1,0:T(8,128)(2,1)} %collective-permute-done.16.f0, ...), custom_call_target="tpu_custom_call" | custom-call | flops 1207959552 | bytes 4194304 | tf_op jit(solution)/shard_map/pallas_call | solution.py:23
  100.7 3.1 %shard_map.114 = (bf16[2,1544,128]{2,1,0:T(8,128)(2,1)S(1)}, bf16[2,1544,128]{2,1,0:T(8,128)(2,1)S(1)}, bf16[512,1536]{1,0:T(8,128)(2,1)S(1)}, bf16[512,768]{1,0:T(8,128)(2,1)S(1)}, bf16[512,384]{1,0:T(8,128)(2,1)S(1)}) custom-call(s32[2]{0:T(128)S(1)} %pad_add_fusion.ids_ref, bf16[1544,128]{1,0:T(8,128)(2,1)S(1)} %collective-permute-done.10.refs_0_, ...), custom_call_target="tpu_custom_call" | custom-call | flops 1509949440 | bytes 4194304 | tf_op jit(solution)/shard_map/pallas_call | solution.py:23
  103.9 3.0 %shard_map.116 = (f32[1536,768]{1,0:T(8,128)S(1)}, f32[384,1536]{1,0:T(8,128)S(1)}) custom-call(bf16[128,1536]{1,0:T(8,128)(2,1)S(1)} %copy-done.13, bf16[128,1536]{1,0:T(8,128)(2,1)S(1)} %copy-done.15, bf16[1544,128]{1,0:T(8,128)(2,1)S(1)} %copy-done.9, bf16[1544,128]{1,0:T(8,128)(2,1)S(1)} %copy-done.11, bf16[256,768]{1,0:T(8,128)(2,1)S(1)} %get-tuple-element.63.own_dgu, ...), custom_call_target="tpu_custom_call" | custom-call | flops 3019898880 | bytes 4194304 | tf_op jit(solution)/shard_map/pallas_call | solution.py:23
  106.9 0.9 shard_map.115
  107.8 1.6 %shard_map.117 = (bf16[208,1152]{1,0:T(8,128)(2,1)S(1)}, bf16[176,1152]{1,0:T(8,128)(2,1)S(1)}, bf16[256,768]{1,0:T(8,128)(2,1)S(1)}, bf16[256,384]{1,0:T(8,128)...) custom-call(s32[2]{0:T(128)S(1)} %pad_add_fusion.ids_ref, bf16[1544,128]{1,0:T(8,128)(2,1)S(1)} %add.29.y0, ...), custom_call_target="tpu_custom_call" | custom-call | flops 603979776 | bytes 4194304 | tf_op jit(solution)/shard_map/pallas_call | solution.py:23
  109.4 1.4 shard_map.118
  112.4 1.6 shard_map.120
  114.0 1.6 %collective-permute-start.30 = (bf16[208,1152]{1,0:T(8,128)(2,1)S(1)}, bf16[208,1152]{1,0:T(8,128)(2,1)S(1)}, u32[]{:S(2)}, u32[]{:S(2)}) collective-permute-start(bf16[208,1152]{1,0:T(8,128)(2,1)S(1)} %get-tuple-element.81), channel_id=1, source_target_pairs={{0,16},{8,24},{16,0},{24,8},{1,17},{9,25},{17,1},{25,9},{2,18},{10... | collective-permute-start | bytes 1437704 | tf_op jit(solution)/shard_map/ppermute | solution.py:279
  115.7 7.4 %collective-permute-done.33 = bf16[176,1152]{1,0:T(8,128)(2,1)S(1)} collective-permute-done((bf16[176,1152]{1,0:T(8,128)(2,1)S(1)}, bf16[176,1152]{1,0:T(8,128)(2,1)S(1)}, u32[]{:S(2)}, u32[]{:S(2)}) %collective-permute-start.33) | collective-permute-done | bytes 405536 | tf_op jit(solution)/shard_map/ppermute | solution.py:279
  123.8 2.0 %collective-permute-done.31 = bf16[208,1152]{1,0:T(8,128)(2,1)S(1)} collective-permute-done((bf16[208,1152]{1,0:T(8,128)(2,1)S(1)}, bf16[208,1152]{1,0:T(8,128)(2,1)S(1)}, u32[]{:S(2)}, u32[]{:S(2)}) %collective-permute-start.31) | collective-permute-done | bytes 479264 | tf_op jit(solution)/shard_map/ppermute | solution.py:279
  125.8 3.5 %collective-permute-start.28 = (bf16[1544,128]{1,0:T(8,128)(2,1)S(1)}, bf16[1544,128]{1,0:T(8,128)(2,1)S(1)}, u32[]{:S(2)}, u32[]{:S(2)}) collective-permute-start(bf16[1544,128]{1,0:T(8,128)(2,1)S(1)} %add_convert_fusion.2), channel_id=1, source_target_pairs={{0,6},{1,7},{2,4},{3,5},{4,2},{5,3},{6,0},{7,1},{8,14},{9,15},{10,... | collective-permute-start | bytes 1185800 | tf_op jit(solution)/shard_map/ppermute | solution.py:283
  130.2 1.6 collective-permute-start.32
  131.7 3.6 %collective-permute-done.29.t1b_ref = bf16[176,1152]{1,0:T(8,128)(2,1)S(1)} collective-permute-done((bf16[176,1152]{1,0:T(8,128)(2,1)S(1)}, bf16[176,1152]{1,0:T(8,128)(2,1)S(1)}, u32[]{:S(2)}, u32[]{:S(2)}) %collective-permute-start.29) | collective-permute-done | bytes 405536 | tf_op jit(solution)/shard_map/ppermute | solution.py:279
  136.0 3.4 %collective-permute-start.20 = (bf16[1544,128]{1,0:T(8,128)(2,1)S(1)}, bf16[1544,128]{1,0:T(8,128)(2,1)S(1)}, u32[]{:S(2)}, u32[]{:S(2)}) collective-permute-start(bf16[1544,128]{1,0:T(8,128)(2,1)S(1)} %get-tuple-element.88), channel_id=1, source_target_pairs={{0,4},{1,5},{2,6},{3,7},{4,0},{5,1},{6,2},{7,3},{8,12},{9,13},{10,... | collective-permute-start | bytes 1185800 | tf_op jit(solution)/shard_map/ppermute | solution.py:283
  139.9 4.0 %collective-permute-done.34.t2b_ref = bf16[176,1152]{1,0:T(8,128)(2,1)S(1)} collective-permute-done((bf16[176,1152]{1,0:T(8,128)(2,1)S(1)}, bf16[176,1152]{1,0:T(8,128)(2,1)S(1)}, u32[]{:S(2)}, u32[]{:S(2)}) %collective-permute-start.34) | collective-permute-done | bytes 405536 | tf_op jit(solution)/shard_map/ppermute | solution.py:279
  144.2 1.1 shard_map.122
  145.3 2.0 %collective-permute-done.19.p1 = bf16[1544,128]{1,0:T(8,128)(2,1)S(1)} collective-permute-done((bf16[1544,128]{1,0:T(8,128)(2,1)S(1)}, bf16[1544,128]{1,0:T(8,128)(2,1)S(1)}, u32[]{:S(2)}, u32[]{:S(2)}) %collective-permute-start.19) | collective-permute-done | bytes 395296 | tf_op jit(solution)/shard_map/ppermute | solution.py:283
  147.4 13.2 %collective-permute-done.20.p2 = bf16[1544,128]{1,0:T(8,128)(2,1)S(1)} collective-permute-done((bf16[1544,128]{1,0:T(8,128)(2,1)S(1)}, bf16[1544,128]{1,0:T(8,128)(2,1)S(1)}, u32[]{:S(2)}, u32[]{:S(2)}) %collective-permute-start.20) | collective-permute-done | bytes 395296 | tf_op jit(solution)/shard_map/ppermute | solution.py:283
  160.5 1.0 shard_map.119
  (96 shorter events, 12.0 us)
Async XLA Ops:
  0.6 16.0 %collective-permute-start.7 = (bf16[1,384,384]{2,1,0:T(8,128)(2,1)}, bf16[1,384,384]{2,1,0:T(8,128)(2,1)S(1)}, u32[]{:S(2)}, u32[]{:S(2)}) collective-permute-start(bf16[1,384,384]{2,1,0:T(8,128)(2,1)} %wout_hbm.1), channel_id=1, source_target_pairs={{0,16},{8,24},{16,0},{24,8},{1,17},{9,25},{17,1},{25,9},{2,18},{10... | collective-permute-start | bytes 884744 | tf_op jit(solution)/shard_map/ppermute | solution.py:279
  10.2 66.2 %copy-start.8 = (bf16[1544,128]{1,0:T(8,128)(2,1)}, bf16[1544,128]{1,0:T(8,128)(2,1)S(1)}, u32[]{:S(2)}) copy-start(bf16[1544,128]{1,0:T(8,128)(2,1)S(1)} %get-tuple-element.47.y0) | copy-start | bytes 1185796
  10.2 10.9 %collective-permute-start = (bf16[128,1536]{1,0:T(8,128)(2,1)S(1)}, bf16[128,1536]{1,0:T(8,128)(2,1)S(1)}, u32[]{:S(2)}, u32[]{:S(2)}) collective-permute-start(bf16[128,1536]{1,0:T(8,128)(2,1)S(1)} %get-tuple-element.46.x0), channel_id=1, source_target_pairs={{0,1},{1,0},{2,3},{3,2},{4,5},{5,4},{6,7},{7,6},{8,9},{9,8},{10,11... | collective-permute-start | bytes 1179656 | tf_op jit(solution)/shard_map/ppermute | solution.py:286
  11.0 9.4 %collective-permute-start.6 = (bf16[1,384,384]{2,1,0:T(8,128)(2,1)S(1)}, bf16[1,384,384]{2,1,0:T(8,128)(2,1)S(1)}, u32[]{:S(2)}, u32[]{:S(2)}) collective-permute-start(bf16[1,384,384]{2,1,0:T(8,128)(2,1)S(1)} %copy-done.4), channel_id=1, source_target_pairs={{0,8},{8,0},{16,24},{24,16},{1,9},{9,1},{17,25},{25,17},{2,10},{10... | collective-permute-start | bytes 884744 | tf_op jit(solution)/shard_map/ppermute | solution.py:279
  12.5 21.5 %collective-permute-start.16 = (bf16[128,1536]{1,0:T(8,128)(2,1)S(1)}, bf16[128,1536]{1,0:T(8,128)(2,1)}, u32[]{:S(2)}, u32[]{:S(2)}) collective-permute-start(bf16[128,1536]{1,0:T(8,128)(2,1)S(1)} %copy-done.2), channel_id=1, source_target_pairs={{0,4},{1,5},{2,6},{3,7},{4,0},{5,1},{6,2},{7,3},{8,12},{9,13},{10,... | collective-permute-start | bytes 1179656 | tf_op jit(solution)/shard_map/ppermute | solution.py:283
  15.1 19.4 %collective-permute-start.14 = (bf16[128,1536]{1,0:T(8,128)(2,1)S(1)}, bf16[128,1536]{1,0:T(8,128)(2,1)}, u32[]{:S(2)}, u32[]{:S(2)}) collective-permute-start(bf16[128,1536]{1,0:T(8,128)(2,1)S(1)} %copy-done.2), channel_id=1, source_target_pairs={{0,2},{1,3},{2,0},{3,1},{4,6},{5,7},{6,4},{7,5},{8,10},{9,11},{10,... | collective-permute-start | bytes 1179656 | tf_op jit(solution)/shard_map/ppermute | solution.py:283
  16.7 18.1 %collective-permute-start.25 = (bf16[128,1536]{1,0:T(8,128)(2,1)S(1)}, bf16[128,1536]{1,0:T(8,128)(2,1)S(1)}, u32[]{:S(2)}, u32[]{:S(2)}) collective-permute-start(bf16[128,1536]{1,0:T(8,128)(2,1)S(1)} %copy-done.2), channel_id=1, source_target_pairs={{2,4},{3,5},{4,2},{5,3},{10,12},{11,13},{12,10},{13,11},{18,20},{1... | collective-permute-start | bytes 1179656 | tf_op jit(solution)/shard_map/ppermute | solution.py:283
  21.1 30.2 %collective-permute-start.1 = (bf16[1544,128]{1,0:T(8,128)(2,1)S(1)}, bf16[1544,128]{1,0:T(8,128)(2,1)S(1)}, u32[]{:S(2)}, u32[]{:S(2)}) collective-permute-start(bf16[1544,128]{1,0:T(8,128)(2,1)S(1)} %get-tuple-element.47.y0), channel_id=1, source_target_pairs={{0,1},{1,0},{2,3},{3,2},{4,5},{5,4},{6,7},{7,6},{8,9},{9,8},{10,11... | collective-permute-start | bytes 1185800 | tf_op jit(solution)/shard_map/ppermute | solution.py:286
  21.9 46.3 %collective-permute-start.2 = (bf16[1,384,768]{2,1,0:T(8,128)(2,1)}, bf16[1,384,768]{2,1,0:T(8,128)(2,1)S(1)}, u32[]{:S(2)}, u32[]{:S(2)}) collective-permute-start(bf16[1,384,768]{2,1,0:T(8,128)(2,1)} %win_hbm.1), channel_id=1, source_target_pairs={{0,8},{8,0},{16,24},{24,16},{1,9},{9,1},{17,25},{25,17},{2,10},{10... | collective-permute-start | bytes 1769480 | tf_op jit(solution)/shard_map/ppermute | solution.py:279
  34.0 36.4 %collective-permute-start.3 = (bf16[1,384,768]{2,1,0:T(8,128)(2,1)}, bf16[1,384,768]{2,1,0:T(8,128)(2,1)S(1)}, u32[]{:S(2)}, u32[]{:S(2)}) collective-permute-start(bf16[1,384,768]{2,1,0:T(8,128)(2,1)} %win_hbm.1), channel_id=1, source_target_pairs={{0,16},{8,24},{16,0},{24,8},{1,17},{9,25},{17,1},{25,9},{2,18},{10... | collective-permute-start | bytes 1769480 | tf_op jit(solution)/shard_map/ppermute | solution.py:279
  34.5 24.8 %collective-permute-start.12 = (bf16[1544,128]{1,0:T(8,128)(2,1)S(1)}, bf16[1544,128]{1,0:T(8,128)(2,1)S(1)}, u32[]{:S(2)}, u32[]{:S(2)}) collective-permute-start(bf16[1544,128]{1,0:T(8,128)(2,1)S(1)} %get-tuple-element.47.y0), channel_id=1, source_target_pairs={{0,4},{1,5},{2,6},{3,7},{4,0},{5,1},{6,2},{7,3},{8,12},{9,13},{10,... | collective-permute-start | bytes 1185800 | tf_op jit(solution)/shard_map/ppermute | solution.py:283
  34.8 33.5 %copy-start.25 = (bf16[128,1536]{1,0:T(8,128)(2,1)}, bf16[128,1536]{1,0:T(8,128)(2,1)S(1)}, u32[]{:S(2)}) copy-start(bf16[128,1536]{1,0:T(8,128)(2,1)S(1)} %collective-permute-done.25) | copy-start | bytes 1179652
  34.8 32.1 %collective-permute-start.10 = (bf16[1544,128]{1,0:T(8,128)(2,1)S(1)}, bf16[1544,128]{1,0:T(8,128)(2,1)S(1)}, u32[]{:S(2)}, u32[]{:S(2)}) collective-permute-start(bf16[1544,128]{1,0:T(8,128)(2,1)S(1)} %get-tuple-element.47.y0), channel_id=1, source_target_pairs={{0,2},{1,3},{2,0},{3,1},{4,6},{5,7},{6,4},{7,5},{8,10},{9,11},{10,... | collective-permute-start | bytes 1185800 | tf_op jit(solution)/shard_map/ppermute | solution.py:283
  51.3 37.1 %copy-start.10 = (bf16[1544,128]{1,0:T(8,128)(2,1)}, bf16[1544,128]{1,0:T(8,128)(2,1)S(1)}, u32[]{:S(2)}) copy-start(bf16[1544,128]{1,0:T(8,128)(2,1)S(1)} %collective-permute-done.1.y1) | copy-start | bytes 1185796
  51.3 19.5 %collective-permute-start.22 = (bf16[1544,128]{1,0:T(8,128)(2,1)S(1)}, bf16[1544,128]{1,0:T(8,128)(2,1)S(1)}, u32[]{:S(2)}, u32[]{:S(2)}) collective-permute-start(bf16[1544,128]{1,0:T(8,128)(2,1)S(1)} %get-tuple-element.47.y0), channel_id=1, source_target_pairs={{2,4},{3,5},{4,2},{5,3},{10,12},{11,13},{12,10},{13,11},{18,20},{1... | collective-permute-start | bytes 1185800 | tf_op jit(solution)/shard_map/ppermute | solution.py:283
  59.3 12.2 %collective-permute-start.8 = (bf16[1,384,384]{2,1,0:T(8,128)(2,1)S(1)}, bf16[1,384,384]{2,1,0:T(8,128)(2,1)S(1)}, u32[]{:S(2)}, u32[]{:S(2)}) collective-permute-start(bf16[1,384,384]{2,1,0:T(8,128)(2,1)S(1)} %collective-permute-done.7.refs_7_), channel_id=1, source_target_pairs={{0,8},{8,0},{16,24},{24,16},{1,9},{9,1},{17,25},{25,17},{2,10},{10... | collective-permute-start | bytes 884744 | tf_op jit(solution)/shard_map/ppermute | solution.py:279
  66.9 21.5 %collective-permute-start.21 = (bf16[1544,128]{1,0:T(8,128)(2,1)S(1)}, bf16[1544,128]{1,0:T(8,128)(2,1)}, u32[]{:S(2)}, u32[]{:S(2)}) collective-permute-start(bf16[1544,128]{1,0:T(8,128)(2,1)S(1)} %collective-permute-done.12.refs_2_), channel_id=1, source_target_pairs={{4,6},{5,7},{2,0},{3,1},{12,14},{13,15},{10,8},{11,9},{20,22},{21,... | collective-permute-start | bytes 1185800 | tf_op jit(solution)/shard_map/ppermute | solution.py:283
  68.2 20.2 %collective-permute-start.24 = (bf16[128,1536]{1,0:T(8,128)(2,1)}, bf16[128,1536]{1,0:T(8,128)(2,1)}, u32[]{:S(2)}, u32[]{:S(2)}) collective-permute-start(bf16[128,1536]{1,0:T(8,128)(2,1)} %collective-permute-done.16.f0), channel_id=1, source_target_pairs={{4,6},{5,7},{2,0},{3,1},{12,14},{13,15},{10,8},{11,9},{20,22},{21,... | collective-permute-start | bytes 1179656 | tf_op jit(solution)/shard_map/ppermute | solution.py:283
  70.3 21.4 %collective-permute-start.4 = (bf16[1,288,768]{2,1,0:T(8,128)(2,1)}, bf16[1,288,768]{2,1,0:T(8,128)(2,1)}, u32[]{:S(2)}, u32[]{:S(2)}) collective-permute-start(bf16[1,288,768]{2,1,0:T(8,128)(2,1)} %slice.24), channel_id=1, source_target_pairs={{0,16},{8,24},{16,0},{24,8},{1,17},{9,25},{17,1},{25,9},{2,18},{10... | collective-permute-start | bytes 1327112 | tf_op jit(solution)/shard_map/ppermute | solution.py:279
  70.9 17.6 %copy-start.24 = (bf16[1544,128]{1,0:T(8,128)(2,1)}, bf16[1544,128]{1,0:T(8,128)(2,1)S(1)}, u32[]{:S(2)}) copy-start(bf16[1544,128]{1,0:T(8,128)(2,1)S(1)} %collective-permute-done.22) | copy-start | bytes 1185796
  70.9 5.6 %collective-permute-start.5 = (bf16[1,96,768]{2,1,0:T(8,128)(2,1)S(1)}, bf16[1,96,768]{2,1,0:T(8,128)(2,1)S(1)}, u32[]{:S(2)}, u32[]{:S(2)}) collective-permute-start(bf16[1,96,768]{2,1,0:T(8,128)(2,1)S(1)} %slice.25), channel_id=1, source_target_pairs={{0,8},{8,0},{16,24},{24,16},{1,9},{9,1},{17,25},{25,17},{2,10},{10... | collective-permute-start | bytes 442376 | tf_op jit(solution)/shard_map/ppermute | solution.py:279
  72.1 25.1 %collective-permute-start.17 = (bf16[128,1536]{1,0:T(8,128)(2,1)}, bf16[128,1536]{1,0:T(8,128)(2,1)}, u32[]{:S(2)}, u32[]{:S(2)}) collective-permute-start(bf16[128,1536]{1,0:T(8,128)(2,1)} %collective-permute-done.16.f0), channel_id=1, source_target_pairs={{0,1},{1,0},{2,3},{3,2},{4,5},{5,4},{6,7},{7,6},{8,9},{9,8},{10,11... | collective-permute-start | bytes 1179656 | tf_op jit(solution)/shard_map/ppermute | solution.py:286
  76.4 21.4 %collective-permute-start.15 = (bf16[128,1536]{1,0:T(8,128)(2,1)}, bf16[128,1536]{1,0:T(8,128)(2,1)}, u32[]{:S(2)}, u32[]{:S(2)}) collective-permute-start(bf16[128,1536]{1,0:T(8,128)(2,1)} %collective-permute-done.14.n0), channel_id=1, source_target_pairs={{0,1},{1,0},{2,3},{3,2},{4,5},{5,4},{6,7},{7,6},{8,9},{9,8},{10,11... | collective-permute-start | bytes 1179656 | tf_op jit(solution)/shard_map/ppermute | solution.py:286
  88.4 12.3 %collective-permute-start.13 = (bf16[1544,128]{1,0:T(8,128)(2,1)S(1)}, bf16[1544,128]{1,0:T(8,128)(2,1)S(1)}, u32[]{:S(2)}, u32[]{:S(2)}) collective-permute-start(bf16[1544,128]{1,0:T(8,128)(2,1)S(1)} %collective-permute-done.12.refs_2_), channel_id=1, source_target_pairs={{0,1},{1,0},{2,3},{3,2},{4,5},{5,4},{6,7},{7,6},{8,9},{9,8},{10,11... | collective-permute-start | bytes 1185800 | tf_op jit(solution)/shard_map/ppermute | solution.py:286
  88.4 12.3 %collective-permute-start.11 = (bf16[1544,128]{1,0:T(8,128)(2,1)S(1)}, bf16[1544,128]{1,0:T(8,128)(2,1)S(1)}, u32[]{:S(2)}, u32[]{:S(2)}) collective-permute-start(bf16[1544,128]{1,0:T(8,128)(2,1)S(1)} %collective-permute-done.10.refs_0_), channel_id=1, source_target_pairs={{0,1},{1,0},{2,3},{3,2},{4,5},{5,4},{6,7},{7,6},{8,9},{9,8},{10,11... | collective-permute-start | bytes 1185800 | tf_op jit(solution)/shard_map/ppermute | solution.py:286
  89.0 2.8 %copy-start.9 = (bf16[1544,128]{1,0:T(8,128)(2,1)S(1)}, bf16[1544,128]{1,0:T(8,128)(2,1)}, u32[]{:S(2)}) copy-start(bf16[1544,128]{1,0:T(8,128)(2,1)} %copy-done.8) | copy-start | bytes 1185796
  89.0 2.8 %copy-start.11 = (bf16[1544,128]{1,0:T(8,128)(2,1)S(1)}, bf16[1544,128]{1,0:T(8,128)(2,1)}, u32[]{:S(2)}) copy-start(bf16[1544,128]{1,0:T(8,128)(2,1)} %copy-done.10) | copy-start | bytes 1185796
  89.0 2.8 %copy-start.13 = (bf16[128,1536]{1,0:T(8,128)(2,1)S(1)}, bf16[128,1536]{1,0:T(8,128)(2,1)}, u32[]{:S(2)}) copy-start(bf16[128,1536]{1,0:T(8,128)(2,1)} %copy-done.12) | copy-start | bytes 1179652
  89.0 2.8 %copy-start.15 = (bf16[128,1536]{1,0:T(8,128)(2,1)S(1)}, bf16[128,1536]{1,0:T(8,128)(2,1)}, u32[]{:S(2)}) copy-start(bf16[128,1536]{1,0:T(8,128)(2,1)} %copy-done.14) | copy-start | bytes 1179652
  89.0 2.8 %copy-start.17 = (bf16[1,384,384]{2,1,0:T(8,128)(2,1)S(1)}, bf16[1,384,384]{2,1,0:T(8,128)(2,1)}, u32[]{:S(2)}) copy-start(bf16[1,384,384]{2,1,0:T(8,128)(2,1)} %copy-done.16) | copy-start | bytes 884740
  89.0 2.8 %copy-start.19 = (bf16[1,384,384]{2,1,0:T(8,128)(2,1)S(1)}, bf16[1,384,384]{2,1,0:T(8,128)(2,1)}, u32[]{:S(2)}) copy-start(bf16[1,384,384]{2,1,0:T(8,128)(2,1)} %copy-done.18) | copy-start | bytes 884740
  91.7 15.2 %collective-permute-start.26 = (bf16[128,1536]{1,0:T(8,128)(2,1)S(1)}, bf16[128,1536]{1,0:T(8,128)(2,1)S(1)}, u32[]{:S(2)}, u32[]{:S(2)}) collective-permute-start(bf16[128,1536]{1,0:T(8,128)(2,1)S(1)} %add.30.x0), channel_id=1, source_target_pairs={{0,1},{1,0},{2,3},{3,2},{4,5},{5,4},{6,7},{7,6},{8,9},{9,8},{10,11... | collective-permute-start | bytes 1179656 | tf_op jit(solution)/shard_map/ppermute | solution.py:286
  97.3 10.5 %collective-permute-start.23 = (bf16[1544,128]{1,0:T(8,128)(2,1)S(1)}, bf16[1544,128]{1,0:T(8,128)(2,1)S(1)}, u32[]{:S(2)}, u32[]{:S(2)}) collective-permute-start(bf16[1544,128]{1,0:T(8,128)(2,1)S(1)} %add.29.y0), channel_id=1, source_target_pairs={{0,1},{1,0},{2,3},{3,2},{4,5},{5,4},{6,7},{7,6},{8,9},{9,8},{10,11... | collective-permute-start | bytes 1185800 | tf_op jit(solution)/shard_map/ppermute | solution.py:286
  110.8 3.2 %collective-permute-start.27 = (bf16[1544,128]{1,0:T(8,128)(2,1)S(1)}, bf16[1544,128]{1,0:T(8,128)(2,1)S(1)}, u32[]{:S(2)}, u32[]{:S(2)}) collective-permute-start(bf16[1544,128]{1,0:T(8,128)(2,1)S(1)} %get-tuple-element.74), channel_id=1, source_target_pairs={{0,1},{1,0},{2,3},{3,2},{4,5},{5,4},{6,7},{7,6},{8,9},{9,8},{10,11... | collective-permute-start | bytes 1185800 | tf_op jit(solution)/shard_map/ppermute | solution.py:286
  110.9 18.5 %collective-permute-start.18 = (bf16[2,1544,128]{2,1,0:T(8,128)(2,1)S(1)}, bf16[2,1544,128]{2,1,0:T(8,128)(2,1)S(1)}, u32[]{:S(2)}, u32[]{:S(2)}) collective-permute-start(bf16[2,1544,128]{2,1,0:T(8,128)(2,1)S(1)} %get-tuple-element.58), channel_id=1, source_target_pairs={{0,1},{1,0},{2,3},{3,2},{4,5},{5,4},{6,7},{7,6},{8,9},{9,8},{10,11... | collective-permute-start | bytes 2371592 | tf_op jit(solution)/shard_map/ppermute | solution.py:286
  111.3 18.8 %collective-permute-start.9 = (bf16[1544,128]{1,0:T(8,128)(2,1)S(1)}, bf16[1544,128]{1,0:T(8,128)(2,1)S(1)}, u32[]{:S(2)}, u32[]{:S(2)}) collective-permute-start(bf16[1544,128]{1,0:T(8,128)(2,1)S(1)} %get-tuple-element.51), channel_id=1, source_target_pairs={{0,1},{1,0},{2,3},{3,2},{4,5},{5,4},{6,7},{7,6},{8,9},{9,8},{10,11... | collective-permute-start | bytes 1185800 | tf_op jit(solution)/shard_map/ppermute | solution.py:286
  111.4 11.7 %collective-permute-start.33 = (bf16[176,1152]{1,0:T(8,128)(2,1)S(1)}, bf16[176,1152]{1,0:T(8,128)(2,1)S(1)}, u32[]{:S(2)}, u32[]{:S(2)}) collective-permute-start(bf16[176,1152]{1,0:T(8,128)(2,1)S(1)} %get-tuple-element.85), channel_id=1, source_target_pairs={{0,8},{8,0},{16,24},{24,16},{1,9},{9,1},{17,25},{25,17},{2,10},{10... | collective-permute-start | bytes 1216520 | tf_op jit(solution)/shard_map/ppermute | solution.py:279
  111.9 13.8 %collective-permute-start.31 = (bf16[208,1152]{1,0:T(8,128)(2,1)S(1)}, bf16[208,1152]{1,0:T(8,128)(2,1)S(1)}, u32[]{:S(2)}, u32[]{:S(2)}) collective-permute-start(bf16[208,1152]{1,0:T(8,128)(2,1)S(1)} %get-tuple-element.83), channel_id=1, source_target_pairs={{0,16},{8,24},{16,0},{24,8},{1,17},{9,25},{17,1},{25,9},{2,18},{10... | collective-permute-start | bytes 1437704 | tf_op jit(solution)/shard_map/ppermute | solution.py:279
  114.0 22.0 %collective-permute-start.30 = (bf16[208,1152]{1,0:T(8,128)(2,1)S(1)}, bf16[208,1152]{1,0:T(8,128)(2,1)S(1)}, u32[]{:S(2)}, u32[]{:S(2)}) collective-permute-start(bf16[208,1152]{1,0:T(8,128)(2,1)S(1)} %get-tuple-element.81), channel_id=1, source_target_pairs={{0,16},{8,24},{16,0},{24,8},{1,17},{9,25},{17,1},{25,9},{2,18},{10... | collective-permute-start | bytes 1437704 | tf_op jit(solution)/shard_map/ppermute | solution.py:279
  123.1 12.2 %collective-permute-start.29 = (bf16[176,1152]{1,0:T(8,128)(2,1)S(1)}, bf16[176,1152]{1,0:T(8,128)(2,1)S(1)}, u32[]{:S(2)}, u32[]{:S(2)}) collective-permute-start(bf16[176,1152]{1,0:T(8,128)(2,1)S(1)} %get-tuple-element.80), channel_id=1, source_target_pairs={{0,8},{8,0},{16,24},{24,16},{1,9},{9,1},{17,25},{25,17},{2,10},{10... | collective-permute-start | bytes 1216520 | tf_op jit(solution)/shard_map/ppermute | solution.py:279
  125.8 19.6 %collective-permute-start.28 = (bf16[1544,128]{1,0:T(8,128)(2,1)S(1)}, bf16[1544,128]{1,0:T(8,128)(2,1)S(1)}, u32[]{:S(2)}, u32[]{:S(2)}) collective-permute-start(bf16[1544,128]{1,0:T(8,128)(2,1)S(1)} %add_convert_fusion.2), channel_id=1, source_target_pairs={{0,6},{1,7},{2,4},{3,5},{4,2},{5,3},{6,0},{7,1},{8,14},{9,15},{10,... | collective-permute-start | bytes 1185800 | tf_op jit(solution)/shard_map/ppermute | solution.py:283
  129.4 14.5 %collective-permute-start.34 = (bf16[176,1152]{1,0:T(8,128)(2,1)S(1)}, bf16[176,1152]{1,0:T(8,128)(2,1)S(1)}, u32[]{:S(2)}, u32[]{:S(2)}) collective-permute-start(bf16[176,1152]{1,0:T(8,128)(2,1)S(1)} %add_convert_fusion.1), channel_id=1, source_target_pairs={{0,16},{8,24},{16,0},{24,8},{1,17},{9,25},{17,1},{25,9},{2,18},{10... | collective-permute-start | bytes 1216520 | tf_op jit(solution)/shard_map/ppermute | solution.py:279
  130.0 9.6 %copy-start = (bf16[1,384,768]{2,1,0:T(8,128)(2,1)S(1)}, bf16[1,384,768]{2,1,0:T(8,128)(2,1)}, u32[]{:S(2)}) copy-start(bf16[1,384,768]{2,1,0:T(8,128)(2,1)} %min_ref.1) | copy-start | bytes 1769476
  130.0 9.6 %copy-start.3 = (bf16[1,384,384]{2,1,0:T(8,128)(2,1)S(1)}, bf16[1,384,384]{2,1,0:T(8,128)(2,1)}, u32[]{:S(2)}) copy-start(bf16[1,384,384]{2,1,0:T(8,128)(2,1)} %mout_ref.1) | copy-start | bytes 884740
  130.2 14.1 %collective-permute-start.32 = (bf16[208,1152]{1,0:T(8,128)(2,1)S(1)}, bf16[208,1152]{1,0:T(8,128)(2,1)S(1)}, u32[]{:S(2)}, u32[]{:S(2)}) collective-permute-start(bf16[208,1152]{1,0:T(8,128)(2,1)S(1)} %add_convert_fusion), channel_id=1, source_target_pairs={{0,8},{8,0},{16,24},{24,16},{1,9},{9,1},{17,25},{25,17},{2,10},{10... | collective-permute-start | bytes 1437704 | tf_op jit(solution)/shard_map/ppermute | solution.py:279
  135.4 12.0 %collective-permute-start.19 = (bf16[1544,128]{1,0:T(8,128)(2,1)S(1)}, bf16[1544,128]{1,0:T(8,128)(2,1)S(1)}, u32[]{:S(2)}, u32[]{:S(2)}) collective-permute-start(bf16[1544,128]{1,0:T(8,128)(2,1)S(1)} %get-tuple-element.89), channel_id=1, source_target_pairs={{0,2},{1,3},{2,0},{3,1},{4,6},{5,7},{6,4},{7,5},{8,10},{9,11},{10,... | collective-permute-start | bytes 1185800 | tf_op jit(solution)/shard_map/ppermute | solution.py:283
  136.0 24.5 %collective-permute-start.20 = (bf16[1544,128]{1,0:T(8,128)(2,1)S(1)}, bf16[1544,128]{1,0:T(8,128)(2,1)S(1)}, u32[]{:S(2)}, u32[]{:S(2)}) collective-permute-start(bf16[1544,128]{1,0:T(8,128)(2,1)S(1)} %get-tuple-element.88), channel_id=1, source_target_pairs={{0,4},{1,5},{2,6},{3,7},{4,0},{5,1},{6,2},{7,3},{8,12},{9,13},{10,... | collective-permute-start | bytes 1185800 | tf_op jit(solution)/shard_map/ppermute | solution.py:283
  139.9 20.7 %copy-start.6 = (s32[128,4]{0,1:T(4,128)S(1)}, s32[128,4]{0,1:T(4,128)}, u32[]{:S(2)}) copy-start(s32[128,4]{0,1:T(4,128)} %param.9) | copy-start | bytes 6148
  (13 other events, 10.6 us)

commit v7 on v6

--- a/solution.py
+++ b/solution.py
@@ -194,9 +194,9 @@
         at = rows.stop
 
 
-def grad_kernel(ids_ref, y0, y1, xs, silu, slope, hidden, wout, acc_in, acc_out, *refs):
+def grad_kernel(y0, y1, xs, silu, slope, hidden, wout, acc_in, acc_out, *refs):
     r3a_ref, r3b_ref, dgus, chs, ys, gate_ref = refs
-    rep, expert = ids_ref[0], ids_ref[1]
+    rep, expert = lax.axis_index("rep"), lax.axis_index("expert")
     tok, width = ys.shape[0] // 2, ys.shape[1]
     ffn = wout.shape[0]
     ys[0:tok, :] = unstack(y0, width)
@@ -213,21 +213,21 @@
     shard_grads((r3a_ref, r3b_ref), acc_in, acc_out, xs, ys, dgus, chs, rep ^ 3)
 
 
-def other_grads_kernel(ids_ref, xs, ys, dgus, chs, acc_in, acc_out, mine_ref, r1a_ref, r1b_ref, r2a_ref, r2b_ref):
-    rep = ids_ref[0]
+def other_grads_kernel(xs, ys, dgus, chs, acc_in, acc_out, mine_ref, r1a_ref, r1b_ref, r2a_ref, r2b_ref):
+    rep = lax.axis_index("rep")
     args = (acc_in, acc_out, xs, ys, dgus, chs)
     shard_grads((r1a_ref, r1b_ref), *args, rep ^ 1)
     shard_grads((r2a_ref, r2b_ref), *args, rep ^ 2)
     shard_grads((mine_ref,), *args, rep)
 
 
-def rows_kernel(ids_ref, dgus, win, gate_ref, keep_ref, give_ref):
+def rows_kernel(dgus, win, gate_ref, keep_ref, give_ref):
     tok, width = dgus.shape[0] // 2, win.shape[0]
     experts = keep_ref.shape[0] - width // 128 * tok
     row_grad = dot(dgus[...], win[...], 1, 1).astype(bf16)
     for i, out in enumerate((keep_ref, give_ref)):
         part = slice(i * tok, (i + 1) * tok)
-        write_rows(out, row_grad[part], gate_table(gate_ref[part, :], experts, ids_ref[1]))
+        write_rows(out, row_grad[part], gate_table(gate_ref[part, :], experts, lax.axis_index("expert")))
 
 
 def combine_kernel(routes_ref, p0, p1, p2, p3, token_ref, gate_ref):
@@ -382,25 +382,23 @@
     part_b = shard - part_a
     r3a, r3b, dgus, chs, ys, gate_last = call(
         grad_kernel,
-        [ids, cross_y, cross_yp, xs, silu, slope, hidden, wout]
+        [cross_y, cross_yp, xs, silu, slope, hidden, wout]
         + [acc_in, acc_out],
         [((part_a, cols), bf16), ((part_b, cols), bf16)]
         + [((rows, both_w), bf16), ((rows, ffn), bf16), ((rows, width), bf16), ((rows, 1), f32)],
         mib=8,
-        scalars=1,
         flops=rows * width * both_w * 2,
     )
     s3a = over_rep(r3a, 2)
     s3b = over_rep(r3b, 1)
     mine, r1a, r1b, r2a, r2b = call(
         other_grads_kernel,
-        [ids, xs, ys, dgus, chs, acc_in, acc_out],
+        [xs, ys, dgus, chs, acc_in, acc_out],
         [((shard, cols), bf16)] + [((part_a, cols), bf16), ((part_b, cols), bf16)] * 2,
         mib=8,
-        scalars=1,
         flops=2 * rows * width * both_w,
     )
-    keep2, give2 = call(rows_kernel, [ids, dgus, win, gate_last], [block, block], scalars=1)
+    keep2, give2 = call(rows_kernel, [dgus, win, gate_last], [block, block])
     got2 = partner(give2)
     t2a = over_rep(r2a, 2)
     t1b = over_rep(r1b, 1)

time: 162 us -> 161 us (level)
  no operation moved by 1% of the time
where the time goes in v7:
time: 161 us; the launch traced here: 160 us
  waiting for transfers between devices  77.4 us (48%)
  starting transfers between devices  47.1 us (29%)
  Pallas kernels  20.3 us (13%)
  local copies, waits for them, and re-layouts  11.5 us (7%)
  other arithmetic  3.28 us (2%)
    ppermute x11, waiting for transfers between devices, over_chips(): return lax.ppermute(value, 'expert', pairs)  51.5 us
    ppermute x11, starting transfers between devices, over_chips(): return lax.ppermute(value, 'expert', pairs)  31.8 us
    ppermute x13, waiting for transfers between devices, over_rep(): return lax.ppermute(value, 'rep', [(i, i ^ bits) for i in range(4)])  25.8 us
    pallas_call x12, Pallas kernels, call(): pl.pallas_call(kernel, out_shape=[jax.ShapeDtypeStruct(shape, dtype) for...  20.3 us
    ppermute x13, starting transfers between devices, over_rep(): return lax.ppermute(value, 'rep', [(i, i ^ bits) for i in range(4)])  13.4 us
    unnamed x52, local copies, waits for them, and re-layouts  10.7 us
  transfers between devices with their start and end apart: 35, of which 14 were waited for; matrix products, arithmetic and copies ran while one was open for 3% of the time, Pallas kernels for 11%

profile of v7, /device:TPU:0, one launch (start us, length us, event | category | flops | bytes accessed | tf_op | source)
XLA Modules:
  0.0 160.5 jit_solution(424679831076575584)
XLA Ops:
  0.6 3.1 %collective-permute-start.7 = (bf16[1,384,384]{2,1,0:T(8,128)(2,1)}, bf16[1,384,384]{2,1,0:T(8,128)(2,1)S(1)}, u32[]{:S(2)}, u32[]{:S(2)}) collective-permute-start(bf16[1,384,384]{2,1,0:T(8,128)(2,1)} %wout_hbm.1), channel_id=1, source_target_pairs={{0,16},{8,24},{16,0},{24,8},{1,17},{9,25},{17,1},{25,9},{2,18},{10... | collective-permute-start | bytes 884744 | tf_op jit(solution)/shard_map/ppermute | solution.py:279
  3.7 1.0 copy-done.1
  4.7 1.0 copy-done.2
  5.7 1.0 copy-done.4
  8.0 1.5 shard_map.111
  10.2 0.8 copy-done.12
  11.0 1.5 collective-permute-start.6
  12.5 2.6 %collective-permute-start.16 = (bf16[128,1536]{1,0:T(8,128)(2,1)S(1)}, bf16[128,1536]{1,0:T(8,128)(2,1)}, u32[]{:S(2)}, u32[]{:S(2)}) collective-permute-start(bf16[128,1536]{1,0:T(8,128)(2,1)S(1)} %copy-done.2), channel_id=1, source_target_pairs={{0,4},{1,5},{2,6},{3,7},{4,0},{5,1},{6,2},{7,3},{8,12},{9,13},{10,... | collective-permute-start | bytes 1179656 | tf_op jit(solution)/shard_map/ppermute | solution.py:283
  15.1 1.6 collective-permute-start.14
  17.3 3.1 %collective-permute-done.6.refs_6_ = bf16[1,384,384]{2,1,0:T(8,128)(2,1)S(1)} collective-permute-done((bf16[1,384,384]{2,1,0:T(8,128)(2,1)S(1)}, bf16[1,384,384]{2,1,0:T(8,128)(2,1)S(1)}, u32[]{:S(2)}, u32[]{:S(2)}) %collective-permute-start.6) | collective-permute-done | bytes 294944 | tf_op jit(solution)/shard_map/ppermute | solution.py:279
  20.4 0.7 copy-done.20
  21.1 0.7 copy-done.14
  21.9 1.5 collective-permute-start.2
  23.4 10.6 %collective-permute-done.16.f0 = bf16[128,1536]{1,0:T(8,128)(2,1)} collective-permute-done((bf16[128,1536]{1,0:T(8,128)(2,1)S(1)}, bf16[128,1536]{1,0:T(8,128)(2,1)}, u32[]{:S(2)}, u32[]{:S(2)}) %collective-permute-start.16) | collective-permute-done | bytes 393248 | tf_op jit(solution)/shard_map/ppermute | solution.py:283
  34.8 16.5 %collective-permute-start.10 = (bf16[1544,128]{1,0:T(8,128)(2,1)S(1)}, bf16[1544,128]{1,0:T(8,128)(2,1)S(1)}, u32[]{:S(2)}, u32[]{:S(2)}) collective-permute-start(bf16[1544,128]{1,0:T(8,128)(2,1)S(1)} %get-tuple-element.47.y0), channel_id=1, source_target_pairs={{0,2},{1,3},{2,0},{3,1},{4,6},{5,7},{6,4},{7,5},{8,10},{9,11},{10,... | collective-permute-start | bytes 1185800 | tf_op jit(solution)/shard_map/ppermute | solution.py:283
  52.0 7.3 %collective-permute-done.12.refs_2_ = bf16[1544,128]{1,0:T(8,128)(2,1)S(1)} collective-permute-done((bf16[1544,128]{1,0:T(8,128)(2,1)S(1)}, bf16[1544,128]{1,0:T(8,128)(2,1)S(1)}, u32[]{:S(2)}, u32[]{:S(2)}) %collective-permute-start.12) | collective-permute-done | bytes 395296 | tf_op jit(solution)/shard_map/ppermute | solution.py:283
  59.8 0.7 copy-done.16
  60.5 6.4 %collective-permute-done.10.refs_0_ = bf16[1544,128]{1,0:T(8,128)(2,1)S(1)} collective-permute-done((bf16[1544,128]{1,0:T(8,128)(2,1)S(1)}, bf16[1544,128]{1,0:T(8,128)(2,1)S(1)}, u32[]{:S(2)}, u32[]{:S(2)}) %collective-permute-start.10) | collective-permute-done | bytes 395296 | tf_op jit(solution)/shard_map/ppermute | solution.py:283
  66.9 1.3 collective-permute-start.21
  68.2 1.3 collective-permute-start.24
  69.5 0.8 slice.24
  71.4 0.7 copy-done.22
  72.1 4.3 %collective-permute-done.5.refs_4_ = bf16[1,96,768]{2,1,0:T(8,128)(2,1)S(1)} collective-permute-done((bf16[1,96,768]{2,1,0:T(8,128)(2,1)S(1)}, bf16[1,96,768]{2,1,0:T(8,128)(2,1)S(1)}, u32[]{:S(2)}, u32[]{:S(2)}) %collective-permute-start.5) | collective-permute-done | bytes 147488 | tf_op jit(solution)/shard_map/ppermute | solution.py:279
  76.4 12.0 %collective-permute-done.24 = bf16[128,1536]{1,0:T(8,128)(2,1)} collective-permute-done((bf16[128,1536]{1,0:T(8,128)(2,1)}, bf16[128,1536]{1,0:T(8,128)(2,1)}, u32[]{:S(2)}, u32[]{:S(2)}) %collective-permute-start.24) | collective-permute-done | bytes 393248 | tf_op jit(solution)/shard_map/ppermute | solution.py:283
  89.1 1.3 add.30.x0
  90.5 1.2 add.29.y0
  91.8 1.0 copy-done.21
  92.8 1.0 copy-done.23
  93.8 3.6 %shard_map.112 = (bf16[1544,128]{1,0:T(8,128)(2,1)S(1)}, bf16[1544,128]{1,0:T(8,128)(2,1)S(1)}, bf16[256,768]{1,0:T(8,128)(2,1)S(1)}, bf16[256,384]{1,0:T(8,128)...) custom-call(s32[2]{0:T(128)S(1)} %pad_add_fusion.ids_ref, bf16[128,1536]{1,0:T(8,128)(2,1)S(1)} %copy-done.13, ...), custom_call_target="tpu_custom_call" | custom-call | flops 1509949440 | bytes 4194304 | tf_op jit(solution)/shard_map/pallas_call | solution.py:23
  97.9 2.9 %shard_map.113 = (bf16[512,1536]{1,0:T(8,128)(2,1)S(1)}, f32[512,384]{1,0:T(8,128)S(1)}, f32[512,384]{1,0:T(8,128)S(1)}, bf16[512,384]{1,0:T(8,128)(2,1)S(1)}) custom-call(bf16[128,1536]{1,0:T(8,128)(2,1)} %collective-permute-done.14.n0, bf16[128,1536]{1,0:T(8,128)(2,1)} %collective-permute-done.15.n1, bf16[128,1536]{1,0:T(8,128)(2,1)} %collective-permute-done.16.f0, ...), custom_call_target="tpu_custom_call" | custom-call | flops 1207959552 | bytes 4194304 | tf_op jit(solution)/shard_map/pallas_call | solution.py:23
  100.8 3.1 %shard_map.114 = (bf16[2,1544,128]{2,1,0:T(8,128)(2,1)S(1)}, bf16[2,1544,128]{2,1,0:T(8,128)(2,1)S(1)}, bf16[512,1536]{1,0:T(8,128)(2,1)S(1)}, bf16[512,768]{1,0:T(8,128)(2,1)S(1)}, bf16[512,384]{1,0:T(8,128)(2,1)S(1)}) custom-call(s32[2]{0:T(128)S(1)} %pad_add_fusion.ids_ref, bf16[1544,128]{1,0:T(8,128)(2,1)S(1)} %collective-permute-done.10.refs_0_, ...), custom_call_target="tpu_custom_call" | custom-call | flops 1509949440 | bytes 4194304 | tf_op jit(solution)/shard_map/pallas_call | solution.py:23
  103.9 3.0 %shard_map.116 = (f32[1536,768]{1,0:T(8,128)S(1)}, f32[384,1536]{1,0:T(8,128)S(1)}) custom-call(bf16[128,1536]{1,0:T(8,128)(2,1)S(1)} %copy-done.13, bf16[128,1536]{1,0:T(8,128)(2,1)S(1)} %copy-done.15, bf16[1544,128]{1,0:T(8,128)(2,1)S(1)} %copy-done.9, bf16[1544,128]{1,0:T(8,128)(2,1)S(1)} %copy-done.11, bf16[256,768]{1,0:T(8,128)(2,1)S(1)} %get-tuple-element.63.own_dgu, ...), custom_call_target="tpu_custom_call" | custom-call | flops 3019898880 | bytes 4194304 | tf_op jit(solution)/shard_map/pallas_call | solution.py:23
  106.9 0.9 shard_map.115
  107.8 1.1 shard_map.117
  108.9 0.8 shard_map.118
  111.4 1.1 shard_map.120
  112.5 1.6 %collective-permute-start.30 = (bf16[208,1152]{1,0:T(8,128)(2,1)S(1)}, bf16[208,1152]{1,0:T(8,128)(2,1)S(1)}, u32[]{:S(2)}, u32[]{:S(2)}) collective-permute-start(bf16[208,1152]{1,0:T(8,128)(2,1)S(1)} %get-tuple-element.81), channel_id=1, source_target_pairs={{0,16},{8,24},{16,0},{24,8},{1,17},{9,25},{17,1},{25,9},{2,18},{10... | collective-permute-start | bytes 1437704 | tf_op jit(solution)/shard_map/ppermute | solution.py:279
  114.2 7.9 %collective-permute-done.33 = bf16[176,1152]{1,0:T(8,128)(2,1)S(1)} collective-permute-done((bf16[176,1152]{1,0:T(8,128)(2,1)S(1)}, bf16[176,1152]{1,0:T(8,128)(2,1)S(1)}, u32[]{:S(2)}, u32[]{:S(2)}) %collective-permute-start.33) | collective-permute-done | bytes 405536 | tf_op jit(solution)/shard_map/ppermute | solution.py:279
  122.7 2.0 %collective-permute-done.31 = bf16[208,1152]{1,0:T(8,128)(2,1)S(1)} collective-permute-done((bf16[208,1152]{1,0:T(8,128)(2,1)S(1)}, bf16[208,1152]{1,0:T(8,128)(2,1)S(1)}, u32[]{:S(2)}, u32[]{:S(2)}) %collective-permute-start.31) | collective-permute-done | bytes 479264 | tf_op jit(solution)/shard_map/ppermute | solution.py:279
  124.8 3.5 %collective-permute-start.28 = (bf16[1544,128]{1,0:T(8,128)(2,1)S(1)}, bf16[1544,128]{1,0:T(8,128)(2,1)S(1)}, u32[]{:S(2)}, u32[]{:S(2)}) collective-permute-start(bf16[1544,128]{1,0:T(8,128)(2,1)S(1)} %add_convert_fusion.2), channel_id=1, source_target_pairs={{0,6},{1,7},{2,4},{3,5},{4,2},{5,3},{6,0},{7,1},{8,14},{9,15},{10,... | collective-permute-start | bytes 1185800 | tf_op jit(solution)/shard_map/ppermute | solution.py:283
  129.2 1.6 collective-permute-start.32
  130.7 3.6 %collective-permute-done.29.t1b_ref = bf16[176,1152]{1,0:T(8,128)(2,1)S(1)} collective-permute-done((bf16[176,1152]{1,0:T(8,128)(2,1)S(1)}, bf16[176,1152]{1,0:T(8,128)(2,1)S(1)}, u32[]{:S(2)}, u32[]{:S(2)}) %collective-permute-start.29) | collective-permute-done | bytes 405536 | tf_op jit(solution)/shard_map/ppermute | solution.py:279
  135.0 3.4 %collective-permute-start.20 = (bf16[1544,128]{1,0:T(8,128)(2,1)S(1)}, bf16[1544,128]{1,0:T(8,128)(2,1)S(1)}, u32[]{:S(2)}, u32[]{:S(2)}) collective-permute-start(bf16[1544,128]{1,0:T(8,128)(2,1)S(1)} %get-tuple-element.88), channel_id=1, source_target_pairs={{0,4},{1,5},{2,6},{3,7},{4,0},{5,1},{6,2},{7,3},{8,12},{9,13},{10,... | collective-permute-start | bytes 1185800 | tf_op jit(solution)/shard_map/ppermute | solution.py:283
  138.9 4.0 %collective-permute-done.34.t2b_ref = bf16[176,1152]{1,0:T(8,128)(2,1)S(1)} collective-permute-done((bf16[176,1152]{1,0:T(8,128)(2,1)S(1)}, bf16[176,1152]{1,0:T(8,128)(2,1)S(1)}, u32[]{:S(2)}, u32[]{:S(2)}) %collective-permute-start.34) | collective-permute-done | bytes 405536 | tf_op jit(solution)/shard_map/ppermute | solution.py:279
  143.2 1.1 shard_map.122
  144.3 2.1 %collective-permute-done.19.p1 = bf16[1544,128]{1,0:T(8,128)(2,1)S(1)} collective-permute-done((bf16[1544,128]{1,0:T(8,128)(2,1)S(1)}, bf16[1544,128]{1,0:T(8,128)(2,1)S(1)}, u32[]{:S(2)}, u32[]{:S(2)}) %collective-permute-start.19) | collective-permute-done | bytes 395296 | tf_op jit(solution)/shard_map/ppermute | solution.py:283
  146.4 13.1 %collective-permute-done.20.p2 = bf16[1544,128]{1,0:T(8,128)(2,1)S(1)} collective-permute-done((bf16[1544,128]{1,0:T(8,128)(2,1)S(1)}, bf16[1544,128]{1,0:T(8,128)(2,1)S(1)}, u32[]{:S(2)}, u32[]{:S(2)}) %collective-permute-start.20) | collective-permute-done | bytes 395296 | tf_op jit(solution)/shard_map/ppermute | solution.py:283
  159.5 1.0 shard_map.119
  (96 shorter events, 12.0 us)
Async XLA Ops:
  0.6 16.0 %collective-permute-start.7 = (bf16[1,384,384]{2,1,0:T(8,128)(2,1)}, bf16[1,384,384]{2,1,0:T(8,128)(2,1)S(1)}, u32[]{:S(2)}, u32[]{:S(2)}) collective-permute-start(bf16[1,384,384]{2,1,0:T(8,128)(2,1)} %wout_hbm.1), channel_id=1, source_target_pairs={{0,16},{8,24},{16,0},{24,8},{1,17},{9,25},{17,1},{25,9},{2,18},{10... | collective-permute-start | bytes 884744 | tf_op jit(solution)/shard_map/ppermute | solution.py:279
  10.2 66.2 %copy-start.8 = (bf16[1544,128]{1,0:T(8,128)(2,1)}, bf16[1544,128]{1,0:T(8,128)(2,1)S(1)}, u32[]{:S(2)}) copy-start(bf16[1544,128]{1,0:T(8,128)(2,1)S(1)} %get-tuple-element.47.y0) | copy-start | bytes 1185796
  10.2 10.9 %collective-permute-start = (bf16[128,1536]{1,0:T(8,128)(2,1)S(1)}, bf16[128,1536]{1,0:T(8,128)(2,1)S(1)}, u32[]{:S(2)}, u32[]{:S(2)}) collective-permute-start(bf16[128,1536]{1,0:T(8,128)(2,1)S(1)} %get-tuple-element.46.x0), channel_id=1, source_target_pairs={{0,1},{1,0},{2,3},{3,2},{4,5},{5,4},{6,7},{7,6},{8,9},{9,8},{10,11... | collective-permute-start | bytes 1179656 | tf_op jit(solution)/shard_map/ppermute | solution.py:286
  11.0 9.4 %collective-permute-start.6 = (bf16[1,384,384]{2,1,0:T(8,128)(2,1)S(1)}, bf16[1,384,384]{2,1,0:T(8,128)(2,1)S(1)}, u32[]{:S(2)}, u32[]{:S(2)}) collective-permute-start(bf16[1,384,384]{2,1,0:T(8,128)(2,1)S(1)} %copy-done.4), channel_id=1, source_target_pairs={{0,8},{8,0},{16,24},{24,16},{1,9},{9,1},{17,25},{25,17},{2,10},{10... | collective-permute-start | bytes 884744 | tf_op jit(solution)/shard_map/ppermute | solution.py:279
  12.5 21.5 %collective-permute-start.16 = (bf16[128,1536]{1,0:T(8,128)(2,1)S(1)}, bf16[128,1536]{1,0:T(8,128)(2,1)}, u32[]{:S(2)}, u32[]{:S(2)}) collective-permute-start(bf16[128,1536]{1,0:T(8,128)(2,1)S(1)} %copy-done.2), channel_id=1, source_target_pairs={{0,4},{1,5},{2,6},{3,7},{4,0},{5,1},{6,2},{7,3},{8,12},{9,13},{10,... | collective-permute-start | bytes 1179656 | tf_op jit(solution)/shard_map/ppermute | solution.py:283
  15.1 19.4 %collective-permute-start.14 = (bf16[128,1536]{1,0:T(8,128)(2,1)S(1)}, bf16[128,1536]{1,0:T(8,128)(2,1)}, u32[]{:S(2)}, u32[]{:S(2)}) collective-permute-start(bf16[128,1536]{1,0:T(8,128)(2,1)S(1)} %copy-done.2), channel_id=1, source_target_pairs={{0,2},{1,3},{2,0},{3,1},{4,6},{5,7},{6,4},{7,5},{8,10},{9,11},{10,... | collective-permute-start | bytes 1179656 | tf_op jit(solution)/shard_map/ppermute | solution.py:283
  16.7 18.1 %collective-permute-start.25 = (bf16[128,1536]{1,0:T(8,128)(2,1)S(1)}, bf16[128,1536]{1,0:T(8,128)(2,1)S(1)}, u32[]{:S(2)}, u32[]{:S(2)}) collective-permute-start(bf16[128,1536]{1,0:T(8,128)(2,1)S(1)} %copy-done.2), channel_id=1, source_target_pairs={{2,4},{3,5},{4,2},{5,3},{10,12},{11,13},{12,10},{13,11},{18,20},{1... | collective-permute-start | bytes 1179656 | tf_op jit(solution)/shard_map/ppermute | solution.py:283
  21.1 30.2 %collective-permute-start.1 = (bf16[1544,128]{1,0:T(8,128)(2,1)S(1)}, bf16[1544,128]{1,0:T(8,128)(2,1)S(1)}, u32[]{:S(2)}, u32[]{:S(2)}) collective-permute-start(bf16[1544,128]{1,0:T(8,128)(2,1)S(1)} %get-tuple-element.47.y0), channel_id=1, source_target_pairs={{0,1},{1,0},{2,3},{3,2},{4,5},{5,4},{6,7},{7,6},{8,9},{9,8},{10,11... | collective-permute-start | bytes 1185800 | tf_op jit(solution)/shard_map/ppermute | solution.py:286
  21.9 46.3 %collective-permute-start.2 = (bf16[1,384,768]{2,1,0:T(8,128)(2,1)}, bf16[1,384,768]{2,1,0:T(8,128)(2,1)S(1)}, u32[]{:S(2)}, u32[]{:S(2)}) collective-permute-start(bf16[1,384,768]{2,1,0:T(8,128)(2,1)} %win_hbm.1), channel_id=1, source_target_pairs={{0,8},{8,0},{16,24},{24,16},{1,9},{9,1},{17,25},{25,17},{2,10},{10... | collective-permute-start | bytes 1769480 | tf_op jit(solution)/shard_map/ppermute | solution.py:279
  34.0 36.4 %collective-permute-start.3 = (bf16[1,384,768]{2,1,0:T(8,128)(2,1)}, bf16[1,384,768]{2,1,0:T(8,128)(2,1)S(1)}, u32[]{:S(2)}, u32[]{:S(2)}) collective-permute-start(bf16[1,384,768]{2,1,0:T(8,128)(2,1)} %win_hbm.1), channel_id=1, source_target_pairs={{0,16},{8,24},{16,0},{24,8},{1,17},{9,25},{17,1},{25,9},{2,18},{10... | collective-permute-start | bytes 1769480 | tf_op jit(solution)/shard_map/ppermute | solution.py:279
  34.5 24.8 %collective-permute-start.12 = (bf16[1544,128]{1,0:T(8,128)(2,1)S(1)}, bf16[1544,128]{1,0:T(8,128)(2,1)S(1)}, u32[]{:S(2)}, u32[]{:S(2)}) collective-permute-start(bf16[1544,128]{1,0:T(8,128)(2,1)S(1)} %get-tuple-element.47.y0), channel_id=1, source_target_pairs={{0,4},{1,5},{2,6},{3,7},{4,0},{5,1},{6,2},{7,3},{8,12},{9,13},{10,... | collective-permute-start | bytes 1185800 | tf_op jit(solution)/shard_map/ppermute | solution.py:283
  34.8 33.5 %copy-start.25 = (bf16[128,1536]{1,0:T(8,128)(2,1)}, bf16[128,1536]{1,0:T(8,128)(2,1)S(1)}, u32[]{:S(2)}) copy-start(bf16[128,1536]{1,0:T(8,128)(2,1)S(1)} %collective-permute-done.25) | copy-start | bytes 1179652
  34.8 32.1 %collective-permute-start.10 = (bf16[1544,128]{1,0:T(8,128)(2,1)S(1)}, bf16[1544,128]{1,0:T(8,128)(2,1)S(1)}, u32[]{:S(2)}, u32[]{:S(2)}) collective-permute-start(bf16[1544,128]{1,0:T(8,128)(2,1)S(1)} %get-tuple-element.47.y0), channel_id=1, source_target_pairs={{0,2},{1,3},{2,0},{3,1},{4,6},{5,7},{6,4},{7,5},{8,10},{9,11},{10,... | collective-permute-start | bytes 1185800 | tf_op jit(solution)/shard_map/ppermute | solution.py:283
  51.3 37.1 %copy-start.10 = (bf16[1544,128]{1,0:T(8,128)(2,1)}, bf16[1544,128]{1,0:T(8,128)(2,1)S(1)}, u32[]{:S(2)}) copy-start(bf16[1544,128]{1,0:T(8,128)(2,1)S(1)} %collective-permute-done.1.y1) | copy-start | bytes 1185796
  51.3 19.5 %collective-permute-start.22 = (bf16[1544,128]{1,0:T(8,128)(2,1)S(1)}, bf16[1544,128]{1,0:T(8,128)(2,1)S(1)}, u32[]{:S(2)}, u32[]{:S(2)}) collective-permute-start(bf16[1544,128]{1,0:T(8,128)(2,1)S(1)} %get-tuple-element.47.y0), channel_id=1, source_target_pairs={{2,4},{3,5},{4,2},{5,3},{10,12},{11,13},{12,10},{13,11},{18,20},{1... | collective-permute-start | bytes 1185800 | tf_op jit(solution)/shard_map/ppermute | solution.py:283
  59.3 12.2 %collective-permute-start.8 = (bf16[1,384,384]{2,1,0:T(8,128)(2,1)S(1)}, bf16[1,384,384]{2,1,0:T(8,128)(2,1)S(1)}, u32[]{:S(2)}, u32[]{:S(2)}) collective-permute-start(bf16[1,384,384]{2,1,0:T(8,128)(2,1)S(1)} %collective-permute-done.7.refs_7_), channel_id=1, source_target_pairs={{0,8},{8,0},{16,24},{24,16},{1,9},{9,1},{17,25},{25,17},{2,10},{10... | collective-permute-start | bytes 884744 | tf_op jit(solution)/shard_map/ppermute | solution.py:279
  66.9 21.5 %collective-permute-start.21 = (bf16[1544,128]{1,0:T(8,128)(2,1)S(1)}, bf16[1544,128]{1,0:T(8,128)(2,1)}, u32[]{:S(2)}, u32[]{:S(2)}) collective-permute-start(bf16[1544,128]{1,0:T(8,128)(2,1)S(1)} %collective-permute-done.12.refs_2_), channel_id=1, source_target_pairs={{4,6},{5,7},{2,0},{3,1},{12,14},{13,15},{10,8},{11,9},{20,22},{21,... | collective-permute-start | bytes 1185800 | tf_op jit(solution)/shard_map/ppermute | solution.py:283
  68.2 20.2 %collective-permute-start.24 = (bf16[128,1536]{1,0:T(8,128)(2,1)}, bf16[128,1536]{1,0:T(8,128)(2,1)}, u32[]{:S(2)}, u32[]{:S(2)}) collective-permute-start(bf16[128,1536]{1,0:T(8,128)(2,1)} %collective-permute-done.16.f0), channel_id=1, source_target_pairs={{4,6},{5,7},{2,0},{3,1},{12,14},{13,15},{10,8},{11,9},{20,22},{21,... | collective-permute-start | bytes 1179656 | tf_op jit(solution)/shard_map/ppermute | solution.py:283
  70.3 21.4 %collective-permute-start.4 = (bf16[1,288,768]{2,1,0:T(8,128)(2,1)}, bf16[1,288,768]{2,1,0:T(8,128)(2,1)}, u32[]{:S(2)}, u32[]{:S(2)}) collective-permute-start(bf16[1,288,768]{2,1,0:T(8,128)(2,1)} %slice.24), channel_id=1, source_target_pairs={{0,16},{8,24},{16,0},{24,8},{1,17},{9,25},{17,1},{25,9},{2,18},{10... | collective-permute-start | bytes 1327112 | tf_op jit(solution)/shard_map/ppermute | solution.py:279
  70.9 17.6 %copy-start.24 = (bf16[1544,128]{1,0:T(8,128)(2,1)}, bf16[1544,128]{1,0:T(8,128)(2,1)S(1)}, u32[]{:S(2)}) copy-start(bf16[1544,128]{1,0:T(8,128)(2,1)S(1)} %collective-permute-done.22) | copy-start | bytes 1185796
  70.9 5.6 %collective-permute-start.5 = (bf16[1,96,768]{2,1,0:T(8,128)(2,1)S(1)}, bf16[1,96,768]{2,1,0:T(8,128)(2,1)S(1)}, u32[]{:S(2)}, u32[]{:S(2)}) collective-permute-start(bf16[1,96,768]{2,1,0:T(8,128)(2,1)S(1)} %slice.25), channel_id=1, source_target_pairs={{0,8},{8,0},{16,24},{24,16},{1,9},{9,1},{17,25},{25,17},{2,10},{10... | collective-permute-start | bytes 442376 | tf_op jit(solution)/shard_map/ppermute | solution.py:279
  72.1 25.2 %collective-permute-start.17 = (bf16[128,1536]{1,0:T(8,128)(2,1)}, bf16[128,1536]{1,0:T(8,128)(2,1)}, u32[]{:S(2)}, u32[]{:S(2)}) collective-permute-start(bf16[128,1536]{1,0:T(8,128)(2,1)} %collective-permute-done.16.f0), channel_id=1, source_target_pairs={{0,1},{1,0},{2,3},{3,2},{4,5},{5,4},{6,7},{7,6},{8,9},{9,8},{10,11... | collective-permute-start | bytes 1179656 | tf_op jit(solution)/shard_map/ppermute | solution.py:286
  76.4 21.4 %collective-permute-start.15 = (bf16[128,1536]{1,0:T(8,128)(2,1)}, bf16[128,1536]{1,0:T(8,128)(2,1)}, u32[]{:S(2)}, u32[]{:S(2)}) collective-permute-start(bf16[128,1536]{1,0:T(8,128)(2,1)} %collective-permute-done.14.n0), channel_id=1, source_target_pairs={{0,1},{1,0},{2,3},{3,2},{4,5},{5,4},{6,7},{7,6},{8,9},{9,8},{10,11... | collective-permute-start | bytes 1179656 | tf_op jit(solution)/shard_map/ppermute | solution.py:286
  88.4 12.3 %collective-permute-start.13 = (bf16[1544,128]{1,0:T(8,128)(2,1)S(1)}, bf16[1544,128]{1,0:T(8,128)(2,1)S(1)}, u32[]{:S(2)}, u32[]{:S(2)}) collective-permute-start(bf16[1544,128]{1,0:T(8,128)(2,1)S(1)} %collective-permute-done.12.refs_2_), channel_id=1, source_target_pairs={{0,1},{1,0},{2,3},{3,2},{4,5},{5,4},{6,7},{7,6},{8,9},{9,8},{10,11... | collective-permute-start | bytes 1185800 | tf_op jit(solution)/shard_map/ppermute | solution.py:286
  88.4 12.3 %collective-permute-start.11 = (bf16[1544,128]{1,0:T(8,128)(2,1)S(1)}, bf16[1544,128]{1,0:T(8,128)(2,1)S(1)}, u32[]{:S(2)}, u32[]{:S(2)}) collective-permute-start(bf16[1544,128]{1,0:T(8,128)(2,1)S(1)} %collective-permute-done.10.refs_0_), channel_id=1, source_target_pairs={{0,1},{1,0},{2,3},{3,2},{4,5},{5,4},{6,7},{7,6},{8,9},{9,8},{10,11... | collective-permute-start | bytes 1185800 | tf_op jit(solution)/shard_map/ppermute | solution.py:286
  89.0 2.8 %copy-start.9 = (bf16[1544,128]{1,0:T(8,128)(2,1)S(1)}, bf16[1544,128]{1,0:T(8,128)(2,1)}, u32[]{:S(2)}) copy-start(bf16[1544,128]{1,0:T(8,128)(2,1)} %copy-done.8) | copy-start | bytes 1185796
  89.0 2.8 %copy-start.11 = (bf16[1544,128]{1,0:T(8,128)(2,1)S(1)}, bf16[1544,128]{1,0:T(8,128)(2,1)}, u32[]{:S(2)}) copy-start(bf16[1544,128]{1,0:T(8,128)(2,1)} %copy-done.10) | copy-start | bytes 1185796
  89.0 2.8 %copy-start.13 = (bf16[128,1536]{1,0:T(8,128)(2,1)S(1)}, bf16[128,1536]{1,0:T(8,128)(2,1)}, u32[]{:S(2)}) copy-start(bf16[128,1536]{1,0:T(8,128)(2,1)} %copy-done.12) | copy-start | bytes 1179652
  89.0 2.8 %copy-start.15 = (bf16[128,1536]{1,0:T(8,128)(2,1)S(1)}, bf16[128,1536]{1,0:T(8,128)(2,1)}, u32[]{:S(2)}) copy-start(bf16[128,1536]{1,0:T(8,128)(2,1)} %copy-done.14) | copy-start | bytes 1179652
  89.0 2.8 %copy-start.17 = (bf16[1,384,384]{2,1,0:T(8,128)(2,1)S(1)}, bf16[1,384,384]{2,1,0:T(8,128)(2,1)}, u32[]{:S(2)}) copy-start(bf16[1,384,384]{2,1,0:T(8,128)(2,1)} %copy-done.16) | copy-start | bytes 884740
  89.0 2.8 %copy-start.19 = (bf16[1,384,384]{2,1,0:T(8,128)(2,1)S(1)}, bf16[1,384,384]{2,1,0:T(8,128)(2,1)}, u32[]{:S(2)}) copy-start(bf16[1,384,384]{2,1,0:T(8,128)(2,1)} %copy-done.18) | copy-start | bytes 884740
  91.7 15.2 %collective-permute-start.26 = (bf16[128,1536]{1,0:T(8,128)(2,1)S(1)}, bf16[128,1536]{1,0:T(8,128)(2,1)S(1)}, u32[]{:S(2)}, u32[]{:S(2)}) collective-permute-start(bf16[128,1536]{1,0:T(8,128)(2,1)S(1)} %add.30.x0), channel_id=1, source_target_pairs={{0,1},{1,0},{2,3},{3,2},{4,5},{5,4},{6,7},{7,6},{8,9},{9,8},{10,11... | collective-permute-start | bytes 1179656 | tf_op jit(solution)/shard_map/ppermute | solution.py:286
  97.3 10.5 %collective-permute-start.23 = (bf16[1544,128]{1,0:T(8,128)(2,1)S(1)}, bf16[1544,128]{1,0:T(8,128)(2,1)S(1)}, u32[]{:S(2)}, u32[]{:S(2)}) collective-permute-start(bf16[1544,128]{1,0:T(8,128)(2,1)S(1)} %add.29.y0), channel_id=1, source_target_pairs={{0,1},{1,0},{2,3},{3,2},{4,5},{5,4},{6,7},{7,6},{8,9},{9,8},{10,11... | collective-permute-start | bytes 1185800 | tf_op jit(solution)/shard_map/ppermute | solution.py:286
  109.7 2.8 %collective-permute-start.27 = (bf16[1544,128]{1,0:T(8,128)(2,1)S(1)}, bf16[1544,128]{1,0:T(8,128)(2,1)S(1)}, u32[]{:S(2)}, u32[]{:S(2)}) collective-permute-start(bf16[1544,128]{1,0:T(8,128)(2,1)S(1)} %get-tuple-element.74), channel_id=1, source_target_pairs={{0,1},{1,0},{2,3},{3,2},{4,5},{5,4},{6,7},{7,6},{8,9},{9,8},{10,11... | collective-permute-start | bytes 1185800 | tf_op jit(solution)/shard_map/ppermute | solution.py:286
  109.8 18.5 %collective-permute-start.18 = (bf16[2,1544,128]{2,1,0:T(8,128)(2,1)S(1)}, bf16[2,1544,128]{2,1,0:T(8,128)(2,1)S(1)}, u32[]{:S(2)}, u32[]{:S(2)}) collective-permute-start(bf16[2,1544,128]{2,1,0:T(8,128)(2,1)S(1)} %get-tuple-element.58), channel_id=1, source_target_pairs={{0,1},{1,0},{2,3},{3,2},{4,5},{5,4},{6,7},{7,6},{8,9},{9,8},{10,11... | collective-permute-start | bytes 2371592 | tf_op jit(solution)/shard_map/ppermute | solution.py:286
  110.3 18.9 %collective-permute-start.9 = (bf16[1544,128]{1,0:T(8,128)(2,1)S(1)}, bf16[1544,128]{1,0:T(8,128)(2,1)S(1)}, u32[]{:S(2)}, u32[]{:S(2)}) collective-permute-start(bf16[1544,128]{1,0:T(8,128)(2,1)S(1)} %get-tuple-element.51), channel_id=1, source_target_pairs={{0,1},{1,0},{2,3},{3,2},{4,5},{5,4},{6,7},{7,6},{8,9},{9,8},{10,11... | collective-permute-start | bytes 1185800 | tf_op jit(solution)/shard_map/ppermute | solution.py:286
  110.4 11.7 %collective-permute-start.33 = (bf16[176,1152]{1,0:T(8,128)(2,1)S(1)}, bf16[176,1152]{1,0:T(8,128)(2,1)S(1)}, u32[]{:S(2)}, u32[]{:S(2)}) collective-permute-start(bf16[176,1152]{1,0:T(8,128)(2,1)S(1)} %get-tuple-element.85), channel_id=1, source_target_pairs={{0,8},{8,0},{16,24},{24,16},{1,9},{9,1},{17,25},{25,17},{2,10},{10... | collective-permute-start | bytes 1216520 | tf_op jit(solution)/shard_map/ppermute | solution.py:279
  110.9 13.8 %collective-permute-start.31 = (bf16[208,1152]{1,0:T(8,128)(2,1)S(1)}, bf16[208,1152]{1,0:T(8,128)(2,1)S(1)}, u32[]{:S(2)}, u32[]{:S(2)}) collective-permute-start(bf16[208,1152]{1,0:T(8,128)(2,1)S(1)} %get-tuple-element.83), channel_id=1, source_target_pairs={{0,16},{8,24},{16,0},{24,8},{1,17},{9,25},{17,1},{25,9},{2,18},{10... | collective-permute-start | bytes 1437704 | tf_op jit(solution)/shard_map/ppermute | solution.py:279
  112.5 22.5 %collective-permute-start.30 = (bf16[208,1152]{1,0:T(8,128)(2,1)S(1)}, bf16[208,1152]{1,0:T(8,128)(2,1)S(1)}, u32[]{:S(2)}, u32[]{:S(2)}) collective-permute-start(bf16[208,1152]{1,0:T(8,128)(2,1)S(1)} %get-tuple-element.81), channel_id=1, source_target_pairs={{0,16},{8,24},{16,0},{24,8},{1,17},{9,25},{17,1},{25,9},{2,18},{10... | collective-permute-start | bytes 1437704 | tf_op jit(solution)/shard_map/ppermute | solution.py:279
  122.1 12.2 %collective-permute-start.29 = (bf16[176,1152]{1,0:T(8,128)(2,1)S(1)}, bf16[176,1152]{1,0:T(8,128)(2,1)S(1)}, u32[]{:S(2)}, u32[]{:S(2)}) collective-permute-start(bf16[176,1152]{1,0:T(8,128)(2,1)S(1)} %get-tuple-element.80), channel_id=1, source_target_pairs={{0,8},{8,0},{16,24},{24,16},{1,9},{9,1},{17,25},{25,17},{2,10},{10... | collective-permute-start | bytes 1216520 | tf_op jit(solution)/shard_map/ppermute | solution.py:279
  124.8 19.5 %collective-permute-start.28 = (bf16[1544,128]{1,0:T(8,128)(2,1)S(1)}, bf16[1544,128]{1,0:T(8,128)(2,1)S(1)}, u32[]{:S(2)}, u32[]{:S(2)}) collective-permute-start(bf16[1544,128]{1,0:T(8,128)(2,1)S(1)} %add_convert_fusion.2), channel_id=1, source_target_pairs={{0,6},{1,7},{2,4},{3,5},{4,2},{5,3},{6,0},{7,1},{8,14},{9,15},{10,... | collective-permute-start | bytes 1185800 | tf_op jit(solution)/shard_map/ppermute | solution.py:283
  128.4 14.5 %collective-permute-start.34 = (bf16[176,1152]{1,0:T(8,128)(2,1)S(1)}, bf16[176,1152]{1,0:T(8,128)(2,1)S(1)}, u32[]{:S(2)}, u32[]{:S(2)}) collective-permute-start(bf16[176,1152]{1,0:T(8,128)(2,1)S(1)} %add_convert_fusion.1), channel_id=1, source_target_pairs={{0,16},{8,24},{16,0},{24,8},{1,17},{9,25},{17,1},{25,9},{2,18},{10... | collective-permute-start | bytes 1216520 | tf_op jit(solution)/shard_map/ppermute | solution.py:279
  128.9 9.6 %copy-start = (bf16[1,384,768]{2,1,0:T(8,128)(2,1)S(1)}, bf16[1,384,768]{2,1,0:T(8,128)(2,1)}, u32[]{:S(2)}) copy-start(bf16[1,384,768]{2,1,0:T(8,128)(2,1)} %min_ref.1) | copy-start | bytes 1769476
  128.9 9.6 %copy-start.3 = (bf16[1,384,384]{2,1,0:T(8,128)(2,1)S(1)}, bf16[1,384,384]{2,1,0:T(8,128)(2,1)}, u32[]{:S(2)}) copy-start(bf16[1,384,384]{2,1,0:T(8,128)(2,1)} %mout_ref.1) | copy-start | bytes 884740
  129.2 14.1 %collective-permute-start.32 = (bf16[208,1152]{1,0:T(8,128)(2,1)S(1)}, bf16[208,1152]{1,0:T(8,128)(2,1)S(1)}, u32[]{:S(2)}, u32[]{:S(2)}) collective-permute-start(bf16[208,1152]{1,0:T(8,128)(2,1)S(1)} %add_convert_fusion), channel_id=1, source_target_pairs={{0,8},{8,0},{16,24},{24,16},{1,9},{9,1},{17,25},{25,17},{2,10},{10... | collective-permute-start | bytes 1437704 | tf_op jit(solution)/shard_map/ppermute | solution.py:279
  134.3 12.0 %collective-permute-start.19 = (bf16[1544,128]{1,0:T(8,128)(2,1)S(1)}, bf16[1544,128]{1,0:T(8,128)(2,1)S(1)}, u32[]{:S(2)}, u32[]{:S(2)}) collective-permute-start(bf16[1544,128]{1,0:T(8,128)(2,1)S(1)} %get-tuple-element.89), channel_id=1, source_target_pairs={{0,2},{1,3},{2,0},{3,1},{4,6},{5,7},{6,4},{7,5},{8,10},{9,11},{10,... | collective-permute-start | bytes 1185800 | tf_op jit(solution)/shard_map/ppermute | solution.py:283
  135.0 24.5 %collective-permute-start.20 = (bf16[1544,128]{1,0:T(8,128)(2,1)S(1)}, bf16[1544,128]{1,0:T(8,128)(2,1)S(1)}, u32[]{:S(2)}, u32[]{:S(2)}) collective-permute-start(bf16[1544,128]{1,0:T(8,128)(2,1)S(1)} %get-tuple-element.88), channel_id=1, source_target_pairs={{0,4},{1,5},{2,6},{3,7},{4,0},{5,1},{6,2},{7,3},{8,12},{9,13},{10,... | collective-permute-start | bytes 1185800 | tf_op jit(solution)/shard_map/ppermute | solution.py:283
  138.9 20.6 %copy-start.6 = (s32[128,4]{0,1:T(4,128)S(1)}, s32[128,4]{0,1:T(4,128)}, u32[]{:S(2)}) copy-start(s32[128,4]{0,1:T(4,128)} %param.9) | copy-start | bytes 6148
  (13 other events, 10.6 us)
